TPU v7x, 256 devices: a whole 4x4x8 slice. The times are simulated.
256 devices in a mesh: replica: 32 (over z_lo, y, core), model: 8 (over z_hi, x).
Axes of the slice: x: 4, y: 4, z: 8 (z_hi: 2, z_lo: 4; z = z_hi * 4 + z_lo), core: 2. Of those that a mesh axis runs over, the one named last changes fastest.
Arguments:
- layer_grads: bfloat16 [32, 2, 4096, 1024], P('replica', None, 'model'), may hold values from -6 to 6
- last_basis: float32 [2, 1024, 32], replicated, may hold values from -6 to 6
- layer_weights: float32 [2, 4096, 1024], P(None, 'model', 'replica'), may hold values from -0.1875 to 0.1875
- momentum: float32 [2, 4096, 1024], P(None, 'model', 'replica'), may hold values from -0.3125 to 0.3125
Outputs:
- new_weights: float32 [2, 4096, 1024], P(None, 'model', 'replica')
- new_basis: float32 [2, 1024, 32], replicated
- new_momentum: float32 [2, 4096, 1024], P(None, 'model', 'replica')
All inputs are finite; a program needn't handle non-finite values.
Results may differ from a plain program's by a relative error of at most 0.0029.
Values sent between devices are 32-bit elements; how exact they have to be, the bound alone decides.
No kernel may reach another device: no remote copies, remote signals or barrier semaphores. Data moves between devices by JAX's collectives and lax.ppermute only.
A program may use at most 64 MiB of HBM per device.

v0:
```python
import jax
import jax.numpy as jnp
from jax import lax
from jax.sharding import PartitionSpec as P

RANK = 32


def in_blocks(value, dim, length):
    shape = value.shape
    tiles = value.reshape(*shape[:dim], length, shape[dim] // length, *shape[dim + 1 :])
    return jnp.moveaxis(tiles, dim, 0)


def summed_on_arrival(value, axis, dim):
    length = lax.axis_size(axis)
    tiles = lax.all_to_all(in_blocks(value, dim, length), axis, 0, 0, tiled=True)
    return jnp.sum(tiles, axis=0)


def in_order(tiles, dim):
    tiles = jnp.moveaxis(tiles, 0, dim)
    shape = tiles.shape
    return tiles.reshape(*shape[:dim], shape[dim] * shape[dim + 1], *shape[dim + 2 :])


def from_everyone(value, axis):
    length = lax.axis_size(axis)
    return lax.all_to_all(
        jnp.broadcast_to(value[None], (length, *value.shape)), axis, 0, 0, tiled=True
    )


def gather_directly(value, axis, dim):
    return in_order(from_everyone(value, axis), dim)


def packed_total(arrays, axis):
    ends = [0]
    for a in arrays:
        ends.append(ends[-1] + a.size)
    running = lax.psum(jnp.concatenate([a.ravel() for a in arrays]), axis)
    return tuple((running[b:e].reshape(a.shape) for a, b, e in zip(arrays, ends, ends[1:])))


def shards(layer_grads, last_basis, layer_weights, momentum):
    own_grads = layer_grads[0]
    part_left = jnp.einsum(
        "liw,lwr->lir",
        own_grads,
        last_basis.astype(jnp.bfloat16),
        preferred_element_type=jnp.float32,
    )
    shares = summed_on_arrival(part_left, "replica", 1)
    left = gather_directly(shares, "replica", 1)
    part_gram = jnp.einsum("lir,lis->lrs", left, left, precision=lax.Precision.HIGHEST)
    small_left = left.astype(jnp.bfloat16)
    part_right = jnp.einsum(
        "liw,lir->lwr", own_grads, small_left, preferred_element_type=jnp.float32
    )
    own_share = part_gram / lax.axis_size("replica")
    right, gram = packed_total((part_right, own_share), ("replica", "model"))
    gram = gram + 0.001 * jnp.mean(jnp.diagonal(gram, axis1=1, axis2=2), axis=1)[
        :, None, None
    ] * jnp.eye(RANK, dtype=jnp.float32)
    place = lax.axis_index("replica") * layer_weights.shape[2]
    own_right = lax.dynamic_slice_in_dim(right, place, layer_weights.shape[2], axis=1)
    root = jnp.linalg.cholesky(gram)
    half = lax.linalg.triangular_solve(
        root, jnp.swapaxes(own_right, 1, 2), left_side=True, lower=True
    )
    mixed = lax.linalg.triangular_solve(root, half, left_side=True, lower=True, transpose_a=True)
    change = jnp.einsum(
        "lir,lrw->liw", left, mixed, precision=lax.Precision.HIGHEST
    ) / lax.axis_size("replica")
    new_momentum = 0.9 * momentum + change
    new_weights = layer_weights - 0.02 * new_momentum
    new_basis = right * lax.rsqrt(jnp.mean(right * right, axis=(1, 2), keepdims=True) + 1e-12)
    return (new_weights, new_basis, new_momentum)


def solution(mesh):
    in_specs = (
        P("replica", None, "model", None),
        P(),
        P(None, "model", "replica"),
        P(None, "model", "replica"),
    )
    out_specs = (P(None, "model", "replica"), P(), P(None, "model", "replica"))
    return jax.shard_map(shards, mesh=mesh, in_specs=in_specs, out_specs=out_specs, check_vma=False)
```

profile of v0, /device:TPU:1, one launch (start us, length us, event | category | flops | bytes accessed | tf_op | source)
XLA Modules:
  0.0 326.7 jit_solution(10584026967447597187)
XLA Ops:
  7.2 1.6 copy-done
  8.8 1.6 fusion.2
  10.5 0.3 reshape.77
  10.7 18.5 %all_to_all.10 = f32[32,1,1024]{2,1,0:T(1,128)S(1)} all-to-all(f32[32,1,1024]{2,1,0:T(1,128)S(1)} %reshape.77), channel_id=1, replica_groups=mesh['replica'=32,'model'=8] {'replica'}, dimensions={0} | all-to-all | bytes 262144 | tf_op jit(solution)/shard_map/all_to_all | solution.py:17
  29.2 0.5 broadcast.114
  29.7 0.9 reduce.7
  30.7 0.2 reshape.78
  31.0 0.9 reshape.79
  31.9 3.8 %all-to-all-start.1 = ((f32[32,1,1024]{2,1,0:T(1,128)}), f32[32,1,1024]{2,1,0:T(1,128)S(1)}, u32[]{:S(2)}, u32[]{:S(2)}) async-start(f32[32,1,1024]{2,1,0:T(1,128)} %reshape.79), calls=%async_computation.1 | async-start | bytes 262144 | tf_op jit(solution)/shard_map/all_to_all | solution.py:29
  35.8 8.6 %all-to-all-done.1 = f32[32,1,1024]{2,1,0:T(1,128)S(1)} async-done(((f32[32,1,1024]{2,1,0:T(1,128)}), f32[32,1,1024]{2,1,0:T(1,128)S(1)}, u32[]{:S(2)}, u32[]{:S(2)}) %all-to-all-start.1) | async-done | bytes 131104 | tf_op jit(solution)/shard_map/all_to_all | solution.py:29
  44.3 1.0 reduce.8
  45.3 0.2 reshape.80
  45.6 1.0 convolution_multiply_fusion.1
  46.6 0.5 fusion.4
  47.1 1.3 copy.40
  48.4 1.5 reshape.67
  50.0 0.7 pad_maximum_fusion
  50.9 244.9 %all-reduce.2.cloned.1.call-done = f32[67584]{0:T(1024)} async-done(((f32[67584]{0:T(1024)}), f32[67584]{0:T(1024)}) %all-reduce.2.cloned.1.call-update) | async-done | bytes 270352 | tf_op jit(solution)/shard_map/psum | solution.py:42
  295.7 0.7 slice.32
  296.5 0.3 copy.43
  296.9 0.7 gather_fusion
  297.8 5.9 %custom-call.9 = f32[2,32,32]{2,1,0:T(8,128)S(1)} custom-call(f32[2,32,32]{2,1,0:T(8,128)S(1)} %fusion.14), custom_call_target="Cholesky" | custom-call | tf_op jit(solution)/shard_map/jit(cholesky)/cholesky | solution.py:68
  303.7 0.1 compare_reduce_fusion
  303.9 4.9 %custom-call.10 = f32[2,1,32,32]{2,3,1,0:T(8,128)S(1)} custom-call(f32[2,1,32,32]{3,2,1,0:T(8,128)S(1)} %select_bitcast_fusion), custom_call_target="InvertDiagBlocksLowerTriangular" | custom-call | tf_op jit(solution)/shard_map/triangular_solve | solution.py:72
  308.8 1.0 slice.33
  309.8 1.3 reshape.70
  311.1 1.5 multiply_reduce_fusion
  312.6 1.0 fusion.12
  313.6 0.2 fusion.10
  313.9 2.4 broadcast_multiply_fusion
  316.2 2.2 copy.50
  318.5 1.4 multiply_subtract_fusion
  (28 shorter events, 1.1 us)
Async XLA Ops:
  7.2 1.6 copy-start
  31.9 12.4 %all-to-all-start.1 = ((f32[32,1,1024]{2,1,0:T(1,128)}), f32[32,1,1024]{2,1,0:T(1,128)S(1)}, u32[]{:S(2)}, u32[]{:S(2)}) async-start(f32[32,1,1024]{2,1,0:T(1,128)} %reshape.79), calls=%async_computation.1 | async-start | bytes 262144 | tf_op jit(solution)/shard_map/all_to_all | solution.py:29
  35.7 260.0 %all-reduce.2.cloned.1.call-start = ((), (), s32[]{:S(2)}) async-start(), calls=%async_computation.2 | async-start | bytes 540672 | tf_op jit(solution)/shard_map/psum | solution.py:42
  311.1 7.4 %copy-start.1 = (f32[2,512,32]{1,2,0:T(8,128)S(1)}, f32[2,512,32]{1,2,0:T(8,128)}, u32[]{:S(2)}) copy-start(f32[2,512,32]{1,2,0:T(8,128)} %param.6) | copy-start | bytes 393220
  311.1 7.4 %copy-start.2 = (f32[2,512,32]{1,2,0:T(8,128)S(1)}, f32[2,512,32]{1,2,0:T(8,128)}, u32[]{:S(2)}) copy-start(f32[2,512,32]{1,2,0:T(8,128)} %param.7) | copy-start | bytes 393220
Sparse Core Ops, SparseCore 0:
  50.9 244.8 all-reduce.1
where the time goes:
time: 327 us
  waiting for transfers between devices  253 us (77%)
  blocking collectives  18.5 us (6%)
  other arithmetic  17.8 us (5%)
  between operations  14.2 us (4%)
  local copies, waits for them, and re-layouts  13.2 us (4%)
  matrix products  5.67 us (2%)
  starting transfers between devices  3.85 us (1%)
    psum x1, waiting for transfers between devices, packed_total(): running = lax.psum(jnp.concatenate([a.ravel() for a in arrays]), axis)  245 us
    all_to_all x1, blocking collectives, summed_on_arrival(): lax.all_to_all(in_blocks(value, dim, length), axis, 0, 0, tiled=True)  18.5 us
    all_to_all x1, waiting for transfers between devices, from_everyone(): lax.all_to_all(jnp.broadcast_to(value[None], (length, *value.shape)), axi...  8.55 us
  transfers between devices with their start and end apart: 2, of which 2 were waited for; matrix products, arithmetic and copies ran while one was open for 0% of the time, Pallas kernels for 0%

commit v1 on v0

v1 whole, which is shorter than its diff:
```python
import functools

import jax
import jax.numpy as jnp
from jax import lax
from jax.experimental import pallas as pl
from jax.experimental.pallas import tpu as pltpu
from jax.sharding import Mesh
from jax.sharding import PartitionSpec as P

RANK = 32
LANES = 128
SIZES = {"zlo": 4, "y": 4, "core": 2, "zhi": 2, "x": 4}
REPLICA = ("zlo", "y", "core")
MODEL = ("zhi", "x")
PLANE = ("y", "core", "x")
COLUMN = ("zlo", "zhi")
REPLICAS, PEERS, STACK = 32, 32, 8
SHARES = 8
CHUNK = 18
EXACT = lax.Precision.HIGHEST
VMEM_LIMIT = 24 * 1024 * 1024


def kernel_call(body, outs, flops=1 << 20, moved=1 << 18):
    many = isinstance(outs, (list, tuple))
    count = len(outs) if many else 1
    spec = pl.BlockSpec(memory_space=pltpu.VMEM)
    return lambda *args: pl.pallas_call(
        body,
        out_shape=outs,
        in_specs=[spec] * len(args),
        out_specs=[spec] * count if many else spec,
        compiler_params=pltpu.CompilerParams(vmem_limit_bytes=VMEM_LIMIT),
        cost_estimate=pl.CostEstimate(flops=flops, bytes_accessed=moved, transcendentals=0),
    )(*args)


def f32(*shape):
    return jax.ShapeDtypeStruct(shape, jnp.float32)


def joined(ref, rows, columns):
    return jnp.concatenate(
        [
            jnp.concatenate([ref[t * columns + j] for j in range(columns)], axis=1)
            for t in range(rows)
        ],
        axis=0,
    )


def lane_of(shape):
    return lax.broadcasted_iota(jnp.int32, shape, 1)


def row_of(shape):
    return lax.broadcasted_iota(jnp.int32, shape, 0)


def right_body(left_ref, grads_ref, out_ref):
    left = joined(left_ref, 8, 4)
    share = lax.axis_index("y") * 2 + lax.axis_index("core")
    twice = jnp.concatenate([left, left], axis=0)
    gram = lax.dot_general(
        left, twice, (((1,), (1,)), ((), ())), precision=EXACT, preferred_element_type=jnp.float32
    )
    lane = lane_of((16, LANES))
    packed = jnp.where(
        lane < 32,
        gram[0:16],
        jnp.where(lane < 64, gram[32:48], jnp.where(lane < 96, gram[16:32], gram[48:64])),
    )
    mine = packed[0:2]
    for s in range(1, SHARES):
        mine = jnp.where(share == s, packed[2 * s : 2 * s + 2], mine)
    for l in range(2):
        right = jnp.dot(
            left[l * RANK : (l + 1) * RANK].astype(jnp.bfloat16),
            grads_ref[l],
            preferred_element_type=jnp.float32,
        )
        for t in range(4):
            for j in range(4):
                at = CHUNK * (16 * l + 4 * t + j)
                rows = right[8 * t : 8 * t + 8]
                out_ref[at : at + 8] = rows[:, 256 * j : 256 * j + 128]
                out_ref[at + 8 : at + 16] = rows[:, 256 * j + 128 : 256 * j + 256]
                out_ref[at + 16 : at + 18] = mine


def plane_body(in_ref, out_ref):
    total = in_ref[0:16]
    for s in range(1, PEERS):
        total = total + in_ref[CHUNK * s : CHUNK * s + 16]
    for z in range(STACK):
        out_ref[z, 0:16] = total
    for share in range(SHARES):
        part = None
        for x in range(4):
            at = CHUNK * (4 * share + x) + 16
            piece = in_ref[at : at + 2]
            part = piece if part is None else part + piece
        for z in range(STACK):
            out_ref[z, 16 + 2 * share : 18 + 2 * share] = part


def column_body(in_ref, out_ref, gram_ref):
    total = in_ref[0]
    for z in range(1, STACK):
        total = total + in_ref[z]
    for d in range(PEERS):
        out_ref[d] = total[0:16]
    gram_ref[...] = total[16:32] * 0.25


def factor_body(gram_ref, left_ref, inverse_ref, frame_ref):
    packed = gram_ref[...]
    shape = (RANK, LANES)
    lane, row = lane_of(shape), row_of(shape)
    gram = jnp.concatenate([packed, pltpu.roll(packed, 64, 1)], axis=0)
    first = (lane // RANK) % 2 == 0
    unit = (lane % RANK) == row
    diagonal = jnp.where(unit & (lane < 64), gram, 0.0)
    mean0 = jnp.sum(jnp.where(first, diagonal, 0.0)) * (1.0 / RANK)
    mean1 = jnp.sum(jnp.where(first, 0.0, diagonal)) * (1.0 / RANK)
    ridge = 0.001 * jnp.where(first, mean0, mean1)
    work = jnp.where(lane < 64, gram, 0.0) + jnp.where(unit, jnp.where(lane < 64, ridge, 1.0), 0.0)
    pivots = jnp.ones(shape, jnp.float32)
    for k in range(RANK):
        column = jnp.where(first, work[:, k : k + 1], work[:, RANK + k : RANK + k + 1])
        pivot = column[k : k + 1]
        pivots = jnp.where(row == k, column, pivots)
        if k + 1 < RANK:
            step = work[k : k + 1] / pivot
            work = work - jnp.where(row > k, column * step, 0.0)
    inverse = pltpu.roll(work / jnp.sqrt(pivots), 64, 1)
    inverse_ref[...] = inverse
    left = joined(left_ref, 8, 4)
    for l in range(2):
        frame_ref[l] = (
            jnp.dot(
                inverse[:, l * RANK : (l + 1) * RANK],
                left[l * RANK : (l + 1) * RANK],
                precision=EXACT,
                preferred_element_type=jnp.float32,
            )
            * (1.0 / REPLICAS)
        )


def final_body(right_ref, inverse_ref, frame_ref, weights_ref, momentum_ref, basis_ref, new_w_ref, new_m_ref):
    place = (lax.axis_index("zlo") * 4 + lax.axis_index("y")) * 2 + lax.axis_index("core")
    block = place // 4
    shift = (4 - place % 4) * 32
    for l in range(2):
        square = jnp.zeros((8, LANES), jnp.float32)
        for i in range(32):
            tile = right_ref[32 * l + i]
            square = square + tile * tile
        scale = lax.rsqrt(jnp.sum(square) * (1.0 / (RANK * 1024)) + 1e-12)
        for t in range(4):
            for j in range(8):
                basis_ref[l, 8 * t : 8 * t + 8, 128 * j : 128 * j + 128] = (
                    right_ref[32 * l + 8 * t + j] * scale
                )
        own = jnp.concatenate([right_ref[32 * l + 8 * t + block] for t in range(4)], axis=0)
        half = jnp.dot(
            inverse_ref[:, l * RANK : (l + 1) * RANK],
            own,
            precision=EXACT,
            preferred_element_type=jnp.float32,
        )
        half = pltpu.roll(half, shift, 1)[:, :RANK]
        change = lax.dot_general(
            half,
            frame_ref[l],
            (((0,), (0,)), ((), ())),
            precision=EXACT,
            preferred_element_type=jnp.float32,
        )
        new = 0.9 * momentum_ref[l] + change
        new_m_ref[l] = new
        new_w_ref[l] = weights_ref[l] - 0.02 * new


def shards(layer_grads, last_basis, layer_weights, momentum):
    grads = layer_grads[0]
    layers, rows, width = grads.shape
    basis = jnp.swapaxes(last_basis, 1, 2).astype(jnp.bfloat16)
    part_left = jnp.einsum("lrw,liw->lri", basis, grads, preferred_element_type=jnp.float32)
    tiles = part_left.reshape(8, 8, 4, LANES).transpose(0, 2, 1, 3).reshape(REPLICAS, 8, LANES)
    tile = jnp.sum(lax.all_to_all(tiles, REPLICA, 0, 0, tiled=True), axis=0)
    copies = jnp.broadcast_to(tile[None], tiles.shape)
    left = lax.all_to_all(copies, REPLICA, 0, 0, tiled=True)

    sent = kernel_call(right_body, f32(PEERS * CHUNK, LANES))(left, grads)
    sent = sent.reshape(PEERS * CHUNK // 2, 2, LANES)
    came = lax.all_to_all(sent, PLANE, 0, 0, tiled=True).reshape(PEERS * CHUNK, LANES)
    sent = kernel_call(plane_body, f32(STACK, 32, LANES))(came)
    came = lax.all_to_all(sent, COLUMN, 0, 0, tiled=True)
    sent, gram = kernel_call(column_body, [f32(PEERS, 16, LANES), f32(16, LANES)])(came)
    right = lax.all_to_all(sent, PLANE, 0, 0, tiled=True).reshape(64, 8, LANES)
    inverse, frame = kernel_call(
        factor_body, [f32(RANK, LANES), f32(layers, RANK, rows)], flops=1 << 28
    )(gram, left)
    new_basis, new_weights, new_momentum = kernel_call(
        final_body,
        [f32(layers, RANK, width), f32(layers, RANK, rows), f32(layers, RANK, rows)],
    )(right, inverse, frame, jnp.swapaxes(layer_weights, 1, 2), jnp.swapaxes(momentum, 1, 2))
    return tuple(jnp.swapaxes(a, 1, 2) for a in (new_weights, new_basis, new_momentum))


def solution(mesh):
    fine = Mesh(mesh.devices.reshape(tuple(SIZES.values())), tuple(SIZES))
    sharded = P(None, MODEL, REPLICA)
    return jax.shard_map(
        shards,
        mesh=fine,
        in_specs=(P(REPLICA, None, MODEL, None), P(), sharded, sharded),
        out_specs=(sharded, P(), sharded),
        check_vma=False,
    )
```

time: 327 us -> 78.5 us (0.24)
  waiting for transfers between devices: 253 us -> 5.71 us
  blocking collectives: 18.5 us -> 57.2 us
  other arithmetic: 17.8 us -> 0.04 us
  between operations: 14.2 us -> 0.67 us
  local copies, waits for them, and re-layouts: 13.2 us -> 0.03 us
  Pallas kernels: 0 us -> 6.24 us
    psum x1 -> x0, waiting for transfers between devices: 245 us -> none  [packed_total(): running = lax.psum(jnp.concatenate([a.ravel() for a in arrays]), axis)]
    all_to_all x1 -> x4, blocking collectives: 18.5 us -> 57.2 us  [the longest x1 18.5 us: shards(): tile = jnp.sum(lax.all_to_all(tiles, REPLICA, 0, 0, tiled=True), axis=0)]
    another operation x7 -> x0, other arithmetic: 11 us -> none  [the longest x4 6.01 us: shards(): root = jnp.linalg.cholesky(gram)]
    pallas_call x0 -> x5, Pallas kernels: none -> 6.24 us  [kernel_call(): pl.pallas_call(body, out_shape=outs, in_specs=[spec] * len(args), out_spe...]
    unnamed x11 -> x6, local copies, waits for them, and re-layouts: 5.34 us -> 0.01 us
    reshape x7 -> x0, local copies, waits for them, and re-layouts: 3.36 us -> none  [the longest x4 1.68 us: packed_total(): running[b:e].reshape(a.shape)]
  transfers between devices with their start and end apart: 2 -> 1, of which waited for: 2 -> 1; matrix products, arithmetic and copies ran while one was open for 0% -> 0% of each run, Pallas kernels for 0% -> 4%
where the time goes in v1:
time: 78.5 us; the launch traced here: 78.2 us
  blocking collectives  57.2 us (73%)
  Pallas kernels  6.24 us (8%)
  starting transfers between devices  5.78 us (7%)
  waiting for transfers between devices  5.71 us (7%)
  matrix products  2.54 us (3%)
    all_to_all x1, blocking collectives, shards(): tile = jnp.sum(lax.all_to_all(tiles, REPLICA, 0, 0, tiled=True), axis=0)  18.5 us
    all_to_all x1, blocking collectives, shards(): lax.all_to_all(sent, PLANE, 0, 0, tiled=True).reshape(PEERS * CHUNK, LANES)  14.6 us
    all_to_all x1, blocking collectives, shards(): left = lax.all_to_all(copies, REPLICA, 0, 0, tiled=True)  12.1 us
    all_to_all x1, blocking collectives, shards(): came = lax.all_to_all(sent, COLUMN, 0, 0, tiled=True)  12 us
    pallas_call x5, Pallas kernels, kernel_call(): pl.pallas_call(body, out_shape=outs, in_specs=[spec] * len(args), out_spe...  6.24 us
    all_to_all x1, starting transfers between devices, shards(): right = lax.all_to_all(sent, PLANE, 0, 0, tiled=True).reshape(64, 8, LANES)  5.78 us
    all_to_all x1, waiting for transfers between devices, shards(): right = lax.all_to_all(sent, PLANE, 0, 0, tiled=True).reshape(64, 8, LANES)  5.71 us
    dot_general x1, matrix products, shards(): jnp.einsum('lrw,liw->lri', basis, grads, preferred_element_type=jnp.float32)  2.54 us
  transfers between devices with their start and end apart: 1, of which 1 were waited for; matrix products, arithmetic and copies ran while one was open for 0% of the time, Pallas kernels for 4%

profile of v1, /device:TPU:1, one launch (start us, length us, event | category | flops | bytes accessed | tf_op | source)
XLA Modules:
  0.0 78.2 jit_solution(11417973922005182880)
XLA Ops:
  0.6 0.0 copy-start
  0.6 2.5 %fusion = f32[2,32,512]{2,1,0:T(8,128)S(1)} fusion(f32[2,1024,32]{1,2,0:T(8,128)} %param.5, bf16[1,2,512,1024]{3,2,1,0:T(8,128)(2,1)} %param.4), kind=kOutput, calls=%fused_computation | convolution fusion | flops 67174400 | bytes 2490368 | tf_op jit(solution)/shard_map/lrw,liw->lri/dot_general | solution.py:191
  3.2 18.5 %all_to_all.25 = f32[32,8,128]{2,1,0:T(8,128)S(1)} all-to-all(f32[32,8,128]{2,1,0:T(8,128)S(1)} %bitcast.22), channel_id=1, replica_groups=mesh['zlo'=4,'y'=4,'core'=2,'zhi'=2,'x'=4] {'zlo','y','core'}, dimensions={0} | all-to-all | bytes 262144 | tf_op jit(solution)/shard_map/all_to_all | solution.py:193
  21.7 12.1 %all_to_all.26.left_ref = f32[32,8,128]{2,1,0:T(8,128)S(1)} all-to-all(f32[32,8,128]{2,1,0:T(8,128)S(1)} %broadcast_in_dim.2), channel_id=1, replica_groups=mesh['zlo'=4,'y'=4,'core'=2,'zhi'=2,'x'=4] {'zlo','y','core'}, dimensions={0} | all-to-all | bytes 262144 | tf_op jit(solution)/shard_map/all_to_all | solution.py:195
  33.8 0.0 copy-done
  33.8 0.7 shard_map.67
  34.5 0.0 copy-start.1
  34.5 0.0 copy-start.2
  34.5 14.6 %all_to_all.27 = f32[288,2,128]{2,1,0:T(2,128)S(1)} all-to-all(f32[288,2,128]{2,1,0:T(2,128)S(1)} %bitcast.17), channel_id=1, replica_groups=mesh['zlo'=4,'y'=4,'core'=2,'zhi'=2,'x'=4] {'y','core','x'}, dimensions={0} | all-to-all | bytes 589824 | tf_op jit(solution)/shard_map/all_to_all | solution.py:199
  49.1 12.0 %all_to_all.28.in_ref = f32[8,32,128]{2,1,0:T(8,128)S(1)} all-to-all(f32[8,32,128]{2,1,0:T(8,128)S(1)} %shard_map.68), channel_id=1, replica_groups=mesh['zlo'=4,'y'=4,'core'=2,'zhi'=2,'x'=4] {'zlo','zhi'}, dimensions={0} | all-to-all | bytes 262144 | tf_op jit(solution)/shard_map/all_to_all | solution.py:201
  61.2 0.7 shard_map.69
  61.9 5.8 %all-to-all-start.4 = ((f32[32,16,128]{2,1,0:T(8,128)}), f32[32,16,128]{2,1,0:T(8,128)S(1)}, u32[]{:S(2)}, u32[]{:S(2)}) async-start(f32[32,16,128]{2,1,0:T(8,128)} %get-tuple-element.10), calls=%async_computation.4 | async-start | bytes 524288 | tf_op jit(solution)/shard_map/all_to_all | solution.py:203
  67.7 3.2 %shard_map.70 = (f32[32,128]{1,0:T(8,128)S(1)}, f32[2,32,512]{2,1,0:T(8,128)S(1)}) custom-call(f32[16,128]{1,0:T(8,128)S(1)} %get-tuple-element.11.gram_ref, f32[32,8,128]{2,1,0:T(8,128)S(1)} %all_to_all.26.left_ref), custom_call_target="tpu_custom_call" | custom-call | flops 268435456 | bytes 262144 | tf_op jit(solution)/shard_map/pallas_call | solution.py:29
  70.8 5.7 %all-to-all-done.4 = f32[32,16,128]{2,1,0:T(8,128)S(1)} async-done(((f32[32,16,128]{2,1,0:T(8,128)}), f32[32,16,128]{2,1,0:T(8,128)S(1)}, u32[]{:S(2)}, u32[]{:S(2)}) %all-to-all-start.4) | async-done | bytes 262176 | tf_op jit(solution)/shard_map/all_to_all | solution.py:203
  76.6 0.0 copy-done.1
  76.6 0.0 copy-done.2
  76.6 1.6 %shard_map.71 = (f32[2,32,1024]{2,1,0:T(8,128)}, f32[2,32,512]{2,1,0:T(8,128)}, f32[2,32,512]{2,1,0:T(8,128)}) custom-call(f32[64,8,128]{2,1,0:T(8,128)S(1)} %bitcast.19, f32[32,128]{1,0:T(8,128)S(1)} %get-tuple-element.12.inverse_ref, f32[2,32,512]{2,1,0:T(8,128)S(1)} %get-tuple-element.13.frame_ref, f32[2,32,512]{2,1,0:T(8,128)S(1)} %bitcast.20, ...), custom_call_target="tpu_custom_call" | custom-call | flops 1048576 | bytes 262144 | tf_op jit(solution)/shard_map/pallas_call | solution.py:29
  (3 shorter events, 0.1 us)
Async XLA Ops:
  0.6 33.2 %copy-start = (bf16[1,2,512,1024]{3,2,1,0:T(8,128)(2,1)S(1)}, bf16[1,2,512,1024]{3,2,1,0:T(8,128)(2,1)}, u32[]{:S(2)}) copy-start(bf16[1,2,512,1024]{3,2,1,0:T(8,128)(2,1)} %param.4) | copy-start | bytes 6291460
  34.5 42.0 %copy-start.1 = (f32[2,512,32]{1,2,0:T(8,128)S(1)}, f32[2,512,32]{1,2,0:T(8,128)}, u32[]{:S(2)}) copy-start(f32[2,512,32]{1,2,0:T(8,128)} %param.6) | copy-start | bytes 393220
  34.5 42.0 %copy-start.2 = (f32[2,512,32]{1,2,0:T(8,128)S(1)}, f32[2,512,32]{1,2,0:T(8,128)}, u32[]{:S(2)}) copy-start(f32[2,512,32]{1,2,0:T(8,128)} %param.7) | copy-start | bytes 393220
  61.9 14.7 %all-to-all-start.4 = ((f32[32,16,128]{2,1,0:T(8,128)}), f32[32,16,128]{2,1,0:T(8,128)S(1)}, u32[]{:S(2)}, u32[]{:S(2)}) async-start(f32[32,16,128]{2,1,0:T(8,128)} %get-tuple-element.10), calls=%async_computation.4 | async-start | bytes 524288 | tf_op jit(solution)/shard_map/all_to_all | solution.py:203

commit v2 on v1

v2 whole, which is shorter than its diff:
```python
import functools

import jax
import jax.numpy as jnp
from jax import lax
from jax.experimental import pallas as pl
from jax.experimental.pallas import tpu as pltpu
from jax.sharding import Mesh
from jax.sharding import PartitionSpec as P

RANK = 32
LANES = 128
SIZES = {"zlo": 4, "y": 4, "core": 2, "zhi": 2, "x": 4}
REPLICA = ("zlo", "y", "core")
MODEL = ("zhi", "x")
LINES = ("zlo", "y")
PLANE = ("y", "x")
COLUMN = ("zlo", "zhi")
REPLICAS, PEERS, STACK = 32, 16, 8
CHUNK = 20
EXACT = lax.Precision.HIGHEST
VMEM_LIMIT = 24 * 1024 * 1024


def kernel_call(body, outs, flops=1 << 20, moved=1 << 18):
    many = isinstance(outs, (list, tuple))
    count = len(outs) if many else 1
    spec = pl.BlockSpec(memory_space=pltpu.VMEM)
    return lambda *args: pl.pallas_call(
        body,
        out_shape=outs,
        in_specs=[spec] * len(args),
        out_specs=[spec] * count if many else spec,
        compiler_params=pltpu.CompilerParams(vmem_limit_bytes=VMEM_LIMIT),
        cost_estimate=pl.CostEstimate(flops=flops, bytes_accessed=moved, transcendentals=0),
    )(*args)


def f32(*shape):
    return jax.ShapeDtypeStruct(shape, jnp.float32)


def joined(ref, rows, columns):
    return jnp.concatenate(
        [
            jnp.concatenate([ref[t * columns + j] for j in range(columns)], axis=1)
            for t in range(rows)
        ],
        axis=0,
    )


def lane_of(shape):
    return lax.broadcasted_iota(jnp.int32, shape, 1)


def row_of(shape):
    return lax.broadcasted_iota(jnp.int32, shape, 0)


def core():
    return lax.axis_index("core")


def left_body(mine, basis_ref, grads_ref, out_ref):
    layer = core() if mine else 1 - core()
    left = lax.dot_general(
        basis_ref[layer].astype(jnp.bfloat16),
        grads_ref[layer],
        (((1,), (1,)), ((), ())),
        preferred_element_type=jnp.float32,
    )
    for t in range(4):
        for j in range(4):
            out_ref[4 * t + j] = left[8 * t : 8 * t + 8, LANES * j : LANES * j + LANES]


def right_body(mine, left_ref, grads_ref, out_ref):
    layer = core() if mine else 1 - core()
    right = jnp.dot(
        joined(left_ref, 4, 4).astype(jnp.bfloat16),
        grads_ref[layer],
        preferred_element_type=jnp.float32,
    )
    for t in range(4):
        for j in range(8):
            d, h = divmod(8 * t + j, 2)
            out_ref[d, 8 * h : 8 * h + 8] = right[8 * t : 8 * t + 8, LANES * j : LANES * j + LANES]


def by_layer(mine_ref, other_ref):
    mine, other = joined(mine_ref, 4, 4), joined(other_ref, 4, 4)
    first = core() == 0
    return jnp.where(first, mine, other), jnp.where(first, other, mine)


def gram_body(mine_ref, other_ref, share_ref):
    left = jnp.concatenate(by_layer(mine_ref, other_ref), axis=0)
    twice = jnp.concatenate([left, left], axis=0)
    gram = lax.dot_general(
        left, twice, (((1,), (1,)), ((), ())), precision=EXACT, preferred_element_type=jnp.float32
    )
    lane = lane_of((16, LANES))
    packed = jnp.where(
        lane < 32,
        gram[0:16],
        jnp.where(lane < 64, gram[32:48], jnp.where(lane < 96, gram[16:32], gram[48:64])),
    )
    share_ref[...] = picked([packed[4 * s : 4 * s + 4] for s in range(4)], lax.axis_index("y"))


def picked(values, index):
    out = values[0]
    for s in range(1, len(values)):
        out = jnp.where(index == s, values[s], out)
    return out


def pack_body(mine_ref, other_ref, share_ref, out_ref):
    share = share_ref[...]
    for d in range(PEERS):
        out_ref[CHUNK * d : CHUNK * d + 16] = mine_ref[d] + other_ref[d]
        out_ref[CHUNK * d + 16 : CHUNK * d + CHUNK] = share


def plane_body(in_ref, out_ref):
    total = in_ref[0:16]
    for s in range(1, PEERS):
        total = total + in_ref[CHUNK * s : CHUNK * s + 16]
    parts = []
    for y in range(4):
        part = None
        for x in range(4):
            at = CHUNK * (4 * y + x) + 16
            piece = in_ref[at : at + 4]
            part = piece if part is None else part + piece
        parts.append(part)
    share = picked(parts, lax.axis_index("zlo"))
    for z in range(STACK):
        out_ref[CHUNK * z : CHUNK * z + 16] = total
        out_ref[CHUNK * z + 16 : CHUNK * z + CHUNK] = share


def column_body(in_ref, out_ref, gram_ref):
    total = in_ref[0:16]
    for s in range(1, STACK):
        total = total + in_ref[CHUNK * s : CHUNK * s + 16]
    for d in range(PEERS):
        out_ref[d] = total
    for q in range(4):
        at = 2 * CHUNK * q + 16
        gram_ref[4 * q : 4 * q + 4] = in_ref[at : at + 4] + in_ref[at + CHUNK : at + CHUNK + 4]


def factor_body(gram_ref, mine_ref, other_ref, inverse_ref, frame_ref):
    packed = gram_ref[...]
    shape = (RANK, LANES)
    lane, row = lane_of(shape), row_of(shape)
    gram = jnp.concatenate([packed, pltpu.roll(packed, 64, 1)], axis=0)
    first = (lane // RANK) % 2 == 0
    unit = (lane % RANK) == row
    diagonal = jnp.where(unit & (lane < 64), gram, 0.0)
    mean0 = jnp.sum(jnp.where(first, diagonal, 0.0)) * (1.0 / RANK)
    mean1 = jnp.sum(jnp.where(first, 0.0, diagonal)) * (1.0 / RANK)
    ridge = 0.001 * jnp.where(first, mean0, mean1)
    work = jnp.where(lane < 64, gram, 0.0) + jnp.where(unit, jnp.where(lane < 64, ridge, 1.0), 0.0)
    pivots = jnp.ones(shape, jnp.float32)
    for k in range(RANK):
        column = jnp.where(first, work[:, k : k + 1], work[:, RANK + k : RANK + k + 1])
        pivot = column[k : k + 1]
        pivots = jnp.where(row == k, column, pivots)
        if k + 1 < RANK:
            step = work[k : k + 1] / pivot
            work = work - jnp.where(row > k, column * step, 0.0)
    inverse = pltpu.roll(work / jnp.sqrt(pivots), 64, 1)
    inverse_ref[...] = inverse
    left = by_layer(mine_ref, other_ref)
    for l in range(2):
        frame_ref[l] = (
            jnp.dot(
                inverse[:, l * RANK : (l + 1) * RANK],
                left[l],
                precision=EXACT,
                preferred_element_type=jnp.float32,
            )
            * (1.0 / REPLICAS)
        )


def settle(layer, right_ref, inverse_ref, frame_ref, weights_ref, momentum_ref):
    place = (lax.axis_index("zlo") * 4 + lax.axis_index("y")) * 2 + core()
    block = place // 4
    shift = (4 - place % 4) * 32
    square = jnp.zeros((8, LANES), jnp.float32)
    for i in range(32):
        tile = right_ref[i]
        square = square + tile * tile
    scale = lax.rsqrt(jnp.sum(square) * (1.0 / (RANK * 1024)) + 1e-12)
    own = jnp.concatenate([right_ref[8 * t + block] for t in range(4)], axis=0)
    inverse = inverse_ref[...]
    inverse = jnp.where(layer == 0, inverse[:, :RANK], inverse[:, RANK : 2 * RANK])
    half = jnp.dot(inverse, own, precision=EXACT, preferred_element_type=jnp.float32)
    half = pltpu.roll(half, shift, 1)[:, :RANK]
    change = lax.dot_general(
        half,
        frame_ref[layer],
        (((0,), (0,)), ((), ())),
        precision=EXACT,
        preferred_element_type=jnp.float32,
    )
    new = 0.9 * momentum_ref[layer] + change
    return scale, new, weights_ref[layer] - 0.02 * new


def scaled(right_ref, scale, basis_ref, layer):
    for t in range(4):
        for j in range(8):
            at = (slice(8 * t, 8 * t + 8), slice(LANES * j, LANES * j + LANES))
            at = at if layer is None else (layer, *at)
            basis_ref[at] = right_ref[8 * t + j] * scale


def early_body(right_ref, inverse_ref, frame_ref, weights_ref, momentum_ref, basis_ref, w_ref, m_ref):
    scale, new, weights = settle(core(), right_ref, inverse_ref, frame_ref, weights_ref, momentum_ref)
    scaled(right_ref, scale, basis_ref, None)
    m_ref[...] = new
    w_ref[...] = weights


def late_body(
    right_ref, inverse_ref, frame_ref, weights_ref, momentum_ref, b_ref, w_ref, m_ref,
    basis_ref, new_w_ref, new_m_ref,
):
    c = core()
    basis_ref[c] = b_ref[...]
    new_w_ref[c] = w_ref[...]
    new_m_ref[c] = m_ref[...]
    layer = 1 - c
    scale, new, weights = settle(layer, right_ref, inverse_ref, frame_ref, weights_ref, momentum_ref)
    scaled(right_ref, scale, basis_ref, layer)
    new_m_ref[layer] = new
    new_w_ref[layer] = weights


def swapped(value):
    return lax.ppermute(value, "core", [(0, 1), (1, 0)])


def all_to_all(value, axes):
    return lax.all_to_all(value, axes, 0, 0, tiled=True)


def shards(layer_grads, last_basis, layer_weights, momentum):
    grads = layer_grads[0]
    layers, rows, width = grads.shape
    basis = jnp.swapaxes(last_basis, 1, 2)
    weights, momentum = jnp.swapaxes(layer_weights, 1, 2), jnp.swapaxes(momentum, 1, 2)
    lefts, rights = f32(PEERS, 8, LANES), f32(PEERS, 16, LANES)

    away = swapped(kernel_call(functools.partial(left_body, False), lefts)(basis, grads))
    mine = kernel_call(functools.partial(left_body, True), lefts)(basis, grads)
    tile = jnp.sum(all_to_all(mine + away, LINES), axis=0)
    mine = all_to_all(jnp.broadcast_to(tile[None], lefts.shape), LINES)
    other = swapped(mine)
    kept = kernel_call(functools.partial(right_body, True), rights)(mine, grads)
    kept, other = lax.optimization_barrier((kept, other))
    away = swapped(kernel_call(functools.partial(right_body, False), rights)(other, grads))
    share = kernel_call(gram_body, f32(4, LANES))(mine, other)

    sent = kernel_call(pack_body, f32(PEERS * CHUNK, LANES))(kept, away, share)
    came = all_to_all(sent.reshape(PEERS * CHUNK // 4, 4, LANES), PLANE)
    sent = kernel_call(plane_body, f32(STACK * CHUNK, LANES))(came.reshape(-1, LANES))
    came = all_to_all(sent.reshape(STACK * CHUNK // 4, 4, LANES), COLUMN)
    sent, gram = kernel_call(column_body, [rights, f32(16, LANES)])(came.reshape(-1, LANES))
    right = all_to_all(sent, PLANE)
    inverse, frame = kernel_call(
        factor_body, [f32(RANK, LANES), f32(layers, RANK, rows)], flops=1 << 28
    )(gram, mine, other)
    right, inverse, frame = lax.optimization_barrier((right.reshape(32, 8, LANES), inverse, frame))
    late = swapped(right)
    solved = (inverse, frame, weights, momentum)
    early = kernel_call(
        early_body, [f32(RANK, width), f32(RANK, rows), f32(RANK, rows)]
    )(right, *solved)
    new_basis, new_weights, new_momentum = kernel_call(
        late_body,
        [f32(layers, RANK, width), f32(layers, RANK, rows), f32(layers, RANK, rows)],
    )(late, *solved, *early)
    return tuple(jnp.swapaxes(a, 1, 2) for a in (new_weights, new_basis, new_momentum))


def solution(mesh):
    fine = Mesh(mesh.devices.reshape(tuple(SIZES.values())), tuple(SIZES))
    sharded = P(None, MODEL, REPLICA)
    return jax.shard_map(
        shards,
        mesh=fine,
        in_specs=(P(REPLICA, None, MODEL, None), P(), sharded, sharded),
        out_specs=(sharded, P(), sharded),
        check_vma=False,
    )
```

time: 78.5 us -> 78.4 us (level)
  blocking collectives: 57.2 us -> 47 us
  starting transfers between devices: 5.78 us -> 14.5 us
  matrix products: 2.54 us -> 0 us
  local copies, waits for them, and re-layouts: 0.03 us -> 2.56 us
  Pallas kernels: 6.24 us -> 7.48 us
    ppermute x0 -> x4, starting transfers between devices: none -> 11 us  [swapped(): return lax.ppermute(value, 'core', [(0, 1), (1, 0)])]
    all_to_all x4, blocking collectives: 57.2 us -> 47 us  [all_to_all(): return lax.all_to_all(value, axes, 0, 0, tiled=True)]
    dot_general x1 -> x0, matrix products: 2.54 us -> none  [shards(): jnp.einsum('lrw,liw->lri', basis, grads, preferred_element_type=jnp.float32)]
    unnamed x6 -> x10, local copies, waits for them, and re-layouts: 0.01 us -> 2.55 us
    all_to_all x1, starting transfers between devices: 5.78 us -> 3.51 us  [all_to_all(): return lax.all_to_all(value, axes, 0, 0, tiled=True)]
    ppermute x0 -> x4, waiting for transfers between devices: none -> 2.13 us  [swapped(): return lax.ppermute(value, 'core', [(0, 1), (1, 0)])]
    all_to_all x1, waiting for transfers between devices: 5.71 us -> 3.63 us  [all_to_all(): return lax.all_to_all(value, axes, 0, 0, tiled=True)]
    pallas_call x5 -> x11, Pallas kernels: 6.24 us -> 7.48 us  [kernel_call(): pl.pallas_call(body, out_shape=outs, in_specs=[spec] * len(args), out_spe...]
  transfers between devices with their start and end apart: 1 -> 5, of which waited for: 1 -> 5; matrix products, arithmetic and copies ran while one was open for 0% -> 0% of each run, Pallas kernels for 4% -> 6%
where the time goes in v2:
time: 78.4 us; the launch traced here: 78 us
  blocking collectives  47 us (60%)
  starting transfers between devices  14.5 us (18%)
  Pallas kernels  7.48 us (10%)
  waiting for transfers between devices  5.76 us (7%)
  local copies, waits for them, and re-layouts  2.56 us (3%)
    all_to_all x4, blocking collectives, all_to_all(): return lax.all_to_all(value, axes, 0, 0, tiled=True)  47 us
    ppermute x4, starting transfers between devices, swapped(): return lax.ppermute(value, 'core', [(0, 1), (1, 0)])  11 us
    pallas_call x11, Pallas kernels, kernel_call(): pl.pallas_call(body, out_shape=outs, in_specs=[spec] * len(args), out_spe...  7.48 us
    all_to_all x1, waiting for transfers between devices, all_to_all(): return lax.all_to_all(value, axes, 0, 0, tiled=True)  3.63 us
    all_to_all x1, starting transfers between devices, all_to_all(): return lax.all_to_all(value, axes, 0, 0, tiled=True)  3.51 us
    unnamed x10, local copies, waits for them, and re-layouts  2.55 us
    ppermute x4, waiting for transfers between devices, swapped(): return lax.ppermute(value, 'core', [(0, 1), (1, 0)])  2.13 us
  transfers between devices with their start and end apart: 5, of which 5 were waited for; matrix products, arithmetic and copies ran while one was open for 0% of the time, Pallas kernels for 6%

profile of v2, /device:TPU:1, one launch (start us, length us, event | category | flops | bytes accessed | tf_op | source)
XLA Modules:
  0.0 78.0 jit_solution(4961397319362381302)
XLA Ops:
  0.6 0.0 copy-start
  0.6 1.6 %copy-done = bf16[1,2,512,1024]{3,2,1,0:T(8,128)(2,1)S(1)} copy-done((bf16[1,2,512,1024]{3,2,1,0:T(8,128)(2,1)S(1)}, bf16[1,2,512,1024]{3,2,1,0:T(8,128)(2,1)}, u32[]{:S(2)}) %copy-start) | copy-done | bytes 2097176
  2.2 0.0 copy-start.2
  2.2 0.9 %copy-done.2 = f32[2,1024,32]{1,2,0:T(8,128)S(1)} copy-done((f32[2,1024,32]{1,2,0:T(8,128)S(1)}, f32[2,1024,32]{1,2,0:T(8,128)}, u32[]{:S(2)}) %copy-start.2) | copy-done | bytes 262168
  3.2 0.4 shard_map.68
  3.6 0.0 copy-start.1
  3.6 3.3 %collective-permute-start = (f32[16,8,128]{2,1,0:T(8,128)S(1)}, f32[16,8,128]{2,1,0:T(8,128)S(1)}, u32[]{:S(2)}, u32[]{:S(2)}) collective-permute-start(f32[16,8,128]{2,1,0:T(8,128)S(1)} %shard_map.68), channel_id=1, source_target_pairs={{0,8},{8,0},{1,9},{9,1},{2,10},{10,2},{3,11},{11,3},{4,12},{12,4},... | collective-permute-start | bytes 196616 | tf_op jit(solution)/shard_map/ppermute | solution.py:246
  6.9 0.4 shard_map.67
  7.3 0.5 collective-permute-done
  7.8 13.7 %all_to_all.25 = f32[16,8,128]{2,1,0:T(8,128)S(1)} all-to-all(f32[16,8,128]{2,1,0:T(8,128)S(1)} %add.3), channel_id=1, replica_groups=mesh['zlo'=4,'y'=4,'core'=2,'zhi'=2,'x'=4] {'zlo','y'}, dimensions={0} | all-to-all | bytes 131072 | tf_op jit(solution)/shard_map/all_to_all | solution.py:250
  21.5 9.9 %all_to_all.26.left_ref.mine_ref = f32[16,8,128]{2,1,0:T(8,128)S(1)} all-to-all(f32[16,8,128]{2,1,0:T(8,128)S(1)} %broadcast_in_dim.2), channel_id=1, replica_groups=mesh['zlo'=4,'y'=4,'core'=2,'zhi'=2,'x'=4] {'zlo','y'}, dimensions={0} | all-to-all | bytes 131072 | tf_op jit(solution)/shard_map/all_to_all | solution.py:250
  31.4 2.8 %collective-permute-start.1 = (f32[16,8,128]{2,1,0:T(8,128)S(1)}, f32[16,8,128]{2,1,0:T(8,128)S(1)}, u32[]{:S(2)}, u32[]{:S(2)}) collective-permute-start(f32[16,8,128]{2,1,0:T(8,128)S(1)} %all_to_all.26.left_ref.mine_ref), channel_id=1, source_target_pairs={{0,8},{8,0},{1,9},{9,1},{2,10},{10,2},{3,11},{11,3},{4,12},{12,4},... | collective-permute-start | bytes 196616 | tf_op jit(solution)/shard_map/ppermute | solution.py:246
  34.3 0.0 copy-done.1
  34.3 0.3 shard_map.69.mine_ref
  34.6 0.0 copy-start.3
  34.6 0.6 collective-permute-done.1.left_ref.other_ref
  35.2 0.3 shard_map.70
  35.5 0.4 collective-permute-start.2
  35.8 0.4 shard_map.71.share_ref
  36.2 0.6 collective-permute-done.2.other_ref
  36.9 11.3 %all_to_all.27 = f32[80,4,128]{2,1,0:T(4,128)S(1)} all-to-all(f32[80,4,128]{2,1,0:T(4,128)S(1)} %bitcast.18), channel_id=1, replica_groups=mesh['zlo'=4,'y'=4,'core'=2,'zhi'=2,'x'=4] {'y','x'}, dimensions={0} | all-to-all | bytes 327680 | tf_op jit(solution)/shard_map/all_to_all | solution.py:250
  48.2 12.0 %all_to_all.28 = f32[40,4,128]{2,1,0:T(4,128)S(1)} all-to-all(f32[40,4,128]{2,1,0:T(4,128)S(1)} %bitcast.27), channel_id=1, replica_groups=mesh['zlo'=4,'y'=4,'core'=2,'zhi'=2,'x'=4] {'zlo','zhi'}, dimensions={0} | all-to-all | bytes 163840 | tf_op jit(solution)/shard_map/all_to_all | solution.py:250
  60.2 0.7 shard_map.74
  60.9 3.5 %all-to-all-start.4 = ((f32[16,16,128]{2,1,0:T(8,128)}), f32[16,16,128]{2,1,0:T(8,128)S(1)}, u32[]{:S(2)}, u32[]{:S(2)}) async-start(f32[16,16,128]{2,1,0:T(8,128)} %get-tuple-element.20), calls=%async_computation.4 | async-start | bytes 262144 | tf_op jit(solution)/shard_map/all_to_all | solution.py:250
  64.4 3.2 %shard_map.75 = (f32[32,128]{1,0:T(8,128)S(1)}, f32[2,32,512]{2,1,0:T(8,128)S(1)}) custom-call(f32[16,128]{1,0:T(8,128)S(1)} %get-tuple-element.21.gram_ref, f32[16,8,128]{2,1,0:T(8,128)S(1)} %all_to_all.26.left_ref.mine_ref, f32[16,8,128]{2,1,0:T(8,128)S(1)} %collective-permute-done.1.left_ref.other_ref), custom_call_target="tpu_custom_call" | custom-call | flops 268435456 | bytes 262144 | tf_op jit(solution)/shard_map/pallas_call | solution.py:29
  67.6 3.6 %all-to-all-done.4 = f32[16,16,128]{2,1,0:T(8,128)S(1)} async-done(((f32[16,16,128]{2,1,0:T(8,128)}), f32[16,16,128]{2,1,0:T(8,128)S(1)}, u32[]{:S(2)}, u32[]{:S(2)}) %all-to-all-start.4) | async-done | bytes 131104 | tf_op jit(solution)/shard_map/all_to_all | solution.py:250
  71.2 4.5 %collective-permute-start.3 = (f32[32,8,128]{2,1,0:T(8,128)S(1)}, f32[32,8,128]{2,1,0:T(8,128)S(1)}, u32[]{:S(2)}, u32[]{:S(2)}) collective-permute-start(f32[32,8,128]{2,1,0:T(8,128)S(1)} %bitcast.24), channel_id=1, source_target_pairs={{0,8},{8,0},{1,9},{9,1},{2,10},{10,2},{3,11},{11,3},{4,12},{12,4},... | collective-permute-start | bytes 393224 | tf_op jit(solution)/shard_map/ppermute | solution.py:246
  75.7 0.0 copy-done.3
  75.7 0.0 copy-done.4
  75.7 0.5 shard_map.76
  76.3 0.4 collective-permute-done.3.right_ref
  76.7 1.3 %shard_map.77 = (f32[2,32,1024]{2,1,0:T(8,128)}, f32[2,32,512]{2,1,0:T(8,128)}, f32[2,32,512]{2,1,0:T(8,128)}) custom-call(f32[32,8,128]{2,1,0:T(8,128)S(1)} %collective-permute-done.3.right_ref, f32[32,128]{1,0:T(8,128)S(1)} %get-tuple-element.25.inverse_ref, f32[2,32,512]{2,1,0:T(8,128)S(1)} %get-tuple-element.26.frame_ref, f32[2,32,512]{2,1,0:T(8,128)S(1)} %bitcast.21, ...), custom_call_target="tpu_custom_call" | custom-call | flops 1048576 | bytes 262144 | tf_op jit(solution)/shard_map/pallas_call | solution.py:29
  (6 shorter events, 0.1 us)
Async XLA Ops:
  0.6 1.6 %copy-start = (bf16[1,2,512,1024]{3,2,1,0:T(8,128)(2,1)S(1)}, bf16[1,2,512,1024]{3,2,1,0:T(8,128)(2,1)}, u32[]{:S(2)}) copy-start(bf16[1,2,512,1024]{3,2,1,0:T(8,128)(2,1)} %param.4) | copy-start | bytes 6291460
  2.2 0.9 %copy-start.2 = (f32[2,1024,32]{1,2,0:T(8,128)S(1)}, f32[2,1024,32]{1,2,0:T(8,128)}, u32[]{:S(2)}) copy-start(f32[2,1024,32]{1,2,0:T(8,128)} %param.5) | copy-start | bytes 786436
  3.6 30.7 %copy-start.1 = (bf16[1,2,512,1024]{3,2,1,0:T(8,128)(2,1)S(1)}, bf16[1,2,512,1024]{3,2,1,0:T(8,128)(2,1)}, u32[]{:S(2)}) copy-start(bf16[1,2,512,1024]{3,2,1,0:T(8,128)(2,1)} %param.4) | copy-start | bytes 6291460
  3.6 4.2 %collective-permute-start = (f32[16,8,128]{2,1,0:T(8,128)S(1)}, f32[16,8,128]{2,1,0:T(8,128)S(1)}, u32[]{:S(2)}, u32[]{:S(2)}) collective-permute-start(f32[16,8,128]{2,1,0:T(8,128)S(1)} %shard_map.68), channel_id=1, source_target_pairs={{0,8},{8,0},{1,9},{9,1},{2,10},{10,2},{3,11},{11,3},{4,12},{12,4},... | collective-permute-start | bytes 196616 | tf_op jit(solution)/shard_map/ppermute | solution.py:246
  31.4 3.8 %collective-permute-start.1 = (f32[16,8,128]{2,1,0:T(8,128)S(1)}, f32[16,8,128]{2,1,0:T(8,128)S(1)}, u32[]{:S(2)}, u32[]{:S(2)}) collective-permute-start(f32[16,8,128]{2,1,0:T(8,128)S(1)} %all_to_all.26.left_ref.mine_ref), channel_id=1, source_target_pairs={{0,8},{8,0},{1,9},{9,1},{2,10},{10,2},{3,11},{11,3},{4,12},{12,4},... | collective-permute-start | bytes 196616 | tf_op jit(solution)/shard_map/ppermute | solution.py:246
  34.6 41.1 %copy-start.3 = (f32[2,512,32]{1,2,0:T(8,128)S(1)}, f32[2,512,32]{1,2,0:T(8,128)}, u32[]{:S(2)}) copy-start(f32[2,512,32]{1,2,0:T(8,128)} %param.6) | copy-start | bytes 393220
  34.6 41.1 %copy-start.4 = (f32[2,512,32]{1,2,0:T(8,128)S(1)}, f32[2,512,32]{1,2,0:T(8,128)}, u32[]{:S(2)}) copy-start(f32[2,512,32]{1,2,0:T(8,128)} %param.7) | copy-start | bytes 393220
  35.5 1.4 %collective-permute-start.2 = (f32[16,16,128]{2,1,0:T(8,128)S(1)}, f32[16,16,128]{2,1,0:T(8,128)S(1)}, u32[]{:S(2)}, u32[]{:S(2)}) collective-permute-start(f32[16,16,128]{2,1,0:T(8,128)S(1)} %shard_map.70), channel_id=1, source_target_pairs={{0,8},{8,0},{1,9},{9,1},{2,10},{10,2},{3,11},{11,3},{4,12},{12,4},... | collective-permute-start | bytes 393224 | tf_op jit(solution)/shard_map/ppermute | solution.py:246
  60.9 10.3 %all-to-all-start.4 = ((f32[16,16,128]{2,1,0:T(8,128)}), f32[16,16,128]{2,1,0:T(8,128)S(1)}, u32[]{:S(2)}, u32[]{:S(2)}) async-start(f32[16,16,128]{2,1,0:T(8,128)} %get-tuple-element.20), calls=%async_computation.4 | async-start | bytes 262144 | tf_op jit(solution)/shard_map/all_to_all | solution.py:250
  71.2 5.5 %collective-permute-start.3 = (f32[32,8,128]{2,1,0:T(8,128)S(1)}, f32[32,8,128]{2,1,0:T(8,128)S(1)}, u32[]{:S(2)}, u32[]{:S(2)}) collective-permute-start(f32[32,8,128]{2,1,0:T(8,128)S(1)} %bitcast.24), channel_id=1, source_target_pairs={{0,8},{8,0},{1,9},{9,1},{2,10},{10,2},{3,11},{11,3},{4,12},{12,4},... | collective-permute-start | bytes 393224 | tf_op jit(solution)/shard_map/ppermute | solution.py:246

commit v3 on v2

--- a/solution.py
+++ b/solution.py
@@ -13,7 +13,6 @@
 SIZES = {"zlo": 4, "y": 4, "core": 2, "zhi": 2, "x": 4}
 REPLICA = ("zlo", "y", "core")
 MODEL = ("zhi", "x")
-LINES = ("zlo", "y")
 PLANE = ("y", "x")
 COLUMN = ("zlo", "zhi")
 REPLICAS, PEERS, STACK = 32, 16, 8
@@ -62,14 +61,39 @@
     return lax.axis_index("core")
 
 
-def left_body(mine, basis_ref, grads_ref, out_ref):
-    layer = core() if mine else 1 - core()
-    left = lax.dot_general(
-        basis_ref[layer].astype(jnp.bfloat16),
-        grads_ref[layer],
+ROWS = 128
+
+
+def left_of(basis, grads):
+    return lax.dot_general(
+        basis.astype(jnp.bfloat16),
+        grads,
         (((1,), (1,)), ((), ())),
         preferred_element_type=jnp.float32,
     )
+
+
+def first_body(basis_hbm, grads_hbm, out_ref, grads_ref, basis_ref, sems):
+    c = core()
+    whole = pltpu.make_async_copy(basis_hbm, basis_ref, sems.at[8])
+    whole.start()
+    copies = []
+    for k in range(8):
+        at = (1 - c if k < 4 else c, pl.ds(ROWS * (k % 4), ROWS))
+        copies.append(pltpu.make_async_copy(grads_hbm.at[at], grads_ref.at[at], sems.at[k]))
+        copies[-1].start()
+    whole.wait()
+    for j in range(4):
+        copies[j].wait()
+        left = left_of(basis_ref[1 - c], grads_ref[1 - c, ROWS * j : ROWS * (j + 1)])
+        for t in range(4):
+            out_ref[4 * t + j] = left[8 * t : 8 * t + 8]
+    for k in range(4, 8):
+        copies[k].wait()
+
+
+def left_body(basis_ref, grads_ref, out_ref):
+    left = left_of(basis_ref[core()], grads_ref[core()])
     for t in range(4):
         for j in range(4):
             out_ref[4 * t + j] = left[8 * t : 8 * t + 8, LANES * j : LANES * j + LANES]
@@ -257,10 +281,21 @@
     weights, momentum = jnp.swapaxes(layer_weights, 1, 2), jnp.swapaxes(momentum, 1, 2)
     lefts, rights = f32(PEERS, 8, LANES), f32(PEERS, 16, LANES)
 
-    away = swapped(kernel_call(functools.partial(left_body, False), lefts)(basis, grads))
-    mine = kernel_call(functools.partial(left_body, True), lefts)(basis, grads)
-    tile = jnp.sum(all_to_all(mine + away, LINES), axis=0)
-    mine = all_to_all(jnp.broadcast_to(tile[None], lefts.shape), LINES)
+    anywhere = pl.BlockSpec(memory_space=pltpu.HBM)
+    local = pl.BlockSpec(memory_space=pltpu.VMEM)
+    away, grads, basis = pl.pallas_call(
+        first_body,
+        out_shape=[lefts, jax.ShapeDtypeStruct(grads.shape, grads.dtype), f32(*basis.shape)],
+        in_specs=[anywhere] * 2,
+        out_specs=[local] * 3,
+        scratch_shapes=[pltpu.SemaphoreType.DMA((9,))],
+        compiler_params=pltpu.CompilerParams(vmem_limit_bytes=VMEM_LIMIT),
+        cost_estimate=pl.CostEstimate(flops=1 << 20, bytes_accessed=1 << 18, transcendentals=0),
+    )(*(pltpu.with_memory_space_constraint(a, pltpu.HBM) for a in (basis, grads)))
+    away = swapped(away)
+    mine = kernel_call(left_body, lefts)(basis, grads) + away
+    for axis, bit in (("y", 1), ("y", 3), ("zlo", 1), ("zlo", 2)):
+        mine = mine + lax.ppermute(mine, axis, [(i, i ^ bit) for i in range(SIZES[axis])])
     other = swapped(mine)
     kept = kernel_call(functools.partial(right_body, True), rights)(mine, grads)
     kept, other = lax.optimization_barrier((kept, other))

time: 78.4 us -> 74.7 us (0.953)
  blocking collectives: 47 us -> 26.4 us
  waiting for transfers between devices: 5.76 us -> 18.1 us
  starting transfers between devices: 14.5 us -> 19.9 us
  local copies, waits for them, and re-layouts: 2.56 us -> 0.01 us
  Pallas kernels: 7.48 us -> 9.22 us
    all_to_all x4 -> x2, blocking collectives: 47 us -> 26.4 us  [all_to_all(): return lax.all_to_all(value, axes, 0, 0, tiled=True)]
    ppermute x0 -> x4, waiting for transfers between devices: none -> 12.4 us  [shards(): lax.ppermute(mine, axis, [(i, i ^ bit) for i in range(SIZES[axis])])]
    ppermute x0 -> x4, starting transfers between devices: none -> 2.91 us  [shards(): lax.ppermute(mine, axis, [(i, i ^ bit) for i in range(SIZES[axis])])]
    unnamed x10 -> x4, local copies, waits for them, and re-layouts: 2.55 us -> 0.01 us
    ppermute x4, starting transfers between devices: 11 us -> 13.5 us  [swapped(): return lax.ppermute(value, 'core', [(0, 1), (1, 0)])]
    pallas_call x0 -> x1, Pallas kernels: none -> 2.14 us  [shards(): pl.pallas_call(first_body, out_shape=[lefts, jax.ShapeDtypeStruct(grads.s...]
    pallas_call x11 -> x10, Pallas kernels: 7.48 us -> 7.07 us  [kernel_call(): pl.pallas_call(body, out_shape=outs, in_specs=[spec] * len(args), out_spe...]
  transfers between devices with their start and end apart: 5 -> 9, of which waited for: 5 -> 9; matrix products, arithmetic and copies ran while one was open for 0% -> 0% of each run, Pallas kernels for 6% -> 6%
where the time goes in v3:
time: 74.7 us; the launch traced here: 74.4 us
  blocking collectives  26.4 us (35%)
  starting transfers between devices  19.9 us (27%)
  waiting for transfers between devices  18.1 us (24%)
  Pallas kernels  9.22 us (12%)
    all_to_all x2, blocking collectives, all_to_all(): return lax.all_to_all(value, axes, 0, 0, tiled=True)  26.4 us
    ppermute x4, starting transfers between devices, swapped(): return lax.ppermute(value, 'core', [(0, 1), (1, 0)])  13.5 us
    ppermute x4, waiting for transfers between devices, shards(): lax.ppermute(mine, axis, [(i, i ^ bit) for i in range(SIZES[axis])])  12.4 us
    pallas_call x10, Pallas kernels, kernel_call(): pl.pallas_call(body, out_shape=outs, in_specs=[spec] * len(args), out_spe...  7.07 us
    all_to_all x1, waiting for transfers between devices, all_to_all(): return lax.all_to_all(value, axes, 0, 0, tiled=True)  3.63 us
    all_to_all x1, starting transfers between devices, all_to_all(): return lax.all_to_all(value, axes, 0, 0, tiled=True)  3.51 us
    ppermute x4, starting transfers between devices, shards(): lax.ppermute(mine, axis, [(i, i ^ bit) for i in range(SIZES[axis])])  2.91 us
    pallas_call x1, Pallas kernels, shards(): pl.pallas_call(first_body, out_shape=[lefts, jax.ShapeDtypeStruct(grads.s...  2.14 us
  transfers between devices with their start and end apart: 9, of which 9 were waited for; matrix products, arithmetic and copies ran while one was open for 0% of the time, Pallas kernels for 6%

profile of v3, /device:TPU:1, one launch (start us, length us, event | category | flops | bytes accessed | tf_op | source)
XLA Modules:
  0.0 74.4 jit_solution(15830958323599176853)
XLA Ops:
  0.6 2.1 %shard_map.67 = (f32[16,8,128]{2,1,0:T(8,128)S(1)}, bf16[2,512,1024]{2,1,0:T(8,128)(2,1)S(1)}, f32[2,32,1024]{2,1,0:T(8,128)S(1)}) custom-call(f32[2,32,1024]{2,1,0:T(8,128)} %bitcast.23, bf16[2,512,1024]{2,1,0:T(8,128)(2,1)} %bitcast.22), custom_call_target="tpu_custom_call" | custom-call | flops 1048576 | bytes 262144 | tf_op jit(solution)/shard_map/pallas_call | solution.py:286
  2.8 3.3 %collective-permute-start = (f32[16,8,128]{2,1,0:T(8,128)S(1)}, f32[16,8,128]{2,1,0:T(8,128)S(1)}, u32[]{:S(2)}, u32[]{:S(2)}) collective-permute-start(f32[16,8,128]{2,1,0:T(8,128)S(1)} %get-tuple-element.23), channel_id=1, source_target_pairs={{0,8},{8,0},{1,9},{9,1},{2,10},{10,2},{3,11},{11,3},{4,12},{12,4},... | collective-permute-start | bytes 196616 | tf_op jit(solution)/shard_map/ppermute | solution.py:270
  6.1 0.4 shard_map.68
  6.5 0.5 collective-permute-done
  7.0 0.1 collective-permute-start.1
  7.1 3.1 %collective-permute-done.1 = f32[16,8,128]{2,1,0:T(8,128)S(1)} collective-permute-done((f32[16,8,128]{2,1,0:T(8,128)S(1)}, f32[16,8,128]{2,1,0:T(8,128)S(1)}, u32[]{:S(2)}, u32[]{:S(2)}) %collective-permute-start.1) | collective-permute-done | bytes 65568 | tf_op jit(solution)/shard_map/ppermute | solution.py:298
  10.2 1.1 %collective-permute-start.2 = (f32[16,8,128]{2,1,0:T(8,128)S(1)}, f32[16,8,128]{2,1,0:T(8,128)S(1)}, u32[]{:S(2)}, u32[]{:S(2)}) collective-permute-start(f32[16,8,128]{2,1,0:T(8,128)S(1)} %add.16), channel_id=1, source_target_pairs={{0,48},{16,32},{32,16},{48,0},{1,49},{17,33},{33,17},{49,1},{2,50}... | collective-permute-start | bytes 196616 | tf_op jit(solution)/shard_map/ppermute | solution.py:298
  11.3 3.3 %collective-permute-done.2 = f32[16,8,128]{2,1,0:T(8,128)S(1)} collective-permute-done((f32[16,8,128]{2,1,0:T(8,128)S(1)}, f32[16,8,128]{2,1,0:T(8,128)S(1)}, u32[]{:S(2)}, u32[]{:S(2)}) %collective-permute-start.2) | collective-permute-done | bytes 65568 | tf_op jit(solution)/shard_map/ppermute | solution.py:298
  14.6 0.1 collective-permute-start.3
  14.7 3.1 %collective-permute-done.3 = f32[16,8,128]{2,1,0:T(8,128)S(1)} collective-permute-done((f32[16,8,128]{2,1,0:T(8,128)S(1)}, f32[16,8,128]{2,1,0:T(8,128)S(1)}, u32[]{:S(2)}, u32[]{:S(2)}) %collective-permute-start.3) | collective-permute-done | bytes 65568 | tf_op jit(solution)/shard_map/ppermute | solution.py:298
  17.8 1.6 %collective-permute-start.4 = (f32[16,8,128]{2,1,0:T(8,128)S(1)}, f32[16,8,128]{2,1,0:T(8,128)S(1)}, u32[]{:S(2)}, u32[]{:S(2)}) collective-permute-start(f32[16,8,128]{2,1,0:T(8,128)S(1)} %add.18), channel_id=1, source_target_pairs={{0,128},{64,192},{128,0},{192,64},{1,129},{65,193},{129,1},{193,65... | collective-permute-start | bytes 196616 | tf_op jit(solution)/shard_map/ppermute | solution.py:298
  19.5 2.9 %collective-permute-done.4 = f32[16,8,128]{2,1,0:T(8,128)S(1)} collective-permute-done((f32[16,8,128]{2,1,0:T(8,128)S(1)}, f32[16,8,128]{2,1,0:T(8,128)S(1)}, u32[]{:S(2)}, u32[]{:S(2)}) %collective-permute-start.4) | collective-permute-done | bytes 65568 | tf_op jit(solution)/shard_map/ppermute | solution.py:298
  22.3 5.4 %collective-permute-start.5 = (f32[16,8,128]{2,1,0:T(8,128)S(1)}, f32[16,8,128]{2,1,0:T(8,128)S(1)}, u32[]{:S(2)}, u32[]{:S(2)}) collective-permute-start(f32[16,8,128]{2,1,0:T(8,128)S(1)} %add.19.left_ref.mine_ref), channel_id=1, source_target_pairs={{0,8},{8,0},{1,9},{9,1},{2,10},{10,2},{3,11},{11,3},{4,12},{12,4},... | collective-permute-start | bytes 196616 | tf_op jit(solution)/shard_map/ppermute | solution.py:270
  27.7 0.3 shard_map.69.mine_ref
  28.0 0.0 copy-start
  28.0 0.6 collective-permute-done.5.left_ref.other_ref
  28.6 0.3 shard_map.70
  28.9 0.4 collective-permute-start.6
  29.3 0.4 shard_map.71.share_ref
  29.7 0.6 collective-permute-done.6.other_ref
  30.3 11.8 %all_to_all.15 = f32[80,4,128]{2,1,0:T(4,128)S(1)} all-to-all(f32[80,4,128]{2,1,0:T(4,128)S(1)} %bitcast.12), channel_id=1, replica_groups=mesh['zlo'=4,'y'=4,'core'=2,'zhi'=2,'x'=4] {'y','x'}, dimensions={0} | all-to-all | bytes 327680 | tf_op jit(solution)/shard_map/all_to_all | solution.py:274
  42.1 14.7 %all_to_all.16 = f32[40,4,128]{2,1,0:T(4,128)S(1)} all-to-all(f32[40,4,128]{2,1,0:T(4,128)S(1)} %bitcast.21), channel_id=1, replica_groups=mesh['zlo'=4,'y'=4,'core'=2,'zhi'=2,'x'=4] {'zlo','zhi'}, dimensions={0} | all-to-all | bytes 163840 | tf_op jit(solution)/shard_map/all_to_all | solution.py:274
  56.7 0.7 shard_map.74
  57.4 3.5 %all-to-all-start.2 = ((f32[16,16,128]{2,1,0:T(8,128)}), f32[16,16,128]{2,1,0:T(8,128)S(1)}, u32[]{:S(2)}, u32[]{:S(2)}) async-start(f32[16,16,128]{2,1,0:T(8,128)} %get-tuple-element.26), calls=%async_computation.2 | async-start | bytes 262144 | tf_op jit(solution)/shard_map/all_to_all | solution.py:274
  60.9 3.2 %shard_map.75 = (f32[32,128]{1,0:T(8,128)S(1)}, f32[2,32,512]{2,1,0:T(8,128)S(1)}) custom-call(f32[16,128]{1,0:T(8,128)S(1)} %get-tuple-element.27.gram_ref, f32[16,8,128]{2,1,0:T(8,128)S(1)} %add.19.left_ref.mine_ref, f32[16,8,128]{2,1,0:T(8,128)S(1)} %collective-permute-done.5.left_ref.other_ref), custom_call_target="tpu_custom_call" | custom-call | flops 268435456 | bytes 262144 | tf_op jit(solution)/shard_map/pallas_call | solution.py:28
  64.1 3.6 %all-to-all-done.2 = f32[16,16,128]{2,1,0:T(8,128)S(1)} async-done(((f32[16,16,128]{2,1,0:T(8,128)}), f32[16,16,128]{2,1,0:T(8,128)S(1)}, u32[]{:S(2)}, u32[]{:S(2)}) %all-to-all-start.2) | async-done | bytes 131104 | tf_op jit(solution)/shard_map/all_to_all | solution.py:274
  67.7 4.5 %collective-permute-start.7 = (f32[32,8,128]{2,1,0:T(8,128)S(1)}, f32[32,8,128]{2,1,0:T(8,128)S(1)}, u32[]{:S(2)}, u32[]{:S(2)}) collective-permute-start(f32[32,8,128]{2,1,0:T(8,128)S(1)} %bitcast.18), channel_id=1, source_target_pairs={{0,8},{8,0},{1,9},{9,1},{2,10},{10,2},{3,11},{11,3},{4,12},{12,4},... | collective-permute-start | bytes 393224 | tf_op jit(solution)/shard_map/ppermute | solution.py:270
  72.2 0.0 copy-done
  72.2 0.0 copy-done.1
  72.2 0.5 shard_map.76
  72.7 0.4 collective-permute-done.7.right_ref
  73.2 1.3 %shard_map.77 = (f32[2,32,1024]{2,1,0:T(8,128)}, f32[2,32,512]{2,1,0:T(8,128)}, f32[2,32,512]{2,1,0:T(8,128)}) custom-call(f32[32,8,128]{2,1,0:T(8,128)S(1)} %collective-permute-done.7.right_ref, f32[32,128]{1,0:T(8,128)S(1)} %get-tuple-element.31.inverse_ref, f32[2,32,512]{2,1,0:T(8,128)S(1)} %get-tuple-element.32.frame_ref, f32[2,32,512]{2,1,0:T(8,128)S(1)} %bitcast.15, ...), custom_call_target="tpu_custom_call" | custom-call | flops 1048576 | bytes 262144 | tf_op jit(solution)/shard_map/pallas_call | solution.py:28
  (8 shorter events, 0.1 us)
Async XLA Ops:
  2.8 4.2 %collective-permute-start = (f32[16,8,128]{2,1,0:T(8,128)S(1)}, f32[16,8,128]{2,1,0:T(8,128)S(1)}, u32[]{:S(2)}, u32[]{:S(2)}) collective-permute-start(f32[16,8,128]{2,1,0:T(8,128)S(1)} %get-tuple-element.23), channel_id=1, source_target_pairs={{0,8},{8,0},{1,9},{9,1},{2,10},{10,2},{3,11},{11,3},{4,12},{12,4},... | collective-permute-start | bytes 196616 | tf_op jit(solution)/shard_map/ppermute | solution.py:270
  7.0 3.2 %collective-permute-start.1 = (f32[16,8,128]{2,1,0:T(8,128)S(1)}, f32[16,8,128]{2,1,0:T(8,128)S(1)}, u32[]{:S(2)}, u32[]{:S(2)}) collective-permute-start(f32[16,8,128]{2,1,0:T(8,128)S(1)} %add.15), channel_id=1, source_target_pairs={{0,16},{16,0},{32,48},{48,32},{1,17},{17,1},{33,49},{49,33},{2,18}... | collective-permute-start | bytes 196616 | tf_op jit(solution)/shard_map/ppermute | solution.py:298
  10.2 4.4 %collective-permute-start.2 = (f32[16,8,128]{2,1,0:T(8,128)S(1)}, f32[16,8,128]{2,1,0:T(8,128)S(1)}, u32[]{:S(2)}, u32[]{:S(2)}) collective-permute-start(f32[16,8,128]{2,1,0:T(8,128)S(1)} %add.16), channel_id=1, source_target_pairs={{0,48},{16,32},{32,16},{48,0},{1,49},{17,33},{33,17},{49,1},{2,50}... | collective-permute-start | bytes 196616 | tf_op jit(solution)/shard_map/ppermute | solution.py:298
  14.6 3.2 %collective-permute-start.3 = (f32[16,8,128]{2,1,0:T(8,128)S(1)}, f32[16,8,128]{2,1,0:T(8,128)S(1)}, u32[]{:S(2)}, u32[]{:S(2)}) collective-permute-start(f32[16,8,128]{2,1,0:T(8,128)S(1)} %add.17), channel_id=1, source_target_pairs={{0,64},{64,0},{128,192},{192,128},{1,65},{65,1},{129,193},{193,129... | collective-permute-start | bytes 196616 | tf_op jit(solution)/shard_map/ppermute | solution.py:298
  17.8 4.5 %collective-permute-start.4 = (f32[16,8,128]{2,1,0:T(8,128)S(1)}, f32[16,8,128]{2,1,0:T(8,128)S(1)}, u32[]{:S(2)}, u32[]{:S(2)}) collective-permute-start(f32[16,8,128]{2,1,0:T(8,128)S(1)} %add.18), channel_id=1, source_target_pairs={{0,128},{64,192},{128,0},{192,64},{1,129},{65,193},{129,1},{193,65... | collective-permute-start | bytes 196616 | tf_op jit(solution)/shard_map/ppermute | solution.py:298
  22.3 6.3 %collective-permute-start.5 = (f32[16,8,128]{2,1,0:T(8,128)S(1)}, f32[16,8,128]{2,1,0:T(8,128)S(1)}, u32[]{:S(2)}, u32[]{:S(2)}) collective-permute-start(f32[16,8,128]{2,1,0:T(8,128)S(1)} %add.19.left_ref.mine_ref), channel_id=1, source_target_pairs={{0,8},{8,0},{1,9},{9,1},{2,10},{10,2},{3,11},{11,3},{4,12},{12,4},... | collective-permute-start | bytes 196616 | tf_op jit(solution)/shard_map/ppermute | solution.py:270
  28.0 44.2 %copy-start = (f32[2,512,32]{1,2,0:T(8,128)S(1)}, f32[2,512,32]{1,2,0:T(8,128)}, u32[]{:S(2)}) copy-start(f32[2,512,32]{1,2,0:T(8,128)} %param.6) | copy-start | bytes 393220
  28.0 44.2 %copy-start.1 = (f32[2,512,32]{1,2,0:T(8,128)S(1)}, f32[2,512,32]{1,2,0:T(8,128)}, u32[]{:S(2)}) copy-start(f32[2,512,32]{1,2,0:T(8,128)} %param.7) | copy-start | bytes 393220
  28.9 1.4 %collective-permute-start.6 = (f32[16,16,128]{2,1,0:T(8,128)S(1)}, f32[16,16,128]{2,1,0:T(8,128)S(1)}, u32[]{:S(2)}, u32[]{:S(2)}) collective-permute-start(f32[16,16,128]{2,1,0:T(8,128)S(1)} %shard_map.70), channel_id=1, source_target_pairs={{0,8},{8,0},{1,9},{9,1},{2,10},{10,2},{3,11},{11,3},{4,12},{12,4},... | collective-permute-start | bytes 393224 | tf_op jit(solution)/shard_map/ppermute | solution.py:270
  57.4 10.3 %all-to-all-start.2 = ((f32[16,16,128]{2,1,0:T(8,128)}), f32[16,16,128]{2,1,0:T(8,128)S(1)}, u32[]{:S(2)}, u32[]{:S(2)}) async-start(f32[16,16,128]{2,1,0:T(8,128)} %get-tuple-element.26), calls=%async_computation.2 | async-start | bytes 262144 | tf_op jit(solution)/shard_map/all_to_all | solution.py:274
  67.7 5.5 %collective-permute-start.7 = (f32[32,8,128]{2,1,0:T(8,128)S(1)}, f32[32,8,128]{2,1,0:T(8,128)S(1)}, u32[]{:S(2)}, u32[]{:S(2)}) collective-permute-start(f32[32,8,128]{2,1,0:T(8,128)S(1)} %bitcast.18), channel_id=1, source_target_pairs={{0,8},{8,0},{1,9},{9,1},{2,10},{10,2},{3,11},{11,3},{4,12},{12,4},... | collective-permute-start | bytes 393224 | tf_op jit(solution)/shard_map/ppermute | solution.py:270

commit v4 on v2

--- a/solution.py
+++ b/solution.py
@@ -13,7 +13,6 @@
 SIZES = {"zlo": 4, "y": 4, "core": 2, "zhi": 2, "x": 4}
 REPLICA = ("zlo", "y", "core")
 MODEL = ("zhi", "x")
-LINES = ("zlo", "y")
 PLANE = ("y", "x")
 COLUMN = ("zlo", "zhi")
 REPLICAS, PEERS, STACK = 32, 16, 8
@@ -62,24 +61,41 @@
     return lax.axis_index("core")
 
 
-def left_body(mine, basis_ref, grads_ref, out_ref):
-    layer = core() if mine else 1 - core()
-    left = lax.dot_general(
-        basis_ref[layer].astype(jnp.bfloat16),
-        grads_ref[layer],
+ROWS = 128
+
+
+def left_of(basis, grads):
+    return lax.dot_general(
+        basis.astype(jnp.bfloat16),
+        grads,
         (((1,), (1,)), ((), ())),
         preferred_element_type=jnp.float32,
     )
-    for t in range(4):
-        for j in range(4):
-            out_ref[4 * t + j] = left[8 * t : 8 * t + 8, LANES * j : LANES * j + LANES]
-
-
-def right_body(mine, left_ref, grads_ref, out_ref):
+
+
+def left_body(mine, basis_hbm, grads_hbm, out_ref, grads_ref, basis_ref, sems):
     layer = core() if mine else 1 - core()
+    pieces = [pltpu.make_async_copy(basis_hbm.at[layer], basis_ref, sems.at[4])]
+    for j in range(4):
+        rows = pl.ds(ROWS * j, ROWS)
+        pieces.append(
+            pltpu.make_async_copy(grads_hbm.at[layer, rows], grads_ref.at[rows], sems.at[j])
+        )
+    for piece in pieces:
+        piece.start()
+    pieces[0].wait()
+    basis = basis_ref[...]
+    for j in range(4):
+        pieces[1 + j].wait()
+        left = left_of(basis, grads_ref[ROWS * j : ROWS * (j + 1)])
+        for t in range(4):
+            out_ref[4 * t + j] = left[8 * t : 8 * t + 8]
+
+
+def right_body(left_ref, grads_ref, out_ref):
     right = jnp.dot(
         joined(left_ref, 4, 4).astype(jnp.bfloat16),
-        grads_ref[layer],
+        grads_ref[...],
         preferred_element_type=jnp.float32,
     )
     for t in range(4):
@@ -187,20 +203,34 @@
         )
 
 
-def settle(layer, right_ref, inverse_ref, frame_ref, weights_ref, momentum_ref):
+def finish_body(mine, right_ref, inverse_ref, frame_ref, weights_ref, momentum_ref, *refs):
+    basis_hbm, w_hbm, m_hbm, basis_ref, w_ref, m_ref, sems = refs[-7:]
+    layer = core() if mine else 1 - core()
     place = (lax.axis_index("zlo") * 4 + lax.axis_index("y")) * 2 + core()
     block = place // 4
     shift = (4 - place % 4) * 32
-    square = jnp.zeros((8, LANES), jnp.float32)
-    for i in range(32):
-        tile = right_ref[i]
-        square = square + tile * tile
-    scale = lax.rsqrt(jnp.sum(square) * (1.0 / (RANK * 1024)) + 1e-12)
+    copies = []
+
+    def send(source, target):
+        copies.append(pltpu.make_async_copy(source, target, sems.at[len(copies)]))
+        copies[-1].start()
+
     own = jnp.concatenate([right_ref[8 * t + block] for t in range(4)], axis=0)
     inverse = inverse_ref[...]
     inverse = jnp.where(layer == 0, inverse[:, :RANK], inverse[:, RANK : 2 * RANK])
     half = jnp.dot(inverse, own, precision=EXACT, preferred_element_type=jnp.float32)
     half = pltpu.roll(half, shift, 1)[:, :RANK]
+    squares = [jnp.zeros((8, LANES), jnp.float32)] * 4
+    for i in range(32):
+        tile = right_ref[i]
+        squares[i % 4] = squares[i % 4] + tile * tile
+    square = (squares[0] + squares[1]) + (squares[2] + squares[3])
+    scale = lax.rsqrt(jnp.sum(square) * (1.0 / (RANK * 1024)) + 1e-12)
+    for t in range(4):
+        rows = slice(8 * t, 8 * t + 8)
+        for j in range(8):
+            basis_ref[rows, LANES * j : LANES * j + LANES] = right_ref[8 * t + j] * scale
+        send(basis_ref.at[rows], basis_hbm.at[layer, rows])
     change = lax.dot_general(
         half,
         frame_ref[layer],
@@ -209,37 +239,57 @@
         preferred_element_type=jnp.float32,
     )
     new = 0.9 * momentum_ref[layer] + change
-    return scale, new, weights_ref[layer] - 0.02 * new
-
-
-def scaled(right_ref, scale, basis_ref, layer):
-    for t in range(4):
-        for j in range(8):
-            at = (slice(8 * t, 8 * t + 8), slice(LANES * j, LANES * j + LANES))
-            at = at if layer is None else (layer, *at)
-            basis_ref[at] = right_ref[8 * t + j] * scale
-
-
-def early_body(right_ref, inverse_ref, frame_ref, weights_ref, momentum_ref, basis_ref, w_ref, m_ref):
-    scale, new, weights = settle(core(), right_ref, inverse_ref, frame_ref, weights_ref, momentum_ref)
-    scaled(right_ref, scale, basis_ref, None)
     m_ref[...] = new
-    w_ref[...] = weights
-
-
-def late_body(
-    right_ref, inverse_ref, frame_ref, weights_ref, momentum_ref, b_ref, w_ref, m_ref,
-    basis_ref, new_w_ref, new_m_ref,
-):
-    c = core()
-    basis_ref[c] = b_ref[...]
-    new_w_ref[c] = w_ref[...]
-    new_m_ref[c] = m_ref[...]
-    layer = 1 - c
-    scale, new, weights = settle(layer, right_ref, inverse_ref, frame_ref, weights_ref, momentum_ref)
-    scaled(right_ref, scale, basis_ref, layer)
-    new_m_ref[layer] = new
-    new_w_ref[layer] = weights
+    send(m_ref, m_hbm.at[layer])
+    w_ref[...] = weights_ref[layer] - 0.02 * new
+    send(w_ref, w_hbm.at[layer])
+    for copy in copies:
+        copy.wait()
+
+
+def finish(right, solved, partial, width, rows):
+    local, far = pl.BlockSpec(memory_space=pltpu.VMEM), pl.BlockSpec(memory_space=pltpu.HBM)
+    first = not partial
+    return pl.pallas_call(
+        functools.partial(finish_body, first),
+        out_shape=[f32(2, RANK, width), f32(2, RANK, rows), f32(2, RANK, rows)],
+        in_specs=[local] * 5 + [far] * len(partial),
+        out_specs=[far] * 3,
+        scratch_shapes=[
+            pltpu.VMEM((RANK, width), jnp.float32),
+            pltpu.VMEM((RANK, rows), jnp.float32),
+            pltpu.VMEM((RANK, rows), jnp.float32),
+            pltpu.SemaphoreType.DMA((6,)),
+        ],
+        input_output_aliases={} if first else {5: 0, 6: 1, 7: 2},
+        compiler_params=pltpu.CompilerParams(vmem_limit_bytes=VMEM_LIMIT),
+        cost_estimate=pl.CostEstimate(flops=1 << 20, bytes_accessed=1 << 18, transcendentals=0),
+    )(right, *solved, *partial)
+
+
+def part_left(mine, basis, grads):
+    far, local = pl.BlockSpec(memory_space=pltpu.HBM), pl.BlockSpec(memory_space=pltpu.VMEM)
+    return pl.pallas_call(
+        functools.partial(left_body, mine),
+        out_shape=[f32(PEERS, 8, LANES), jax.ShapeDtypeStruct(grads.shape[1:], grads.dtype)],
+        in_specs=[far] * 2,
+        out_specs=[local] * 2,
+        scratch_shapes=[pltpu.VMEM(basis.shape[1:], jnp.float32), pltpu.SemaphoreType.DMA((5,))],
+        compiler_params=pltpu.CompilerParams(vmem_limit_bytes=VMEM_LIMIT),
+        cost_estimate=pl.CostEstimate(flops=1 << 20, bytes_accessed=1 << 18, transcendentals=0),
+    )(basis, grads)
+
+
+DOUBLING = ((4, 8, 1, 3), (1, 3, 4, 8))
+
+
+def doubled(value, step):
+    flips = []
+    for i in range(REPLICAS):
+        place, c = divmod(i, 2)
+        bit = DOUBLING[c][step]
+        flips.append((i, (place ^ bit) * 2 + c))
+    return value + lax.ppermute(value, REPLICA, flips)
 
 
 def swapped(value):
@@ -257,14 +307,17 @@
     weights, momentum = jnp.swapaxes(layer_weights, 1, 2), jnp.swapaxes(momentum, 1, 2)
     lefts, rights = f32(PEERS, 8, LANES), f32(PEERS, 16, LANES)
 
-    away = swapped(kernel_call(functools.partial(left_body, False), lefts)(basis, grads))
-    mine = kernel_call(functools.partial(left_body, True), lefts)(basis, grads)
-    tile = jnp.sum(all_to_all(mine + away, LINES), axis=0)
-    mine = all_to_all(jnp.broadcast_to(tile[None], lefts.shape), LINES)
+    far = [pltpu.with_memory_space_constraint(a, pltpu.HBM) for a in (basis, grads)]
+    away, other_grads = part_left(False, *far)
+    away = swapped(away)
+    mine, own_grads = part_left(True, *far)
+    mine = mine + away
+    for step in range(4):
+        mine = doubled(mine, step)
     other = swapped(mine)
-    kept = kernel_call(functools.partial(right_body, True), rights)(mine, grads)
+    kept = kernel_call(right_body, rights)(mine, own_grads)
     kept, other = lax.optimization_barrier((kept, other))
-    away = swapped(kernel_call(functools.partial(right_body, False), rights)(other, grads))
+    away = swapped(kernel_call(right_body, rights)(other, other_grads))
     share = kernel_call(gram_body, f32(4, LANES))(mine, other)
 
     sent = kernel_call(pack_body, f32(PEERS * CHUNK, LANES))(kept, away, share)
@@ -279,13 +332,8 @@
     right, inverse, frame = lax.optimization_barrier((right.reshape(32, 8, LANES), inverse, frame))
     late = swapped(right)
     solved = (inverse, frame, weights, momentum)
-    early = kernel_call(
-        early_body, [f32(RANK, width), f32(RANK, rows), f32(RANK, rows)]
-    )(right, *solved)
-    new_basis, new_weights, new_momentum = kernel_call(
-        late_body,
-        [f32(layers, RANK, width), f32(layers, RANK, rows), f32(layers, RANK, rows)],
-    )(late, *solved, *early)
+    early = finish(right, solved, (), width, rows)
+    new_basis, new_weights, new_momentum = finish(late, solved, early, width, rows)
     return tuple(jnp.swapaxes(a, 1, 2) for a in (new_weights, new_basis, new_momentum))
 
 

time: 78.4 us -> 75.8 us (0.967)
  blocking collectives: 47 us -> 26.4 us
  waiting for transfers between devices: 5.76 us -> 17.8 us
  starting transfers between devices: 14.5 us -> 19 us
  Pallas kernels: 7.48 us -> 11.5 us
  local copies, waits for them, and re-layouts: 2.56 us -> 0.01 us
    all_to_all x4 -> x2, blocking collectives: 47 us -> 26.4 us  [all_to_all(): return lax.all_to_all(value, axes, 0, 0, tiled=True)]
    ppermute x0 -> x4, waiting for transfers between devices: none -> 13 us  [doubled(): return value + lax.ppermute(value, REPLICA, flips)]
    pallas_call x0 -> x4, Pallas kernels: none -> 6.7 us  [the longest x2 4.19 us: part_left(): pl.pallas_call(functools.partial(left_body, mine), out_shape=[f32(PEERS,...]
    ppermute x0 -> x4, starting transfers between devices: none -> 2.91 us  [doubled(): return value + lax.ppermute(value, REPLICA, flips)]
    pallas_call x11 -> x7, Pallas kernels: 7.48 us -> 4.82 us  [kernel_call(): pl.pallas_call(body, out_shape=outs, in_specs=[spec] * len(args), out_spe...]
    unnamed x10 -> x4, local copies, waits for them, and re-layouts: 2.55 us -> 0.01 us
    ppermute x4, starting transfers between devices: 11 us -> 12.5 us  [swapped(): return lax.ppermute(value, 'core', [(0, 1), (1, 0)])]
    ppermute x4, waiting for transfers between devices: 2.13 us -> 1.21 us  [swapped(): return lax.ppermute(value, 'core', [(0, 1), (1, 0)])]
  transfers between devices with their start and end apart: 5 -> 9, of which waited for: 5 -> 7; matrix products, arithmetic and copies ran while one was open for 0% -> 0% of each run, Pallas kernels for 6% -> 10%
where the time goes in v4:
time: 75.8 us; the launch traced here: 75.5 us
  blocking collectives  26.4 us (35%)
  starting transfers between devices  19 us (25%)
  waiting for transfers between devices  17.8 us (23%)
  Pallas kernels  11.5 us (15%)
    all_to_all x2, blocking collectives, all_to_all(): return lax.all_to_all(value, axes, 0, 0, tiled=True)  26.4 us
    ppermute x4, waiting for transfers between devices, doubled(): return value + lax.ppermute(value, REPLICA, flips)  13 us
    ppermute x4, starting transfers between devices, swapped(): return lax.ppermute(value, 'core', [(0, 1), (1, 0)])  12.5 us
    pallas_call x7, Pallas kernels, kernel_call(): pl.pallas_call(body, out_shape=outs, in_specs=[spec] * len(args), out_spe...  4.82 us
    pallas_call x2, Pallas kernels, part_left(): pl.pallas_call(functools.partial(left_body, mine), out_shape=[f32(PEERS,...  4.19 us
    all_to_all x1, waiting for transfers between devices, all_to_all(): return lax.all_to_all(value, axes, 0, 0, tiled=True)  3.63 us
    all_to_all x1, starting transfers between devices, all_to_all(): return lax.all_to_all(value, axes, 0, 0, tiled=True)  3.51 us
    ppermute x4, starting transfers between devices, doubled(): return value + lax.ppermute(value, REPLICA, flips)  2.91 us
  transfers between devices with their start and end apart: 9, of which 7 were waited for; matrix products, arithmetic and copies ran while one was open for 0% of the time, Pallas kernels for 10%

profile of v4, /device:TPU:1, one launch (start us, length us, event | category | flops | bytes accessed | tf_op | source)
XLA Modules:
  0.0 75.5 jit_solution(5723317265017325441)
XLA Ops:
  0.6 2.1 %shard_map.68 = (f32[16,8,128]{2,1,0:T(8,128)S(1)}, bf16[512,1024]{1,0:T(8,128)(2,1)S(1)}) custom-call(f32[2,32,1024]{2,1,0:T(8,128)} %bitcast.24, bf16[2,512,1024]{2,1,0:T(8,128)(2,1)} %bitcast.22), custom_call_target="tpu_custom_call" | custom-call | flops 1048576 | bytes 262144 | tf_op jit(solution)/shard_map/pallas_call | solution.py:272
  2.7 3.3 %collective-permute-start = (f32[16,8,128]{2,1,0:T(8,128)S(1)}, f32[16,8,128]{2,1,0:T(8,128)S(1)}, u32[]{:S(2)}, u32[]{:S(2)}) collective-permute-start(f32[16,8,128]{2,1,0:T(8,128)S(1)} %get-tuple-element.23), channel_id=1, source_target_pairs={{0,8},{8,0},{1,9},{9,1},{2,10},{10,2},{3,11},{11,3},{4,12},{12,4},... | collective-permute-start | bytes 196616 | tf_op jit(solution)/shard_map/ppermute | solution.py:296
  6.0 2.1 %shard_map.67 = (f32[16,8,128]{2,1,0:T(8,128)S(1)}, bf16[512,1024]{1,0:T(8,128)(2,1)S(1)}) custom-call(f32[2,32,1024]{2,1,0:T(8,128)} %bitcast.25, bf16[2,512,1024]{2,1,0:T(8,128)(2,1)} %bitcast.23), custom_call_target="tpu_custom_call" | custom-call | flops 1048576 | bytes 262144 | tf_op jit(solution)/shard_map/pallas_call | solution.py:272
  8.1 0.0 collective-permute-done
  8.2 0.1 collective-permute-start.1
  8.3 3.4 %collective-permute-done.1 = f32[16,8,128]{2,1,0:T(8,128)S(1)} collective-permute-done((f32[16,8,128]{2,1,0:T(8,128)S(1)}, f32[16,8,128]{2,1,0:T(8,128)S(1)}, u32[]{:S(2)}, u32[]{:S(2)}) %collective-permute-start.1) | collective-permute-done | bytes 65568 | tf_op jit(solution)/shard_map/ppermute | solution.py:292
  11.7 1.1 %collective-permute-start.2 = (f32[16,8,128]{2,1,0:T(8,128)S(1)}, f32[16,8,128]{2,1,0:T(8,128)S(1)}, u32[]{:S(2)}, u32[]{:S(2)}) collective-permute-start(f32[16,8,128]{2,1,0:T(8,128)S(1)} %add.16), channel_id=1, source_target_pairs={{0,128},{8,56},{16,144},{24,40},{32,160},{40,24},{48,176},{56,8},{... | collective-permute-start | bytes 196616 | tf_op jit(solution)/shard_map/ppermute | solution.py:292
  12.8 3.3 %collective-permute-done.2 = f32[16,8,128]{2,1,0:T(8,128)S(1)} collective-permute-done((f32[16,8,128]{2,1,0:T(8,128)S(1)}, f32[16,8,128]{2,1,0:T(8,128)S(1)}, u32[]{:S(2)}, u32[]{:S(2)}) %collective-permute-start.2) | collective-permute-done | bytes 65568 | tf_op jit(solution)/shard_map/ppermute | solution.py:292
  16.1 0.1 collective-permute-start.3
  16.2 3.1 %collective-permute-done.3 = f32[16,8,128]{2,1,0:T(8,128)S(1)} collective-permute-done((f32[16,8,128]{2,1,0:T(8,128)S(1)}, f32[16,8,128]{2,1,0:T(8,128)S(1)}, u32[]{:S(2)}, u32[]{:S(2)}) %collective-permute-start.3) | collective-permute-done | bytes 65568 | tf_op jit(solution)/shard_map/ppermute | solution.py:292
  19.3 1.6 %collective-permute-start.4 = (f32[16,8,128]{2,1,0:T(8,128)S(1)}, f32[16,8,128]{2,1,0:T(8,128)S(1)}, u32[]{:S(2)}, u32[]{:S(2)}) collective-permute-start(f32[16,8,128]{2,1,0:T(8,128)S(1)} %add.18), channel_id=1, source_target_pairs={{0,48},{8,136},{16,32},{24,152},{32,16},{40,168},{48,0},{56,184},{... | collective-permute-start | bytes 196616 | tf_op jit(solution)/shard_map/ppermute | solution.py:292
  20.9 3.2 %collective-permute-done.4 = f32[16,8,128]{2,1,0:T(8,128)S(1)} collective-permute-done((f32[16,8,128]{2,1,0:T(8,128)S(1)}, f32[16,8,128]{2,1,0:T(8,128)S(1)}, u32[]{:S(2)}, u32[]{:S(2)}) %collective-permute-start.4) | collective-permute-done | bytes 65568 | tf_op jit(solution)/shard_map/ppermute | solution.py:292
  24.1 4.4 %collective-permute-start.5 = (f32[16,8,128]{2,1,0:T(8,128)S(1)}, f32[16,8,128]{2,1,0:T(8,128)S(1)}, u32[]{:S(2)}, u32[]{:S(2)}) collective-permute-start(f32[16,8,128]{2,1,0:T(8,128)S(1)} %add.19.left_ref.mine_ref), channel_id=1, source_target_pairs={{0,8},{8,0},{1,9},{9,1},{2,10},{10,2},{3,11},{11,3},{4,12},{12,4},... | collective-permute-start | bytes 196616 | tf_op jit(solution)/shard_map/ppermute | solution.py:296
  28.5 0.3 shard_map.69.mine_ref
  28.8 0.0 copy-start
  28.8 0.6 collective-permute-done.5.left_ref.other_ref
  29.4 0.3 shard_map.70
  29.7 0.4 collective-permute-start.6
  30.1 0.4 shard_map.71.share_ref
  30.5 0.6 collective-permute-done.6.other_ref
  31.1 11.3 %all_to_all.15 = f32[80,4,128]{2,1,0:T(4,128)S(1)} all-to-all(f32[80,4,128]{2,1,0:T(4,128)S(1)} %bitcast.12), channel_id=1, replica_groups=mesh['zlo'=4,'y'=4,'core'=2,'zhi'=2,'x'=4] {'y','x'}, dimensions={0} | all-to-all | bytes 327680 | tf_op jit(solution)/shard_map/all_to_all | solution.py:300
  42.5 15.1 %all_to_all.16 = f32[40,4,128]{2,1,0:T(4,128)S(1)} all-to-all(f32[40,4,128]{2,1,0:T(4,128)S(1)} %bitcast.21), channel_id=1, replica_groups=mesh['zlo'=4,'y'=4,'core'=2,'zhi'=2,'x'=4] {'zlo','zhi'}, dimensions={0} | all-to-all | bytes 163840 | tf_op jit(solution)/shard_map/all_to_all | solution.py:300
  57.5 0.7 shard_map.74
  58.2 3.5 %all-to-all-start.2 = ((f32[16,16,128]{2,1,0:T(8,128)}), f32[16,16,128]{2,1,0:T(8,128)S(1)}, u32[]{:S(2)}, u32[]{:S(2)}) async-start(f32[16,16,128]{2,1,0:T(8,128)} %get-tuple-element.28), calls=%async_computation.2 | async-start | bytes 262144 | tf_op jit(solution)/shard_map/all_to_all | solution.py:300
  61.7 3.2 %shard_map.75 = (f32[32,128]{1,0:T(8,128)S(1)}, f32[2,32,512]{2,1,0:T(8,128)S(1)}) custom-call(f32[16,128]{1,0:T(8,128)S(1)} %get-tuple-element.29.gram_ref, f32[16,8,128]{2,1,0:T(8,128)S(1)} %add.19.left_ref.mine_ref, f32[16,8,128]{2,1,0:T(8,128)S(1)} %collective-permute-done.5.left_ref.other_ref), custom_call_target="tpu_custom_call" | custom-call | flops 268435456 | bytes 262144 | tf_op jit(solution)/shard_map/pallas_call | solution.py:28
  64.9 3.6 %all-to-all-done.2 = f32[16,16,128]{2,1,0:T(8,128)S(1)} async-done(((f32[16,16,128]{2,1,0:T(8,128)}), f32[16,16,128]{2,1,0:T(8,128)S(1)}, u32[]{:S(2)}, u32[]{:S(2)}) %all-to-all-start.2) | async-done | bytes 131104 | tf_op jit(solution)/shard_map/all_to_all | solution.py:300
  68.5 4.5 %collective-permute-start.7 = (f32[32,8,128]{2,1,0:T(8,128)S(1)}, f32[32,8,128]{2,1,0:T(8,128)S(1)}, u32[]{:S(2)}, u32[]{:S(2)}) collective-permute-start(f32[32,8,128]{2,1,0:T(8,128)S(1)} %bitcast.14), channel_id=1, source_target_pairs={{0,8},{8,0},{1,9},{9,1},{2,10},{10,2},{3,11},{11,3},{4,12},{12,4},... | collective-permute-start | bytes 393224 | tf_op jit(solution)/shard_map/ppermute | solution.py:296
  73.0 0.0 copy-done
  73.0 0.0 copy-done.1
  73.0 1.3 %shard_map.76 = (f32[2,32,1024]{2,1,0:T(8,128)}, f32[2,32,512]{2,1,0:T(8,128)}, f32[2,32,512]{2,1,0:T(8,128)}) custom-call(f32[32,8,128]{2,1,0:T(8,128)S(1)} %bitcast.15, f32[32,128]{1,0:T(8,128)S(1)} %get-tuple-element.33.inverse_ref, f32[2,32,512]{2,1,0:T(8,128)S(1)} %get-tuple-element.34.frame_ref, f32[2,32,512]{2,1,0:T(8,128)S(1)} %bitcast.16, ...), custom_call_target="tpu_custom_call" | custom-call | flops 1048576 | bytes 262144 | tf_op jit(solution)/shard_map/pallas_call | solution.py:253
  74.3 0.0 collective-permute-done.7.right_ref
  74.3 1.3 %shard_map.77 = (f32[2,32,1024]{2,1,0:T(8,128)}, f32[2,32,512]{2,1,0:T(8,128)}, f32[2,32,512]{2,1,0:T(8,128)}) custom-call(f32[32,8,128]{2,1,0:T(8,128)S(1)} %collective-permute-done.7.right_ref, f32[32,128]{1,0:T(8,128)S(1)} %get-tuple-element.33.inverse_ref, ...), custom_call_target="tpu_custom_call", output_to_operand_aliasing={{0}: (5, {}), {1}: (6, {}), {2}: (7, {})} | custom-call | flops 1048576 | bytes 262144 | tf_op jit(solution)/shard_map/pallas_call | solution.py:253
  (8 shorter events, 0.1 us)
Async XLA Ops:
  2.7 5.4 %collective-permute-start = (f32[16,8,128]{2,1,0:T(8,128)S(1)}, f32[16,8,128]{2,1,0:T(8,128)S(1)}, u32[]{:S(2)}, u32[]{:S(2)}) collective-permute-start(f32[16,8,128]{2,1,0:T(8,128)S(1)} %get-tuple-element.23), channel_id=1, source_target_pairs={{0,8},{8,0},{1,9},{9,1},{2,10},{10,2},{3,11},{11,3},{4,12},{12,4},... | collective-permute-start | bytes 196616 | tf_op jit(solution)/shard_map/ppermute | solution.py:296
  8.2 3.5 %collective-permute-start.1 = (f32[16,8,128]{2,1,0:T(8,128)S(1)}, f32[16,8,128]{2,1,0:T(8,128)S(1)}, u32[]{:S(2)}, u32[]{:S(2)}) collective-permute-start(f32[16,8,128]{2,1,0:T(8,128)S(1)} %add.15), channel_id=1, source_target_pairs={{0,64},{8,24},{16,80},{24,8},{32,96},{40,56},{48,112},{56,40},{64,... | collective-permute-start | bytes 196616 | tf_op jit(solution)/shard_map/ppermute | solution.py:292
  11.7 4.4 %collective-permute-start.2 = (f32[16,8,128]{2,1,0:T(8,128)S(1)}, f32[16,8,128]{2,1,0:T(8,128)S(1)}, u32[]{:S(2)}, u32[]{:S(2)}) collective-permute-start(f32[16,8,128]{2,1,0:T(8,128)S(1)} %add.16), channel_id=1, source_target_pairs={{0,128},{8,56},{16,144},{24,40},{32,160},{40,24},{48,176},{56,8},{... | collective-permute-start | bytes 196616 | tf_op jit(solution)/shard_map/ppermute | solution.py:292
  16.1 3.2 %collective-permute-start.3 = (f32[16,8,128]{2,1,0:T(8,128)S(1)}, f32[16,8,128]{2,1,0:T(8,128)S(1)}, u32[]{:S(2)}, u32[]{:S(2)}) collective-permute-start(f32[16,8,128]{2,1,0:T(8,128)S(1)} %add.17), channel_id=1, source_target_pairs={{0,16},{8,72},{16,0},{24,88},{32,48},{40,104},{48,32},{56,120},{64... | collective-permute-start | bytes 196616 | tf_op jit(solution)/shard_map/ppermute | solution.py:292
  19.3 4.8 %collective-permute-start.4 = (f32[16,8,128]{2,1,0:T(8,128)S(1)}, f32[16,8,128]{2,1,0:T(8,128)S(1)}, u32[]{:S(2)}, u32[]{:S(2)}) collective-permute-start(f32[16,8,128]{2,1,0:T(8,128)S(1)} %add.18), channel_id=1, source_target_pairs={{0,48},{8,136},{16,32},{24,152},{32,16},{40,168},{48,0},{56,184},{... | collective-permute-start | bytes 196616 | tf_op jit(solution)/shard_map/ppermute | solution.py:292
  24.1 5.3 %collective-permute-start.5 = (f32[16,8,128]{2,1,0:T(8,128)S(1)}, f32[16,8,128]{2,1,0:T(8,128)S(1)}, u32[]{:S(2)}, u32[]{:S(2)}) collective-permute-start(f32[16,8,128]{2,1,0:T(8,128)S(1)} %add.19.left_ref.mine_ref), channel_id=1, source_target_pairs={{0,8},{8,0},{1,9},{9,1},{2,10},{10,2},{3,11},{11,3},{4,12},{12,4},... | collective-permute-start | bytes 196616 | tf_op jit(solution)/shard_map/ppermute | solution.py:296
  28.8 44.2 %copy-start = (f32[2,512,32]{1,2,0:T(8,128)S(1)}, f32[2,512,32]{1,2,0:T(8,128)}, u32[]{:S(2)}) copy-start(f32[2,512,32]{1,2,0:T(8,128)} %param.6) | copy-start | bytes 393220
  28.8 44.2 %copy-start.1 = (f32[2,512,32]{1,2,0:T(8,128)S(1)}, f32[2,512,32]{1,2,0:T(8,128)}, u32[]{:S(2)}) copy-start(f32[2,512,32]{1,2,0:T(8,128)} %param.7) | copy-start | bytes 393220
  29.7 1.4 %collective-permute-start.6 = (f32[16,16,128]{2,1,0:T(8,128)S(1)}, f32[16,16,128]{2,1,0:T(8,128)S(1)}, u32[]{:S(2)}, u32[]{:S(2)}) collective-permute-start(f32[16,16,128]{2,1,0:T(8,128)S(1)} %shard_map.70), channel_id=1, source_target_pairs={{0,8},{8,0},{1,9},{9,1},{2,10},{10,2},{3,11},{11,3},{4,12},{12,4},... | collective-permute-start | bytes 393224 | tf_op jit(solution)/shard_map/ppermute | solution.py:296
  58.2 10.3 %all-to-all-start.2 = ((f32[16,16,128]{2,1,0:T(8,128)}), f32[16,16,128]{2,1,0:T(8,128)S(1)}, u32[]{:S(2)}, u32[]{:S(2)}) async-start(f32[16,16,128]{2,1,0:T(8,128)} %get-tuple-element.28), calls=%async_computation.2 | async-start | bytes 262144 | tf_op jit(solution)/shard_map/all_to_all | solution.py:300
  68.5 5.7 %collective-permute-start.7 = (f32[32,8,128]{2,1,0:T(8,128)S(1)}, f32[32,8,128]{2,1,0:T(8,128)S(1)}, u32[]{:S(2)}, u32[]{:S(2)}) collective-permute-start(f32[32,8,128]{2,1,0:T(8,128)S(1)} %bitcast.14), channel_id=1, source_target_pairs={{0,8},{8,0},{1,9},{9,1},{2,10},{10,2},{3,11},{11,3},{4,12},{12,4},... | collective-permute-start | bytes 393224 | tf_op jit(solution)/shard_map/ppermute | solution.py:296

commit v5 on v3

--- a/solution.py
+++ b/solution.py
@@ -17,6 +17,7 @@
 COLUMN = ("zlo", "zhi")
 REPLICAS, PEERS, STACK = 32, 16, 8
 CHUNK = 20
+BLOCK = 16
 EXACT = lax.Precision.HIGHEST
 VMEM_LIMIT = 24 * 1024 * 1024
 
@@ -178,25 +179,43 @@
 
 def factor_body(gram_ref, mine_ref, other_ref, inverse_ref, frame_ref):
     packed = gram_ref[...]
-    shape = (RANK, LANES)
+    turned = pltpu.roll(packed, 64, 1)
+    grams = [packed[0:8], packed[8:16], turned[0:8], turned[8:16]]
+    shape = (8, LANES)
     lane, row = lane_of(shape), row_of(shape)
-    gram = jnp.concatenate([packed, pltpu.roll(packed, 64, 1)], axis=0)
     first = (lane // RANK) % 2 == 0
-    unit = (lane % RANK) == row
-    diagonal = jnp.where(unit & (lane < 64), gram, 0.0)
+    front = lane < 64
+    units = [(lane % RANK) == row + 8 * r for r in range(4)]
+    diagonal = jnp.zeros(shape, jnp.float32)
+    for r in range(4):
+        diagonal = diagonal + jnp.where(units[r] & front, grams[r], 0.0)
     mean0 = jnp.sum(jnp.where(first, diagonal, 0.0)) * (1.0 / RANK)
     mean1 = jnp.sum(jnp.where(first, 0.0, diagonal)) * (1.0 / RANK)
-    ridge = 0.001 * jnp.where(first, mean0, mean1)
-    work = jnp.where(lane < 64, gram, 0.0) + jnp.where(unit, jnp.where(lane < 64, ridge, 1.0), 0.0)
-    pivots = jnp.ones(shape, jnp.float32)
-    for k in range(RANK):
-        column = jnp.where(first, work[:, k : k + 1], work[:, RANK + k : RANK + k + 1])
-        pivot = column[k : k + 1]
-        pivots = jnp.where(row == k, column, pivots)
-        if k + 1 < RANK:
-            step = work[k : k + 1] / pivot
-            work = work - jnp.where(row > k, column * step, 0.0)
-    inverse = pltpu.roll(work / jnp.sqrt(pivots), 64, 1)
+    ridge = jnp.where(front, 0.001 * jnp.where(first, mean0, mean1), 1.0)
+    work = [jnp.where(front, grams[r], 0.0) + jnp.where(units[r], ridge, 0.0) for r in range(4)]
+    for b in range(0, RANK, BLOCK):
+        columns = [
+            {
+                r: jnp.where(first, work[r][:, k : k + 1], work[r][:, RANK + k : RANK + k + 1])
+                for r in range(b // 8, 4)
+            }
+            for k in range(b, b + BLOCK)
+        ]
+        for i in range(BLOCK):
+            at, s = divmod(b + i, 8)
+            pivot = columns[i][at][s : s + 1]
+            inverse = 1.0 / pivot
+            chosen = work[at][s : s + 1]
+            ahead = {j: columns[j][at][s : s + 1] for j in range(i + 1, BLOCK)}
+            for r in range(at, 4):
+                factor = columns[i][r] * inverse
+                if r == at:
+                    factor = jnp.where(row > s, factor, 0.0)
+                work[r] = work[r] - factor * chosen
+                for j in ahead:
+                    columns[j][r] = columns[j][r] - factor * ahead[j]
+            work[at] = jnp.where(row == s, work[at] * lax.rsqrt(pivot), work[at])
+    inverse = pltpu.roll(jnp.concatenate(work, axis=0), 64, 1)
     inverse_ref[...] = inverse
     left = by_layer(mine_ref, other_ref)
     for l in range(2):
@@ -308,11 +327,11 @@
     came = all_to_all(sent.reshape(STACK * CHUNK // 4, 4, LANES), COLUMN)
     sent, gram = kernel_call(column_body, [rights, f32(16, LANES)])(came.reshape(-1, LANES))
     right = all_to_all(sent, PLANE)
-    inverse, frame = kernel_call(
-        factor_body, [f32(RANK, LANES), f32(layers, RANK, rows)], flops=1 << 28
-    )(gram, mine, other)
-    right, inverse, frame = lax.optimization_barrier((right.reshape(32, 8, LANES), inverse, frame))
+    right, gram = lax.optimization_barrier((right.reshape(32, 8, LANES), gram))
     late = swapped(right)
+    inverse, frame = kernel_call(factor_body, [f32(RANK, LANES), f32(layers, RANK, rows)])(
+        gram, mine, other
+    )
     solved = (inverse, frame, weights, momentum)
     early = kernel_call(
         early_body, [f32(RANK, width), f32(RANK, rows), f32(RANK, rows)]

time: 74.7 us -> 74.2 us (level)
  blocking collectives: 26.4 us -> 36.2 us
  waiting for transfers between devices: 18.1 us -> 14.1 us
  starting transfers between devices: 19.9 us -> 16.5 us
  Pallas kernels: 9.22 us -> 6.44 us
    all_to_all x2 -> x3, blocking collectives: 26.4 us -> 36.2 us  [all_to_all(): return lax.all_to_all(value, axes, 0, 0, tiled=True)]
    all_to_all x1 -> x0, waiting for transfers between devices: 3.63 us -> none  [all_to_all(): return lax.all_to_all(value, axes, 0, 0, tiled=True)]
    all_to_all x1 -> x0, starting transfers between devices: 3.51 us -> none  [all_to_all(): return lax.all_to_all(value, axes, 0, 0, tiled=True)]
    pallas_call x10, Pallas kernels: 7.07 us -> 4.29 us  [kernel_call(): pl.pallas_call(body, out_shape=outs, in_specs=[spec] * len(args), out_spe...]
  transfers between devices with their start and end apart: 9 -> 8, of which waited for: 9 -> 7; matrix products, arithmetic and copies ran while one was open for 0% -> 0% of each run, Pallas kernels for 6% -> 4%
where the time goes in v5:
time: 74.2 us; the launch traced here: 74 us
  blocking collectives  36.2 us (49%)
  starting transfers between devices  16.5 us (22%)
  waiting for transfers between devices  14.1 us (19%)
  Pallas kernels  6.44 us (9%)
    all_to_all x3, blocking collectives, all_to_all(): return lax.all_to_all(value, axes, 0, 0, tiled=True)  36.2 us
    ppermute x4, starting transfers between devices, swapped(): return lax.ppermute(value, 'core', [(0, 1), (1, 0)])  13.6 us
    ppermute x4, waiting for transfers between devices, shards(): lax.ppermute(mine, axis, [(i, i ^ bit) for i in range(SIZES[axis])])  12.4 us
    pallas_call x10, Pallas kernels, kernel_call(): pl.pallas_call(body, out_shape=outs, in_specs=[spec] * len(args), out_spe...  4.29 us
    ppermute x4, starting transfers between devices, shards(): lax.ppermute(mine, axis, [(i, i ^ bit) for i in range(SIZES[axis])])  2.91 us
    pallas_call x1, Pallas kernels, shards(): pl.pallas_call(first_body, out_shape=[lefts, jax.ShapeDtypeStruct(grads.s...  2.14 us
    ppermute x4, waiting for transfers between devices, swapped(): return lax.ppermute(value, 'core', [(0, 1), (1, 0)])  1.71 us
  transfers between devices with their start and end apart: 8, of which 7 were waited for; matrix products, arithmetic and copies ran while one was open for 0% of the time, Pallas kernels for 4%

profile of v5, /device:TPU:1, one launch (start us, length us, event | category | flops | bytes accessed | tf_op | source)
XLA Modules:
  0.0 74.0 jit_solution(128137163281160092)
XLA Ops:
  0.6 2.1 %shard_map.67 = (f32[16,8,128]{2,1,0:T(8,128)S(1)}, bf16[2,512,1024]{2,1,0:T(8,128)(2,1)S(1)}, f32[2,32,1024]{2,1,0:T(8,128)S(1)}) custom-call(f32[2,32,1024]{2,1,0:T(8,128)} %bitcast.23, bf16[2,512,1024]{2,1,0:T(8,128)(2,1)} %bitcast.22), custom_call_target="tpu_custom_call" | custom-call | flops 1048576 | bytes 262144 | tf_op jit(solution)/shard_map/pallas_call | solution.py:305
  2.8 3.3 %collective-permute-start = (f32[16,8,128]{2,1,0:T(8,128)S(1)}, f32[16,8,128]{2,1,0:T(8,128)S(1)}, u32[]{:S(2)}, u32[]{:S(2)}) collective-permute-start(f32[16,8,128]{2,1,0:T(8,128)S(1)} %get-tuple-element.22), channel_id=1, source_target_pairs={{0,8},{8,0},{1,9},{9,1},{2,10},{10,2},{3,11},{11,3},{4,12},{12,4},... | collective-permute-start | bytes 196616 | tf_op jit(solution)/shard_map/ppermute | solution.py:289
  6.1 0.4 shard_map.68
  6.5 0.5 collective-permute-done
  7.0 0.1 collective-permute-start.1
  7.1 3.1 %collective-permute-done.1 = f32[16,8,128]{2,1,0:T(8,128)S(1)} collective-permute-done((f32[16,8,128]{2,1,0:T(8,128)S(1)}, f32[16,8,128]{2,1,0:T(8,128)S(1)}, u32[]{:S(2)}, u32[]{:S(2)}) %collective-permute-start.1) | collective-permute-done | bytes 65568 | tf_op jit(solution)/shard_map/ppermute | solution.py:317
  10.2 1.1 %collective-permute-start.2 = (f32[16,8,128]{2,1,0:T(8,128)S(1)}, f32[16,8,128]{2,1,0:T(8,128)S(1)}, u32[]{:S(2)}, u32[]{:S(2)}) collective-permute-start(f32[16,8,128]{2,1,0:T(8,128)S(1)} %add.16), channel_id=1, source_target_pairs={{0,48},{16,32},{32,16},{48,0},{1,49},{17,33},{33,17},{49,1},{2,50}... | collective-permute-start | bytes 196616 | tf_op jit(solution)/shard_map/ppermute | solution.py:317
  11.3 3.3 %collective-permute-done.2 = f32[16,8,128]{2,1,0:T(8,128)S(1)} collective-permute-done((f32[16,8,128]{2,1,0:T(8,128)S(1)}, f32[16,8,128]{2,1,0:T(8,128)S(1)}, u32[]{:S(2)}, u32[]{:S(2)}) %collective-permute-start.2) | collective-permute-done | bytes 65568 | tf_op jit(solution)/shard_map/ppermute | solution.py:317
  14.6 0.1 collective-permute-start.3
  14.7 3.1 %collective-permute-done.3 = f32[16,8,128]{2,1,0:T(8,128)S(1)} collective-permute-done((f32[16,8,128]{2,1,0:T(8,128)S(1)}, f32[16,8,128]{2,1,0:T(8,128)S(1)}, u32[]{:S(2)}, u32[]{:S(2)}) %collective-permute-start.3) | collective-permute-done | bytes 65568 | tf_op jit(solution)/shard_map/ppermute | solution.py:317
  17.8 1.6 %collective-permute-start.4 = (f32[16,8,128]{2,1,0:T(8,128)S(1)}, f32[16,8,128]{2,1,0:T(8,128)S(1)}, u32[]{:S(2)}, u32[]{:S(2)}) collective-permute-start(f32[16,8,128]{2,1,0:T(8,128)S(1)} %add.18), channel_id=1, source_target_pairs={{0,128},{64,192},{128,0},{192,64},{1,129},{65,193},{129,1},{193,65... | collective-permute-start | bytes 196616 | tf_op jit(solution)/shard_map/ppermute | solution.py:317
  19.5 2.9 %collective-permute-done.4 = f32[16,8,128]{2,1,0:T(8,128)S(1)} collective-permute-done((f32[16,8,128]{2,1,0:T(8,128)S(1)}, f32[16,8,128]{2,1,0:T(8,128)S(1)}, u32[]{:S(2)}, u32[]{:S(2)}) %collective-permute-start.4) | collective-permute-done | bytes 65568 | tf_op jit(solution)/shard_map/ppermute | solution.py:317
  22.3 5.4 %collective-permute-start.5 = (f32[16,8,128]{2,1,0:T(8,128)S(1)}, f32[16,8,128]{2,1,0:T(8,128)S(1)}, u32[]{:S(2)}, u32[]{:S(2)}) collective-permute-start(f32[16,8,128]{2,1,0:T(8,128)S(1)} %add.19.left_ref.mine_ref), channel_id=1, source_target_pairs={{0,8},{8,0},{1,9},{9,1},{2,10},{10,2},{3,11},{11,3},{4,12},{12,4},... | collective-permute-start | bytes 196616 | tf_op jit(solution)/shard_map/ppermute | solution.py:289
  27.7 0.3 shard_map.69.mine_ref
  28.0 0.0 copy-start
  28.0 0.0 copy-start.1
  28.0 0.6 collective-permute-done.5.left_ref.other_ref
  28.6 0.3 shard_map.70
  28.9 0.4 collective-permute-start.6
  29.2 0.4 shard_map.71.share_ref
  29.7 0.6 collective-permute-done.6.other_ref
  30.3 11.8 %all_to_all.15 = f32[80,4,128]{2,1,0:T(4,128)S(1)} all-to-all(f32[80,4,128]{2,1,0:T(4,128)S(1)} %bitcast.12), channel_id=1, replica_groups=mesh['zlo'=4,'y'=4,'core'=2,'zhi'=2,'x'=4] {'y','x'}, dimensions={0} | all-to-all | bytes 327680 | tf_op jit(solution)/shard_map/all_to_all | solution.py:293
  42.1 14.7 %all_to_all.16 = f32[40,4,128]{2,1,0:T(4,128)S(1)} all-to-all(f32[40,4,128]{2,1,0:T(4,128)S(1)} %bitcast.21), channel_id=1, replica_groups=mesh['zlo'=4,'y'=4,'core'=2,'zhi'=2,'x'=4] {'zlo','zhi'}, dimensions={0} | all-to-all | bytes 163840 | tf_op jit(solution)/shard_map/all_to_all | solution.py:293
  56.7 9.8 %all_to_all.17 = f32[16,16,128]{2,1,0:T(8,128)S(1)} all-to-all(f32[16,16,128]{2,1,0:T(8,128)S(1)} %get-tuple-element.25), channel_id=1, replica_groups=mesh['zlo'=4,'y'=4,'core'=2,'zhi'=2,'x'=4] {'y','x'}, dimensions={0} | all-to-all | bytes 262144 | tf_op jit(solution)/shard_map/all_to_all | solution.py:293
  66.5 4.5 %collective-permute-start.7 = (f32[32,8,128]{2,1,0:T(8,128)S(1)}, f32[32,8,128]{2,1,0:T(8,128)S(1)}, u32[]{:S(2)}, u32[]{:S(2)}) collective-permute-start(f32[32,8,128]{2,1,0:T(8,128)S(1)} %bitcast.18), channel_id=1, source_target_pairs={{0,8},{8,0},{1,9},{9,1},{2,10},{10,2},{3,11},{11,3},{4,12},{12,4},... | collective-permute-start | bytes 393224 | tf_op jit(solution)/shard_map/ppermute | solution.py:289
  71.1 1.0 %shard_map.75 = (f32[32,128]{1,0:T(8,128)S(1)}, f32[2,32,512]{2,1,0:T(8,128)S(1)}) custom-call(f32[16,128]{1,0:T(8,128)S(1)} %get-tuple-element.28.gram_ref, f32[16,8,128]{2,1,0:T(8,128)S(1)} %add.19.left_ref.mine_ref, f32[16,8,128]{2,1,0:T(8,128)S(1)} %collective-permute-done.5.left_ref.other_ref), custom_call_target="tpu_custom_call" | custom-call | flops 1048576 | bytes 262144 | tf_op jit(solution)/shard_map/pallas_call | solution.py:29
  72.1 0.0 copy-done
  72.1 0.0 copy-done.1
  72.1 0.5 shard_map.76
  72.7 0.0 collective-permute-done.7.right_ref
  72.7 1.3 %shard_map.77 = (f32[2,32,1024]{2,1,0:T(8,128)}, f32[2,32,512]{2,1,0:T(8,128)}, f32[2,32,512]{2,1,0:T(8,128)}) custom-call(f32[32,8,128]{2,1,0:T(8,128)S(1)} %collective-permute-done.7.right_ref, f32[32,128]{1,0:T(8,128)S(1)} %get-tuple-element.29.inverse_ref, f32[2,32,512]{2,1,0:T(8,128)S(1)} %get-tuple-element.30.frame_ref, f32[2,32,512]{2,1,0:T(8,128)S(1)} %bitcast.15, ...), custom_call_target="tpu_custom_call" | custom-call | flops 1048576 | bytes 262144 | tf_op jit(solution)/shard_map/pallas_call | solution.py:29
  (8 shorter events, 0.1 us)
Async XLA Ops:
  2.8 4.2 %collective-permute-start = (f32[16,8,128]{2,1,0:T(8,128)S(1)}, f32[16,8,128]{2,1,0:T(8,128)S(1)}, u32[]{:S(2)}, u32[]{:S(2)}) collective-permute-start(f32[16,8,128]{2,1,0:T(8,128)S(1)} %get-tuple-element.22), channel_id=1, source_target_pairs={{0,8},{8,0},{1,9},{9,1},{2,10},{10,2},{3,11},{11,3},{4,12},{12,4},... | collective-permute-start | bytes 196616 | tf_op jit(solution)/shard_map/ppermute | solution.py:289
  7.0 3.2 %collective-permute-start.1 = (f32[16,8,128]{2,1,0:T(8,128)S(1)}, f32[16,8,128]{2,1,0:T(8,128)S(1)}, u32[]{:S(2)}, u32[]{:S(2)}) collective-permute-start(f32[16,8,128]{2,1,0:T(8,128)S(1)} %add.15), channel_id=1, source_target_pairs={{0,16},{16,0},{32,48},{48,32},{1,17},{17,1},{33,49},{49,33},{2,18}... | collective-permute-start | bytes 196616 | tf_op jit(solution)/shard_map/ppermute | solution.py:317
  10.2 4.4 %collective-permute-start.2 = (f32[16,8,128]{2,1,0:T(8,128)S(1)}, f32[16,8,128]{2,1,0:T(8,128)S(1)}, u32[]{:S(2)}, u32[]{:S(2)}) collective-permute-start(f32[16,8,128]{2,1,0:T(8,128)S(1)} %add.16), channel_id=1, source_target_pairs={{0,48},{16,32},{32,16},{48,0},{1,49},{17,33},{33,17},{49,1},{2,50}... | collective-permute-start | bytes 196616 | tf_op jit(solution)/shard_map/ppermute | solution.py:317
  14.6 3.2 %collective-permute-start.3 = (f32[16,8,128]{2,1,0:T(8,128)S(1)}, f32[16,8,128]{2,1,0:T(8,128)S(1)}, u32[]{:S(2)}, u32[]{:S(2)}) collective-permute-start(f32[16,8,128]{2,1,0:T(8,128)S(1)} %add.17), channel_id=1, source_target_pairs={{0,64},{64,0},{128,192},{192,128},{1,65},{65,1},{129,193},{193,129... | collective-permute-start | bytes 196616 | tf_op jit(solution)/shard_map/ppermute | solution.py:317
  17.8 4.5 %collective-permute-start.4 = (f32[16,8,128]{2,1,0:T(8,128)S(1)}, f32[16,8,128]{2,1,0:T(8,128)S(1)}, u32[]{:S(2)}, u32[]{:S(2)}) collective-permute-start(f32[16,8,128]{2,1,0:T(8,128)S(1)} %add.18), channel_id=1, source_target_pairs={{0,128},{64,192},{128,0},{192,64},{1,129},{65,193},{129,1},{193,65... | collective-permute-start | bytes 196616 | tf_op jit(solution)/shard_map/ppermute | solution.py:317
  22.3 6.3 %collective-permute-start.5 = (f32[16,8,128]{2,1,0:T(8,128)S(1)}, f32[16,8,128]{2,1,0:T(8,128)S(1)}, u32[]{:S(2)}, u32[]{:S(2)}) collective-permute-start(f32[16,8,128]{2,1,0:T(8,128)S(1)} %add.19.left_ref.mine_ref), channel_id=1, source_target_pairs={{0,8},{8,0},{1,9},{9,1},{2,10},{10,2},{3,11},{11,3},{4,12},{12,4},... | collective-permute-start | bytes 196616 | tf_op jit(solution)/shard_map/ppermute | solution.py:289
  28.0 44.1 %copy-start = (f32[2,512,32]{1,2,0:T(8,128)S(1)}, f32[2,512,32]{1,2,0:T(8,128)}, u32[]{:S(2)}) copy-start(f32[2,512,32]{1,2,0:T(8,128)} %param.6) | copy-start | bytes 393220
  28.0 44.1 %copy-start.1 = (f32[2,512,32]{1,2,0:T(8,128)S(1)}, f32[2,512,32]{1,2,0:T(8,128)}, u32[]{:S(2)}) copy-start(f32[2,512,32]{1,2,0:T(8,128)} %param.7) | copy-start | bytes 393220
  28.9 1.4 %collective-permute-start.6 = (f32[16,16,128]{2,1,0:T(8,128)S(1)}, f32[16,16,128]{2,1,0:T(8,128)S(1)}, u32[]{:S(2)}, u32[]{:S(2)}) collective-permute-start(f32[16,16,128]{2,1,0:T(8,128)S(1)} %shard_map.70), channel_id=1, source_target_pairs={{0,8},{8,0},{1,9},{9,1},{2,10},{10,2},{3,11},{11,3},{4,12},{12,4},... | collective-permute-start | bytes 393224 | tf_op jit(solution)/shard_map/ppermute | solution.py:289
  66.5 6.2 %collective-permute-start.7 = (f32[32,8,128]{2,1,0:T(8,128)S(1)}, f32[32,8,128]{2,1,0:T(8,128)S(1)}, u32[]{:S(2)}, u32[]{:S(2)}) collective-permute-start(f32[32,8,128]{2,1,0:T(8,128)S(1)} %bitcast.18), channel_id=1, source_target_pairs={{0,8},{8,0},{1,9},{9,1},{2,10},{10,2},{3,11},{11,3},{4,12},{12,4},... | collective-permute-start | bytes 393224 | tf_op jit(solution)/shard_map/ppermute | solution.py:289

commit v6 on v5

--- a/solution.py
+++ b/solution.py
@@ -62,7 +62,11 @@
     return lax.axis_index("core")
 
 
-ROWS = 128
+def held():
+    return (core() + lax.axis_index("y") + lax.axis_index("zlo")) % 2
+
+
+WIDE = 256
 
 
 def left_of(basis, grads):
@@ -74,36 +78,42 @@
     )
 
 
+def put_left(left, out_ref):
+    for t in range(4):
+        for j in range(4):
+            out_ref[4 * t + j] = left[8 * t : 8 * t + 8, LANES * j : LANES * j + LANES]
+
+
 def first_body(basis_hbm, grads_hbm, out_ref, grads_ref, basis_ref, sems):
-    c = core()
+    h = held()
     whole = pltpu.make_async_copy(basis_hbm, basis_ref, sems.at[8])
     whole.start()
     copies = []
     for k in range(8):
-        at = (1 - c if k < 4 else c, pl.ds(ROWS * (k % 4), ROWS))
+        at = (1 - h if k < 4 else h, slice(None), pl.ds(WIDE * (k % 4), WIDE))
         copies.append(pltpu.make_async_copy(grads_hbm.at[at], grads_ref.at[at], sems.at[k]))
         copies[-1].start()
     whole.wait()
+    left = jnp.zeros((RANK, grads_ref.shape[1]), jnp.float32)
     for j in range(4):
         copies[j].wait()
-        left = left_of(basis_ref[1 - c], grads_ref[1 - c, ROWS * j : ROWS * (j + 1)])
-        for t in range(4):
-            out_ref[4 * t + j] = left[8 * t : 8 * t + 8]
+        columns = slice(WIDE * j, WIDE * (j + 1))
+        left = left + left_of(basis_ref[1 - h, :, columns], grads_ref[1 - h, :, columns])
+    put_left(left, out_ref)
     for k in range(4, 8):
         copies[k].wait()
 
 
 def left_body(basis_ref, grads_ref, out_ref):
-    left = left_of(basis_ref[core()], grads_ref[core()])
-    for t in range(4):
-        for j in range(4):
-            out_ref[4 * t + j] = left[8 * t : 8 * t + 8, LANES * j : LANES * j + LANES]
-
-
-def right_body(mine, left_ref, grads_ref, out_ref):
-    layer = core() if mine else 1 - core()
+    h = held()
+    put_left(left_of(basis_ref[h], grads_ref[h]), out_ref)
+
+
+def right_body(kept, mine_ref, other_ref, grads_ref, out_ref):
+    layer = core() if kept else 1 - core()
+    left = jnp.where(layer == held(), joined(mine_ref, 4, 4), joined(other_ref, 4, 4))
     right = jnp.dot(
-        joined(left_ref, 4, 4).astype(jnp.bfloat16),
+        left.astype(jnp.bfloat16),
         grads_ref[layer],
         preferred_element_type=jnp.float32,
     )
@@ -115,7 +125,7 @@
 
 def by_layer(mine_ref, other_ref):
     mine, other = joined(mine_ref, 4, 4), joined(other_ref, 4, 4)
-    first = core() == 0
+    first = held() == 0
     return jnp.where(first, mine, other), jnp.where(first, other, mine)
 
 
@@ -285,6 +295,9 @@
     new_w_ref[layer] = weights
 
 
+DOUBLING = ((1, 1), (3, 1), (4, 1), (8, 0))
+
+
 def swapped(value):
     return lax.ppermute(value, "core", [(0, 1), (1, 0)])
 
@@ -313,12 +326,12 @@
     )(*(pltpu.with_memory_space_constraint(a, pltpu.HBM) for a in (basis, grads)))
     away = swapped(away)
     mine = kernel_call(left_body, lefts)(basis, grads) + away
-    for axis, bit in (("y", 1), ("y", 3), ("zlo", 1), ("zlo", 2)):
-        mine = mine + lax.ppermute(mine, axis, [(i, i ^ bit) for i in range(SIZES[axis])])
+    for flip, cross in DOUBLING:
+        pairs = [(2 * p + c, 2 * (p ^ flip) + (c ^ cross)) for p in range(16) for c in range(2)]
+        mine = mine + lax.ppermute(mine, REPLICA, pairs)
     other = swapped(mine)
-    kept = kernel_call(functools.partial(right_body, True), rights)(mine, grads)
-    kept, other = lax.optimization_barrier((kept, other))
-    away = swapped(kernel_call(functools.partial(right_body, False), rights)(other, grads))
+    away = swapped(kernel_call(functools.partial(right_body, False), rights)(mine, other, grads))
+    kept = kernel_call(functools.partial(right_body, True), rights)(mine, other, grads)
     share = kernel_call(gram_body, f32(4, LANES))(mine, other)
 
     sent = kernel_call(pack_body, f32(PEERS * CHUNK, LANES))(kept, away, share)

time: 74.2 us -> 73.8 us (level)
  starting transfers between devices: 16.5 us -> 12.1 us
  waiting for transfers between devices: 14.1 us -> 18.4 us
    ppermute x4, starting transfers between devices: 13.6 us -> 9.1 us  [swapped(): return lax.ppermute(value, 'core', [(0, 1), (1, 0)])]
    ppermute x4, waiting for transfers between devices: 12.4 us -> 16.8 us  [shards(): mine = mine + lax.ppermute(mine, REPLICA, pairs)]
where the time goes in v6:
time: 73.8 us; the launch traced here: 73.6 us
  blocking collectives  36.2 us (49%)
  waiting for transfers between devices  18.4 us (25%)
  starting transfers between devices  12.1 us (16%)
  Pallas kernels  6.02 us (8%)
    all_to_all x3, blocking collectives, all_to_all(): return lax.all_to_all(value, axes, 0, 0, tiled=True)  36.2 us
    ppermute x4, waiting for transfers between devices, shards(): mine = mine + lax.ppermute(mine, REPLICA, pairs)  16.8 us
    ppermute x4, starting transfers between devices, swapped(): return lax.ppermute(value, 'core', [(0, 1), (1, 0)])  9.1 us
    pallas_call x10, Pallas kernels, kernel_call(): pl.pallas_call(body, out_shape=outs, in_specs=[spec] * len(args), out_spe...  4.33 us
    ppermute x4, starting transfers between devices, shards(): mine = mine + lax.ppermute(mine, REPLICA, pairs)  3.02 us
    pallas_call x1, Pallas kernels, shards(): pl.pallas_call(first_body, out_shape=[lefts, jax.ShapeDtypeStruct(grads.s...  1.69 us
    ppermute x4, waiting for transfers between devices, swapped(): return lax.ppermute(value, 'core', [(0, 1), (1, 0)])  1.69 us
  transfers between devices with their start and end apart: 8, of which 7 were waited for; matrix products, arithmetic and copies ran while one was open for 0% of the time, Pallas kernels for 4%

profile of v6, /device:TPU:1, one launch (start us, length us, event | category | flops | bytes accessed | tf_op | source)
XLA Modules:
  0.0 73.6 jit_solution(5505363608285776498)
XLA Ops:
  0.6 1.7 %shard_map.67 = (f32[16,8,128]{2,1,0:T(8,128)S(1)}, bf16[2,512,1024]{2,1,0:T(8,128)(2,1)S(1)}, f32[2,32,1024]{2,1,0:T(8,128)S(1)}) custom-call(f32[2,32,1024]{2,1,0:T(8,128)} %bitcast.23, bf16[2,512,1024]{2,1,0:T(8,128)(2,1)} %bitcast.22), custom_call_target="tpu_custom_call" | custom-call | flops 1048576 | bytes 262144 | tf_op jit(solution)/shard_map/pallas_call | solution.py:318
  2.3 3.3 %collective-permute-start = (f32[16,8,128]{2,1,0:T(8,128)S(1)}, f32[16,8,128]{2,1,0:T(8,128)S(1)}, u32[]{:S(2)}, u32[]{:S(2)}) collective-permute-start(f32[16,8,128]{2,1,0:T(8,128)S(1)} %get-tuple-element.20), channel_id=1, source_target_pairs={{0,8},{8,0},{1,9},{9,1},{2,10},{10,2},{3,11},{11,3},{4,12},{12,4},... | collective-permute-start | bytes 196616 | tf_op jit(solution)/shard_map/ppermute | solution.py:302
  5.6 0.4 shard_map.68
  6.0 0.5 collective-permute-done
  6.5 0.1 collective-permute-start.1
  6.6 4.0 %collective-permute-done.1 = f32[16,8,128]{2,1,0:T(8,128)S(1)} collective-permute-done((f32[16,8,128]{2,1,0:T(8,128)S(1)}, f32[16,8,128]{2,1,0:T(8,128)S(1)}, u32[]{:S(2)}, u32[]{:S(2)}) %collective-permute-start.1) | collective-permute-done | bytes 65568 | tf_op jit(solution)/shard_map/ppermute | solution.py:331
  10.7 1.3 %collective-permute-start.2 = (f32[16,8,128]{2,1,0:T(8,128)S(1)}, f32[16,8,128]{2,1,0:T(8,128)S(1)}, u32[]{:S(2)}, u32[]{:S(2)}) collective-permute-start(f32[16,8,128]{2,1,0:T(8,128)S(1)} %add.16), channel_id=1, source_target_pairs={{0,56},{8,48},{16,40},{24,32},{32,24},{40,16},{48,8},{56,0},{64,12... | collective-permute-start | bytes 196616 | tf_op jit(solution)/shard_map/ppermute | solution.py:331
  12.0 4.0 %collective-permute-done.2 = f32[16,8,128]{2,1,0:T(8,128)S(1)} collective-permute-done((f32[16,8,128]{2,1,0:T(8,128)S(1)}, f32[16,8,128]{2,1,0:T(8,128)S(1)}, u32[]{:S(2)}, u32[]{:S(2)}) %collective-permute-start.2) | collective-permute-done | bytes 65568 | tf_op jit(solution)/shard_map/ppermute | solution.py:331
  16.1 0.2 collective-permute-start.3
  16.3 3.9 %collective-permute-done.3 = f32[16,8,128]{2,1,0:T(8,128)S(1)} collective-permute-done((f32[16,8,128]{2,1,0:T(8,128)S(1)}, f32[16,8,128]{2,1,0:T(8,128)S(1)}, u32[]{:S(2)}, u32[]{:S(2)}) %collective-permute-start.3) | collective-permute-done | bytes 65568 | tf_op jit(solution)/shard_map/ppermute | solution.py:331
  20.2 1.3 %collective-permute-start.4 = (f32[16,8,128]{2,1,0:T(8,128)S(1)}, f32[16,8,128]{2,1,0:T(8,128)S(1)}, u32[]{:S(2)}, u32[]{:S(2)}) collective-permute-start(f32[16,8,128]{2,1,0:T(8,128)S(1)} %add.18), channel_id=1, source_target_pairs={{0,128},{8,136},{16,144},{24,152},{32,160},{40,168},{48,176},{56,1... | collective-permute-start | bytes 196616 | tf_op jit(solution)/shard_map/ppermute | solution.py:331
  21.6 4.8 %collective-permute-done.4 = f32[16,8,128]{2,1,0:T(8,128)S(1)} collective-permute-done((f32[16,8,128]{2,1,0:T(8,128)S(1)}, f32[16,8,128]{2,1,0:T(8,128)S(1)}, u32[]{:S(2)}, u32[]{:S(2)}) %collective-permute-start.4) | collective-permute-done | bytes 65568 | tf_op jit(solution)/shard_map/ppermute | solution.py:331
  26.4 0.8 %collective-permute-start.5 = (f32[16,8,128]{2,1,0:T(8,128)S(1)}, f32[16,8,128]{2,1,0:T(8,128)S(1)}, u32[]{:S(2)}, u32[]{:S(2)}) collective-permute-start(f32[16,8,128]{2,1,0:T(8,128)S(1)} %add.19.mine_ref), channel_id=1, source_target_pairs={{0,8},{8,0},{1,9},{9,1},{2,10},{10,2},{3,11},{11,3},{4,12},{12,4},... | collective-permute-start | bytes 196616 | tf_op jit(solution)/shard_map/ppermute | solution.py:302
  27.2 0.9 %collective-permute-done.5.other_ref = f32[16,8,128]{2,1,0:T(8,128)S(1)} collective-permute-done((f32[16,8,128]{2,1,0:T(8,128)S(1)}, f32[16,8,128]{2,1,0:T(8,128)S(1)}, u32[]{:S(2)}, u32[]{:S(2)}) %collective-permute-start.5) | collective-permute-done | bytes 65568 | tf_op jit(solution)/shard_map/ppermute | solution.py:302
  28.1 0.3 shard_map.70
  28.4 0.0 copy-start
  28.4 0.0 copy-start.1
  28.4 0.4 collective-permute-start.6
  28.8 0.3 shard_map.69.mine_ref
  29.1 0.4 shard_map.71.share_ref
  29.5 0.3 collective-permute-done.6.other_ref
  29.9 10.9 %all_to_all.15 = f32[80,4,128]{2,1,0:T(4,128)S(1)} all-to-all(f32[80,4,128]{2,1,0:T(4,128)S(1)} %bitcast.12), channel_id=1, replica_groups=mesh['zlo'=4,'y'=4,'core'=2,'zhi'=2,'x'=4] {'y','x'}, dimensions={0} | all-to-all | bytes 327680 | tf_op jit(solution)/shard_map/all_to_all | solution.py:306
  40.8 15.5 %all_to_all.16 = f32[40,4,128]{2,1,0:T(4,128)S(1)} all-to-all(f32[40,4,128]{2,1,0:T(4,128)S(1)} %bitcast.21), channel_id=1, replica_groups=mesh['zlo'=4,'y'=4,'core'=2,'zhi'=2,'x'=4] {'zlo','zhi'}, dimensions={0} | all-to-all | bytes 163840 | tf_op jit(solution)/shard_map/all_to_all | solution.py:306
  56.3 9.8 %all_to_all.17 = f32[16,16,128]{2,1,0:T(8,128)S(1)} all-to-all(f32[16,16,128]{2,1,0:T(8,128)S(1)} %get-tuple-element.21), channel_id=1, replica_groups=mesh['zlo'=4,'y'=4,'core'=2,'zhi'=2,'x'=4] {'y','x'}, dimensions={0} | all-to-all | bytes 262144 | tf_op jit(solution)/shard_map/all_to_all | solution.py:306
  66.1 4.5 %collective-permute-start.7 = (f32[32,8,128]{2,1,0:T(8,128)S(1)}, f32[32,8,128]{2,1,0:T(8,128)S(1)}, u32[]{:S(2)}, u32[]{:S(2)}) collective-permute-start(f32[32,8,128]{2,1,0:T(8,128)S(1)} %bitcast.18), channel_id=1, source_target_pairs={{0,8},{8,0},{1,9},{9,1},{2,10},{10,2},{3,11},{11,3},{4,12},{12,4},... | collective-permute-start | bytes 393224 | tf_op jit(solution)/shard_map/ppermute | solution.py:302
  70.6 1.0 %shard_map.75 = (f32[32,128]{1,0:T(8,128)S(1)}, f32[2,32,512]{2,1,0:T(8,128)S(1)}) custom-call(f32[16,128]{1,0:T(8,128)S(1)} %get-tuple-element.24.gram_ref, f32[16,8,128]{2,1,0:T(8,128)S(1)} %add.19.mine_ref, f32[16,8,128]{2,1,0:T(8,128)S(1)} %collective-permute-done.5.other_ref), custom_call_target="tpu_custom_call" | custom-call | flops 1048576 | bytes 262144 | tf_op jit(solution)/shard_map/pallas_call | solution.py:29
  71.7 0.0 copy-done
  71.7 0.0 copy-done.1
  71.7 0.6 shard_map.76
  72.3 0.0 collective-permute-done.7.right_ref
  72.3 1.3 %shard_map.77 = (f32[2,32,1024]{2,1,0:T(8,128)}, f32[2,32,512]{2,1,0:T(8,128)}, f32[2,32,512]{2,1,0:T(8,128)}) custom-call(f32[32,8,128]{2,1,0:T(8,128)S(1)} %collective-permute-done.7.right_ref, f32[32,128]{1,0:T(8,128)S(1)} %get-tuple-element.25.inverse_ref, f32[2,32,512]{2,1,0:T(8,128)S(1)} %get-tuple-element.26.frame_ref, f32[2,32,512]{2,1,0:T(8,128)S(1)} %bitcast.15, ...), custom_call_target="tpu_custom_call" | custom-call | flops 1048576 | bytes 262144 | tf_op jit(solution)/shard_map/pallas_call | solution.py:29
  (8 shorter events, 0.1 us)
Async XLA Ops:
  2.3 4.2 %collective-permute-start = (f32[16,8,128]{2,1,0:T(8,128)S(1)}, f32[16,8,128]{2,1,0:T(8,128)S(1)}, u32[]{:S(2)}, u32[]{:S(2)}) collective-permute-start(f32[16,8,128]{2,1,0:T(8,128)S(1)} %get-tuple-element.20), channel_id=1, source_target_pairs={{0,8},{8,0},{1,9},{9,1},{2,10},{10,2},{3,11},{11,3},{4,12},{12,4},... | collective-permute-start | bytes 196616 | tf_op jit(solution)/shard_map/ppermute | solution.py:302
  6.5 4.1 %collective-permute-start.1 = (f32[16,8,128]{2,1,0:T(8,128)S(1)}, f32[16,8,128]{2,1,0:T(8,128)S(1)}, u32[]{:S(2)}, u32[]{:S(2)}) collective-permute-start(f32[16,8,128]{2,1,0:T(8,128)S(1)} %add.15), channel_id=1, source_target_pairs={{0,24},{8,16},{16,8},{24,0},{32,56},{40,48},{48,40},{56,32},{64,88... | collective-permute-start | bytes 196616 | tf_op jit(solution)/shard_map/ppermute | solution.py:331
  10.7 5.4 %collective-permute-start.2 = (f32[16,8,128]{2,1,0:T(8,128)S(1)}, f32[16,8,128]{2,1,0:T(8,128)S(1)}, u32[]{:S(2)}, u32[]{:S(2)}) collective-permute-start(f32[16,8,128]{2,1,0:T(8,128)S(1)} %add.16), channel_id=1, source_target_pairs={{0,56},{8,48},{16,40},{24,32},{32,24},{40,16},{48,8},{56,0},{64,12... | collective-permute-start | bytes 196616 | tf_op jit(solution)/shard_map/ppermute | solution.py:331
  16.1 4.1 %collective-permute-start.3 = (f32[16,8,128]{2,1,0:T(8,128)S(1)}, f32[16,8,128]{2,1,0:T(8,128)S(1)}, u32[]{:S(2)}, u32[]{:S(2)}) collective-permute-start(f32[16,8,128]{2,1,0:T(8,128)S(1)} %add.17), channel_id=1, source_target_pairs={{0,72},{8,64},{16,88},{24,80},{32,104},{40,96},{48,120},{56,112},{... | collective-permute-start | bytes 196616 | tf_op jit(solution)/shard_map/ppermute | solution.py:331
  20.2 6.1 %collective-permute-start.4 = (f32[16,8,128]{2,1,0:T(8,128)S(1)}, f32[16,8,128]{2,1,0:T(8,128)S(1)}, u32[]{:S(2)}, u32[]{:S(2)}) collective-permute-start(f32[16,8,128]{2,1,0:T(8,128)S(1)} %add.18), channel_id=1, source_target_pairs={{0,128},{8,136},{16,144},{24,152},{32,160},{40,168},{48,176},{56,1... | collective-permute-start | bytes 196616 | tf_op jit(solution)/shard_map/ppermute | solution.py:331
  26.4 1.7 %collective-permute-start.5 = (f32[16,8,128]{2,1,0:T(8,128)S(1)}, f32[16,8,128]{2,1,0:T(8,128)S(1)}, u32[]{:S(2)}, u32[]{:S(2)}) collective-permute-start(f32[16,8,128]{2,1,0:T(8,128)S(1)} %add.19.mine_ref), channel_id=1, source_target_pairs={{0,8},{8,0},{1,9},{9,1},{2,10},{10,2},{3,11},{11,3},{4,12},{12,4},... | collective-permute-start | bytes 196616 | tf_op jit(solution)/shard_map/ppermute | solution.py:302
  28.4 43.3 %copy-start = (f32[2,512,32]{1,2,0:T(8,128)S(1)}, f32[2,512,32]{1,2,0:T(8,128)}, u32[]{:S(2)}) copy-start(f32[2,512,32]{1,2,0:T(8,128)} %param.6) | copy-start | bytes 393220
  28.4 43.3 %copy-start.1 = (f32[2,512,32]{1,2,0:T(8,128)S(1)}, f32[2,512,32]{1,2,0:T(8,128)}, u32[]{:S(2)}) copy-start(f32[2,512,32]{1,2,0:T(8,128)} %param.7) | copy-start | bytes 393220
  28.4 1.4 %collective-permute-start.6 = (f32[16,16,128]{2,1,0:T(8,128)S(1)}, f32[16,16,128]{2,1,0:T(8,128)S(1)}, u32[]{:S(2)}, u32[]{:S(2)}) collective-permute-start(f32[16,16,128]{2,1,0:T(8,128)S(1)} %shard_map.70), channel_id=1, source_target_pairs={{0,8},{8,0},{1,9},{9,1},{2,10},{10,2},{3,11},{11,3},{4,12},{12,4},... | collective-permute-start | bytes 393224 | tf_op jit(solution)/shard_map/ppermute | solution.py:302
  66.1 6.2 %collective-permute-start.7 = (f32[32,8,128]{2,1,0:T(8,128)S(1)}, f32[32,8,128]{2,1,0:T(8,128)S(1)}, u32[]{:S(2)}, u32[]{:S(2)}) collective-permute-start(f32[32,8,128]{2,1,0:T(8,128)S(1)} %bitcast.18), channel_id=1, source_target_pairs={{0,8},{8,0},{1,9},{9,1},{2,10},{10,2},{3,11},{11,3},{4,12},{12,4},... | collective-permute-start | bytes 393224 | tf_op jit(solution)/shard_map/ppermute | solution.py:302

commit v7 on v6

--- a/solution.py
+++ b/solution.py
@@ -1,4 +1,5 @@
 import functools
+import itertools
 
 import jax
 import jax.numpy as jnp
@@ -13,8 +14,8 @@
 SIZES = {"zlo": 4, "y": 4, "core": 2, "zhi": 2, "x": 4}
 REPLICA = ("zlo", "y", "core")
 MODEL = ("zhi", "x")
-PLANE = ("y", "x")
-COLUMN = ("zlo", "zhi")
+PLANE = ("y", "core", "x")
+COLUMN = ("zlo", "core", "zhi")
 REPLICAS, PEERS, STACK = 32, 16, 8
 CHUNK = 20
 BLOCK = 16
@@ -64,6 +65,10 @@
 
 def held():
     return (core() + lax.axis_index("y") + lax.axis_index("zlo")) % 2
+
+
+def owned():
+    return (core() + lax.axis_index("y") // 2 + lax.axis_index("zhi")) % 2
 
 
 WIDE = 256
@@ -110,7 +115,7 @@
 
 
 def right_body(kept, mine_ref, other_ref, grads_ref, out_ref):
-    layer = core() if kept else 1 - core()
+    layer = owned() if kept else 1 - owned()
     left = jnp.where(layer == held(), joined(mine_ref, 4, 4), joined(other_ref, 4, 4))
     right = jnp.dot(
         left.astype(jnp.bfloat16),
@@ -274,7 +279,7 @@
 
 
 def early_body(right_ref, inverse_ref, frame_ref, weights_ref, momentum_ref, basis_ref, w_ref, m_ref):
-    scale, new, weights = settle(core(), right_ref, inverse_ref, frame_ref, weights_ref, momentum_ref)
+    scale, new, weights = settle(owned(), right_ref, inverse_ref, frame_ref, weights_ref, momentum_ref)
     scaled(right_ref, scale, basis_ref, None)
     m_ref[...] = new
     w_ref[...] = weights
@@ -284,7 +289,7 @@
     right_ref, inverse_ref, frame_ref, weights_ref, momentum_ref, b_ref, w_ref, m_ref,
     basis_ref, new_w_ref, new_m_ref,
 ):
-    c = core()
+    c = owned()
     basis_ref[c] = b_ref[...]
     new_w_ref[c] = w_ref[...]
     new_m_ref[c] = m_ref[...]
@@ -303,7 +308,11 @@
 
 
 def all_to_all(value, axes):
-    return lax.all_to_all(value, axes, 0, 0, tiled=True)
+    groups = ([], [])
+    for i, place in enumerate(itertools.product(*(range(SIZES[a]) for a in axes))):
+        at = dict(zip(axes, place))
+        groups[(at["core"] + at.get("y", 0) // 2 + at.get("zhi", 0)) % 2].append(i)
+    return lax.all_to_all(value, axes, 0, 0, axis_index_groups=groups, tiled=True)
 
 
 def shards(layer_grads, last_basis, layer_weights, momentum):

time: 73.8 us -> 71.7 us (0.972)
  starting transfers between devices: 12.1 us -> 7.74 us
  blocking collectives: 36.2 us -> 38.5 us
    ppermute x4, starting transfers between devices: 9.1 us -> 4.72 us  [swapped(): return lax.ppermute(value, 'core', [(0, 1), (1, 0)])]
    all_to_all x3, blocking collectives: 36.2 us -> 38.5 us  [all_to_all(): lax.all_to_all(value, axes, 0, 0, axis_index_groups=groups, tiled=True)]
where the time goes in v7:
time: 71.7 us; the launch traced here: 71.5 us
  blocking collectives  38.5 us (54%)
  waiting for transfers between devices  18.4 us (26%)
  starting transfers between devices  7.74 us (11%)
  Pallas kernels  6.02 us (8%)
  between operations  0.73 us (1%)
    all_to_all x3, blocking collectives, all_to_all(): lax.all_to_all(value, axes, 0, 0, axis_index_groups=groups, tiled=True)  38.5 us
    ppermute x4, waiting for transfers between devices, shards(): mine = mine + lax.ppermute(mine, REPLICA, pairs)  16.8 us
    ppermute x4, starting transfers between devices, swapped(): return lax.ppermute(value, 'core', [(0, 1), (1, 0)])  4.72 us
    pallas_call x10, Pallas kernels, kernel_call(): pl.pallas_call(body, out_shape=outs, in_specs=[spec] * len(args), out_spe...  4.33 us
    ppermute x4, starting transfers between devices, shards(): mine = mine + lax.ppermute(mine, REPLICA, pairs)  3.02 us
    pallas_call x1, Pallas kernels, shards(): pl.pallas_call(first_body, out_shape=[lefts, jax.ShapeDtypeStruct(grads.s...  1.69 us
    ppermute x4, waiting for transfers between devices, swapped(): return lax.ppermute(value, 'core', [(0, 1), (1, 0)])  1.69 us
  transfers between devices with their start and end apart: 8, of which 7 were waited for; matrix products, arithmetic and copies ran while one was open for 0% of the time, Pallas kernels for 4%

profile of v7, /device:TPU:1, one launch (start us, length us, event | category | flops | bytes accessed | tf_op | source)
XLA Modules:
  0.0 71.5 jit_solution(800326481476292740)
XLA Ops:
  0.6 1.7 %shard_map.67 = (f32[16,8,128]{2,1,0:T(8,128)S(1)}, bf16[2,512,1024]{2,1,0:T(8,128)(2,1)S(1)}, f32[2,32,1024]{2,1,0:T(8,128)S(1)}) custom-call(f32[2,32,1024]{2,1,0:T(8,128)} %bitcast.23, bf16[2,512,1024]{2,1,0:T(8,128)(2,1)} %bitcast.22), custom_call_target="tpu_custom_call" | custom-call | flops 1048576 | bytes 262144 | tf_op jit(solution)/shard_map/pallas_call | solution.py:327
  2.3 3.3 %collective-permute-start = (f32[16,8,128]{2,1,0:T(8,128)S(1)}, f32[16,8,128]{2,1,0:T(8,128)S(1)}, u32[]{:S(2)}, u32[]{:S(2)}) collective-permute-start(f32[16,8,128]{2,1,0:T(8,128)S(1)} %get-tuple-element.20), channel_id=1, source_target_pairs={{0,8},{8,0},{1,9},{9,1},{2,10},{10,2},{3,11},{11,3},{4,12},{12,4},... | collective-permute-start | bytes 196616 | tf_op jit(solution)/shard_map/ppermute | solution.py:307
  5.6 0.4 shard_map.68
  6.0 0.5 collective-permute-done
  6.5 0.1 collective-permute-start.1
  6.6 4.0 %collective-permute-done.1 = f32[16,8,128]{2,1,0:T(8,128)S(1)} collective-permute-done((f32[16,8,128]{2,1,0:T(8,128)S(1)}, f32[16,8,128]{2,1,0:T(8,128)S(1)}, u32[]{:S(2)}, u32[]{:S(2)}) %collective-permute-start.1) | collective-permute-done | bytes 65568 | tf_op jit(solution)/shard_map/ppermute | solution.py:340
  10.7 1.3 %collective-permute-start.2 = (f32[16,8,128]{2,1,0:T(8,128)S(1)}, f32[16,8,128]{2,1,0:T(8,128)S(1)}, u32[]{:S(2)}, u32[]{:S(2)}) collective-permute-start(f32[16,8,128]{2,1,0:T(8,128)S(1)} %add.16), channel_id=1, source_target_pairs={{0,56},{8,48},{16,40},{24,32},{32,24},{40,16},{48,8},{56,0},{64,12... | collective-permute-start | bytes 196616 | tf_op jit(solution)/shard_map/ppermute | solution.py:340
  12.0 4.0 %collective-permute-done.2 = f32[16,8,128]{2,1,0:T(8,128)S(1)} collective-permute-done((f32[16,8,128]{2,1,0:T(8,128)S(1)}, f32[16,8,128]{2,1,0:T(8,128)S(1)}, u32[]{:S(2)}, u32[]{:S(2)}) %collective-permute-start.2) | collective-permute-done | bytes 65568 | tf_op jit(solution)/shard_map/ppermute | solution.py:340
  16.1 0.2 collective-permute-start.3
  16.3 3.9 %collective-permute-done.3 = f32[16,8,128]{2,1,0:T(8,128)S(1)} collective-permute-done((f32[16,8,128]{2,1,0:T(8,128)S(1)}, f32[16,8,128]{2,1,0:T(8,128)S(1)}, u32[]{:S(2)}, u32[]{:S(2)}) %collective-permute-start.3) | collective-permute-done | bytes 65568 | tf_op jit(solution)/shard_map/ppermute | solution.py:340
  20.2 1.3 %collective-permute-start.4 = (f32[16,8,128]{2,1,0:T(8,128)S(1)}, f32[16,8,128]{2,1,0:T(8,128)S(1)}, u32[]{:S(2)}, u32[]{:S(2)}) collective-permute-start(f32[16,8,128]{2,1,0:T(8,128)S(1)} %add.18), channel_id=1, source_target_pairs={{0,128},{8,136},{16,144},{24,152},{32,160},{40,168},{48,176},{56,1... | collective-permute-start | bytes 196616 | tf_op jit(solution)/shard_map/ppermute | solution.py:340
  21.6 4.8 %collective-permute-done.4 = f32[16,8,128]{2,1,0:T(8,128)S(1)} collective-permute-done((f32[16,8,128]{2,1,0:T(8,128)S(1)}, f32[16,8,128]{2,1,0:T(8,128)S(1)}, u32[]{:S(2)}, u32[]{:S(2)}) %collective-permute-start.4) | collective-permute-done | bytes 65568 | tf_op jit(solution)/shard_map/ppermute | solution.py:340
  26.4 0.8 %collective-permute-start.5 = (f32[16,8,128]{2,1,0:T(8,128)S(1)}, f32[16,8,128]{2,1,0:T(8,128)S(1)}, u32[]{:S(2)}, u32[]{:S(2)}) collective-permute-start(f32[16,8,128]{2,1,0:T(8,128)S(1)} %add.19.mine_ref), channel_id=1, source_target_pairs={{0,8},{8,0},{1,9},{9,1},{2,10},{10,2},{3,11},{11,3},{4,12},{12,4},... | collective-permute-start | bytes 196616 | tf_op jit(solution)/shard_map/ppermute | solution.py:307
  27.2 0.9 %collective-permute-done.5.other_ref = f32[16,8,128]{2,1,0:T(8,128)S(1)} collective-permute-done((f32[16,8,128]{2,1,0:T(8,128)S(1)}, f32[16,8,128]{2,1,0:T(8,128)S(1)}, u32[]{:S(2)}, u32[]{:S(2)}) %collective-permute-start.5) | collective-permute-done | bytes 65568 | tf_op jit(solution)/shard_map/ppermute | solution.py:307
  28.1 0.3 shard_map.70
  28.4 0.0 copy-start
  28.4 0.0 copy-start.1
  28.4 0.4 collective-permute-start.6
  28.8 0.3 shard_map.69.mine_ref
  29.1 0.4 shard_map.71.share_ref
  29.5 0.3 collective-permute-done.6.other_ref
  29.9 12.1 %all_to_all.15 = f32[80,4,128]{2,1,0:T(4,128)S(1)} all-to-all(f32[80,4,128]{2,1,0:T(4,128)S(1)} %bitcast.12), channel_id=1, replica_groups={{0,1,2,3,16,17,18,19,40,41,42,43,56,57,58,59},{8,9,10,11,24,25,26,27,32..., dimensions={0} | all-to-all | bytes 327680 | tf_op jit(solution)/shard_map/all_to_all | solution.py:315
  42.0 13.9 %all_to_all.16 = f32[40,4,128]{2,1,0:T(4,128)S(1)} all-to-all(f32[40,4,128]{2,1,0:T(4,128)S(1)} %bitcast.21), channel_id=1, replica_groups={{0,12,64,76,128,140,192,204},{4,8,68,72,132,136,196,200},{1,13,65,77,12..., dimensions={0} | all-to-all | bytes 163840 | tf_op jit(solution)/shard_map/all_to_all | solution.py:315
  55.9 12.5 %all_to_all.17 = f32[16,16,128]{2,1,0:T(8,128)S(1)} all-to-all(f32[16,16,128]{2,1,0:T(8,128)S(1)} %get-tuple-element.21), channel_id=1, replica_groups={{0,1,2,3,16,17,18,19,40,41,42,43,56,57,58,59},{8,9,10,11,24,25,26,27,32..., dimensions={0} | all-to-all | bytes 262144 | tf_op jit(solution)/shard_map/all_to_all | solution.py:315
  68.4 0.2 collective-permute-start.7
  68.5 1.0 %shard_map.75 = (f32[32,128]{1,0:T(8,128)S(1)}, f32[2,32,512]{2,1,0:T(8,128)S(1)}) custom-call(f32[16,128]{1,0:T(8,128)S(1)} %get-tuple-element.24.gram_ref, f32[16,8,128]{2,1,0:T(8,128)S(1)} %add.19.mine_ref, f32[16,8,128]{2,1,0:T(8,128)S(1)} %collective-permute-done.5.other_ref), custom_call_target="tpu_custom_call" | custom-call | flops 1048576 | bytes 262144 | tf_op jit(solution)/shard_map/pallas_call | solution.py:30
  69.6 0.0 copy-done
  69.6 0.0 copy-done.1
  69.6 0.6 shard_map.76
  70.2 0.0 collective-permute-done.7.right_ref
  70.2 1.3 %shard_map.77 = (f32[2,32,1024]{2,1,0:T(8,128)}, f32[2,32,512]{2,1,0:T(8,128)}, f32[2,32,512]{2,1,0:T(8,128)}) custom-call(f32[32,8,128]{2,1,0:T(8,128)S(1)} %collective-permute-done.7.right_ref, f32[32,128]{1,0:T(8,128)S(1)} %get-tuple-element.25.inverse_ref, f32[2,32,512]{2,1,0:T(8,128)S(1)} %get-tuple-element.26.frame_ref, f32[2,32,512]{2,1,0:T(8,128)S(1)} %bitcast.15, ...), custom_call_target="tpu_custom_call" | custom-call | flops 1048576 | bytes 262144 | tf_op jit(solution)/shard_map/pallas_call | solution.py:30
  (8 shorter events, 0.1 us)
Async XLA Ops:
  2.3 4.2 %collective-permute-start = (f32[16,8,128]{2,1,0:T(8,128)S(1)}, f32[16,8,128]{2,1,0:T(8,128)S(1)}, u32[]{:S(2)}, u32[]{:S(2)}) collective-permute-start(f32[16,8,128]{2,1,0:T(8,128)S(1)} %get-tuple-element.20), channel_id=1, source_target_pairs={{0,8},{8,0},{1,9},{9,1},{2,10},{10,2},{3,11},{11,3},{4,12},{12,4},... | collective-permute-start | bytes 196616 | tf_op jit(solution)/shard_map/ppermute | solution.py:307
  6.5 4.1 %collective-permute-start.1 = (f32[16,8,128]{2,1,0:T(8,128)S(1)}, f32[16,8,128]{2,1,0:T(8,128)S(1)}, u32[]{:S(2)}, u32[]{:S(2)}) collective-permute-start(f32[16,8,128]{2,1,0:T(8,128)S(1)} %add.15), channel_id=1, source_target_pairs={{0,24},{8,16},{16,8},{24,0},{32,56},{40,48},{48,40},{56,32},{64,88... | collective-permute-start | bytes 196616 | tf_op jit(solution)/shard_map/ppermute | solution.py:340
  10.7 5.4 %collective-permute-start.2 = (f32[16,8,128]{2,1,0:T(8,128)S(1)}, f32[16,8,128]{2,1,0:T(8,128)S(1)}, u32[]{:S(2)}, u32[]{:S(2)}) collective-permute-start(f32[16,8,128]{2,1,0:T(8,128)S(1)} %add.16), channel_id=1, source_target_pairs={{0,56},{8,48},{16,40},{24,32},{32,24},{40,16},{48,8},{56,0},{64,12... | collective-permute-start | bytes 196616 | tf_op jit(solution)/shard_map/ppermute | solution.py:340
  16.1 4.1 %collective-permute-start.3 = (f32[16,8,128]{2,1,0:T(8,128)S(1)}, f32[16,8,128]{2,1,0:T(8,128)S(1)}, u32[]{:S(2)}, u32[]{:S(2)}) collective-permute-start(f32[16,8,128]{2,1,0:T(8,128)S(1)} %add.17), channel_id=1, source_target_pairs={{0,72},{8,64},{16,88},{24,80},{32,104},{40,96},{48,120},{56,112},{... | collective-permute-start | bytes 196616 | tf_op jit(solution)/shard_map/ppermute | solution.py:340
  20.2 6.1 %collective-permute-start.4 = (f32[16,8,128]{2,1,0:T(8,128)S(1)}, f32[16,8,128]{2,1,0:T(8,128)S(1)}, u32[]{:S(2)}, u32[]{:S(2)}) collective-permute-start(f32[16,8,128]{2,1,0:T(8,128)S(1)} %add.18), channel_id=1, source_target_pairs={{0,128},{8,136},{16,144},{24,152},{32,160},{40,168},{48,176},{56,1... | collective-permute-start | bytes 196616 | tf_op jit(solution)/shard_map/ppermute | solution.py:340
  26.4 1.7 %collective-permute-start.5 = (f32[16,8,128]{2,1,0:T(8,128)S(1)}, f32[16,8,128]{2,1,0:T(8,128)S(1)}, u32[]{:S(2)}, u32[]{:S(2)}) collective-permute-start(f32[16,8,128]{2,1,0:T(8,128)S(1)} %add.19.mine_ref), channel_id=1, source_target_pairs={{0,8},{8,0},{1,9},{9,1},{2,10},{10,2},{3,11},{11,3},{4,12},{12,4},... | collective-permute-start | bytes 196616 | tf_op jit(solution)/shard_map/ppermute | solution.py:307
  28.4 41.2 %copy-start = (f32[2,512,32]{1,2,0:T(8,128)S(1)}, f32[2,512,32]{1,2,0:T(8,128)}, u32[]{:S(2)}) copy-start(f32[2,512,32]{1,2,0:T(8,128)} %param.6) | copy-start | bytes 393220
  28.4 41.2 %copy-start.1 = (f32[2,512,32]{1,2,0:T(8,128)S(1)}, f32[2,512,32]{1,2,0:T(8,128)}, u32[]{:S(2)}) copy-start(f32[2,512,32]{1,2,0:T(8,128)} %param.7) | copy-start | bytes 393220
  28.4 1.4 %collective-permute-start.6 = (f32[16,16,128]{2,1,0:T(8,128)S(1)}, f32[16,16,128]{2,1,0:T(8,128)S(1)}, u32[]{:S(2)}, u32[]{:S(2)}) collective-permute-start(f32[16,16,128]{2,1,0:T(8,128)S(1)} %shard_map.70), channel_id=1, source_target_pairs={{0,8},{8,0},{1,9},{9,1},{2,10},{10,2},{3,11},{11,3},{4,12},{12,4},... | collective-permute-start | bytes 393224 | tf_op jit(solution)/shard_map/ppermute | solution.py:307
  68.4 1.8 %collective-permute-start.7 = (f32[32,8,128]{2,1,0:T(8,128)S(1)}, f32[32,8,128]{2,1,0:T(8,128)S(1)}, u32[]{:S(2)}, u32[]{:S(2)}) collective-permute-start(f32[32,8,128]{2,1,0:T(8,128)S(1)} %bitcast.18), channel_id=1, source_target_pairs={{0,8},{8,0},{1,9},{9,1},{2,10},{10,2},{3,11},{11,3},{4,12},{12,4},... | collective-permute-start | bytes 393224 | tf_op jit(solution)/shard_map/ppermute | solution.py:307

commit v8 on v7

--- a/solution.py
+++ b/solution.py
@@ -63,12 +63,16 @@
     return lax.axis_index("core")
 
 
+def colour(y, zlo, zhi, c):
+    return (c + y // 2 + zlo + zhi) % 2
+
+
 def held():
-    return (core() + lax.axis_index("y") + lax.axis_index("zlo")) % 2
+    return colour(lax.axis_index("y"), lax.axis_index("zlo"), lax.axis_index("zhi"), core())
 
 
 def owned():
-    return (core() + lax.axis_index("y") // 2 + lax.axis_index("zhi")) % 2
+    return 1 - held()
 
 
 WIDE = 256
@@ -114,12 +118,10 @@
     put_left(left_of(basis_ref[h], grads_ref[h]), out_ref)
 
 
-def right_body(kept, mine_ref, other_ref, grads_ref, out_ref):
-    layer = owned() if kept else 1 - owned()
-    left = jnp.where(layer == held(), joined(mine_ref, 4, 4), joined(other_ref, 4, 4))
+def right_body(kept, left_ref, grads_ref, out_ref):
     right = jnp.dot(
-        left.astype(jnp.bfloat16),
-        grads_ref[layer],
+        joined(left_ref, 4, 4).astype(jnp.bfloat16),
+        grads_ref[owned() if kept else held()],
         preferred_element_type=jnp.float32,
     )
     for t in range(4):
@@ -300,7 +302,7 @@
     new_w_ref[layer] = weights
 
 
-DOUBLING = ((1, 1), (3, 1), (4, 1), (8, 0))
+DOUBLING = ((1, 0), (3, 1), (4, 1), (8, 0))
 
 
 def swapped(value):
@@ -311,7 +313,7 @@
     groups = ([], [])
     for i, place in enumerate(itertools.product(*(range(SIZES[a]) for a in axes))):
         at = dict(zip(axes, place))
-        groups[(at["core"] + at.get("y", 0) // 2 + at.get("zhi", 0)) % 2].append(i)
+        groups[colour(at.get("y", 0), at.get("zlo", 0), at.get("zhi", 0), at["core"])].append(i)
     return lax.all_to_all(value, axes, 0, 0, axis_index_groups=groups, tiled=True)
 
 
@@ -339,8 +341,8 @@
         pairs = [(2 * p + c, 2 * (p ^ flip) + (c ^ cross)) for p in range(16) for c in range(2)]
         mine = mine + lax.ppermute(mine, REPLICA, pairs)
     other = swapped(mine)
-    away = swapped(kernel_call(functools.partial(right_body, False), rights)(mine, other, grads))
-    kept = kernel_call(functools.partial(right_body, True), rights)(mine, other, grads)
+    away = swapped(kernel_call(functools.partial(right_body, False), rights)(mine, grads))
+    kept = kernel_call(functools.partial(right_body, True), rights)(other, grads)
     share = kernel_call(gram_body, f32(4, LANES))(mine, other)
 
     sent = kernel_call(pack_body, f32(PEERS * CHUNK, LANES))(kept, away, share)

time: 71.7 us -> 70.6 us (0.985)
  waiting for transfers between devices: 18.4 us -> 10.9 us
  starting transfers between devices: 7.74 us -> 14.4 us
    ppermute x4, waiting for transfers between devices: 16.8 us -> 9.28 us  [shards(): mine = mine + lax.ppermute(mine, REPLICA, pairs)]
    ppermute x4, starting transfers between devices: 3.02 us -> 7.56 us  [shards(): mine = mine + lax.ppermute(mine, REPLICA, pairs)]
    ppermute x4, starting transfers between devices: 4.72 us -> 6.87 us  [swapped(): return lax.ppermute(value, 'core', [(0, 1), (1, 0)])]
  transfers between devices with their start and end apart: 8 -> 8, of which waited for: 7 -> 6; matrix products, arithmetic and copies ran while one was open for 0% -> 0% of each run, Pallas kernels for 4% -> 4%
where the time goes in v8:
time: 70.6 us; the launch traced here: 70.4 us
  blocking collectives  38.1 us (54%)
  starting transfers between devices  14.4 us (20%)
  waiting for transfers between devices  10.9 us (15%)
  Pallas kernels  6.05 us (9%)
  between operations  0.74 us (1%)
    all_to_all x3, blocking collectives, all_to_all(): lax.all_to_all(value, axes, 0, 0, axis_index_groups=groups, tiled=True)  38.1 us
    ppermute x4, waiting for transfers between devices, shards(): mine = mine + lax.ppermute(mine, REPLICA, pairs)  9.28 us
    ppermute x4, starting transfers between devices, shards(): mine = mine + lax.ppermute(mine, REPLICA, pairs)  7.56 us
    ppermute x4, starting transfers between devices, swapped(): return lax.ppermute(value, 'core', [(0, 1), (1, 0)])  6.87 us
    pallas_call x10, Pallas kernels, kernel_call(): pl.pallas_call(body, out_shape=outs, in_specs=[spec] * len(args), out_spe...  4.36 us
    pallas_call x1, Pallas kernels, shards(): pl.pallas_call(first_body, out_shape=[lefts, jax.ShapeDtypeStruct(grads.s...  1.7 us
    ppermute x4, waiting for transfers between devices, swapped(): return lax.ppermute(value, 'core', [(0, 1), (1, 0)])  1.66 us
  transfers between devices with their start and end apart: 8, of which 6 were waited for; matrix products, arithmetic and copies ran while one was open for 0% of the time, Pallas kernels for 4%

profile of v8, /device:TPU:1, one launch (start us, length us, event | category | flops | bytes accessed | tf_op | source)
XLA Modules:
  0.0 70.4 jit_solution(2807175080175551744)
XLA Ops:
  0.6 1.7 %shard_map.67 = (f32[16,8,128]{2,1,0:T(8,128)S(1)}, bf16[2,512,1024]{2,1,0:T(8,128)(2,1)S(1)}, f32[2,32,1024]{2,1,0:T(8,128)S(1)}) custom-call(f32[2,32,1024]{2,1,0:T(8,128)} %bitcast.23, bf16[2,512,1024]{2,1,0:T(8,128)(2,1)} %bitcast.22), custom_call_target="tpu_custom_call" | custom-call | flops 1048576 | bytes 262144 | tf_op jit(solution)/shard_map/pallas_call | solution.py:329
  2.3 3.3 %collective-permute-start = (f32[16,8,128]{2,1,0:T(8,128)S(1)}, f32[16,8,128]{2,1,0:T(8,128)S(1)}, u32[]{:S(2)}, u32[]{:S(2)}) collective-permute-start(f32[16,8,128]{2,1,0:T(8,128)S(1)} %get-tuple-element.20), channel_id=1, source_target_pairs={{0,8},{8,0},{1,9},{9,1},{2,10},{10,2},{3,11},{11,3},{4,12},{12,4},... | collective-permute-start | bytes 196616 | tf_op jit(solution)/shard_map/ppermute | solution.py:309
  5.6 0.4 shard_map.68
  6.0 0.5 collective-permute-done
  6.5 0.1 collective-permute-start.1
  6.6 3.1 %collective-permute-done.1 = f32[16,8,128]{2,1,0:T(8,128)S(1)} collective-permute-done((f32[16,8,128]{2,1,0:T(8,128)S(1)}, f32[16,8,128]{2,1,0:T(8,128)S(1)}, u32[]{:S(2)}, u32[]{:S(2)}) %collective-permute-start.1) | collective-permute-done | bytes 65568 | tf_op jit(solution)/shard_map/ppermute | solution.py:342
  9.8 2.5 %collective-permute-start.2 = (f32[16,8,128]{2,1,0:T(8,128)S(1)}, f32[16,8,128]{2,1,0:T(8,128)S(1)}, u32[]{:S(2)}, u32[]{:S(2)}) collective-permute-start(f32[16,8,128]{2,1,0:T(8,128)S(1)} %add.16), channel_id=1, source_target_pairs={{0,56},{8,48},{16,40},{24,32},{32,24},{40,16},{48,8},{56,0},{64,12... | collective-permute-start | bytes 196616 | tf_op jit(solution)/shard_map/ppermute | solution.py:342
  12.3 2.5 %collective-permute-done.2 = f32[16,8,128]{2,1,0:T(8,128)S(1)} collective-permute-done((f32[16,8,128]{2,1,0:T(8,128)S(1)}, f32[16,8,128]{2,1,0:T(8,128)S(1)}, u32[]{:S(2)}, u32[]{:S(2)}) %collective-permute-start.2) | collective-permute-done | bytes 65568 | tf_op jit(solution)/shard_map/ppermute | solution.py:342
  14.8 1.7 %collective-permute-start.3 = (f32[16,8,128]{2,1,0:T(8,128)S(1)}, f32[16,8,128]{2,1,0:T(8,128)S(1)}, u32[]{:S(2)}, u32[]{:S(2)}) collective-permute-start(f32[16,8,128]{2,1,0:T(8,128)S(1)} %add.17), channel_id=1, source_target_pairs={{0,72},{8,64},{16,88},{24,80},{32,104},{40,96},{48,120},{56,112},{... | collective-permute-start | bytes 196616 | tf_op jit(solution)/shard_map/ppermute | solution.py:342
  16.5 2.0 %collective-permute-done.3 = f32[16,8,128]{2,1,0:T(8,128)S(1)} collective-permute-done((f32[16,8,128]{2,1,0:T(8,128)S(1)}, f32[16,8,128]{2,1,0:T(8,128)S(1)}, u32[]{:S(2)}, u32[]{:S(2)}) %collective-permute-start.3) | collective-permute-done | bytes 65568 | tf_op jit(solution)/shard_map/ppermute | solution.py:342
  18.5 3.2 %collective-permute-start.4 = (f32[16,8,128]{2,1,0:T(8,128)S(1)}, f32[16,8,128]{2,1,0:T(8,128)S(1)}, u32[]{:S(2)}, u32[]{:S(2)}) collective-permute-start(f32[16,8,128]{2,1,0:T(8,128)S(1)} %add.18), channel_id=1, source_target_pairs={{0,128},{8,136},{16,144},{24,152},{32,160},{40,168},{48,176},{56,1... | collective-permute-start | bytes 196616 | tf_op jit(solution)/shard_map/ppermute | solution.py:342
  21.8 1.7 %collective-permute-done.4 = f32[16,8,128]{2,1,0:T(8,128)S(1)} collective-permute-done((f32[16,8,128]{2,1,0:T(8,128)S(1)}, f32[16,8,128]{2,1,0:T(8,128)S(1)}, u32[]{:S(2)}, u32[]{:S(2)}) %collective-permute-start.4) | collective-permute-done | bytes 65568 | tf_op jit(solution)/shard_map/ppermute | solution.py:342
  23.4 0.3 shard_map.70
  23.7 0.0 copy-start
  23.7 0.0 copy-start.1
  23.8 3.4 %collective-permute-start.6 = (f32[16,16,128]{2,1,0:T(8,128)S(1)}, f32[16,16,128]{2,1,0:T(8,128)S(1)}, u32[]{:S(2)}, u32[]{:S(2)}) collective-permute-start(f32[16,16,128]{2,1,0:T(8,128)S(1)} %shard_map.70), channel_id=1, source_target_pairs={{0,8},{8,0},{1,9},{9,1},{2,10},{10,2},{3,11},{11,3},{4,12},{12,4},... | collective-permute-start | bytes 393224 | tf_op jit(solution)/shard_map/ppermute | solution.py:309
  27.1 0.1 collective-permute-start.5
  27.2 1.2 %collective-permute-done.5.left_ref.other_ref = f32[16,8,128]{2,1,0:T(8,128)S(1)} collective-permute-done((f32[16,8,128]{2,1,0:T(8,128)S(1)}, f32[16,8,128]{2,1,0:T(8,128)S(1)}, u32[]{:S(2)}, u32[]{:S(2)}) %collective-permute-start.5) | collective-permute-done | bytes 65568 | tf_op jit(solution)/shard_map/ppermute | solution.py:309
  28.4 0.3 shard_map.69.mine_ref
  28.7 0.4 shard_map.71.share_ref
  29.1 0.0 collective-permute-done.6.other_ref
  29.1 13.6 %all_to_all.15 = f32[80,4,128]{2,1,0:T(4,128)S(1)} all-to-all(f32[80,4,128]{2,1,0:T(4,128)S(1)} %bitcast.12), channel_id=1, replica_groups={{0,1,2,3,16,17,18,19,40,41,42,43,56,57,58,59},{8,9,10,11,24,25,26,27,32..., dimensions={0} | all-to-all | bytes 327680 | tf_op jit(solution)/shard_map/all_to_all | solution.py:317
  42.7 11.3 %all_to_all.16 = f32[40,4,128]{2,1,0:T(4,128)S(1)} all-to-all(f32[40,4,128]{2,1,0:T(4,128)S(1)} %bitcast.21), channel_id=1, replica_groups={{0,12,68,72,128,140,196,200},{4,8,64,76,132,136,192,204},{1,13,69,73,12..., dimensions={0} | all-to-all | bytes 163840 | tf_op jit(solution)/shard_map/all_to_all | solution.py:317
  54.0 13.3 %all_to_all.17 = f32[16,16,128]{2,1,0:T(8,128)S(1)} all-to-all(f32[16,16,128]{2,1,0:T(8,128)S(1)} %get-tuple-element.21), channel_id=1, replica_groups={{0,1,2,3,16,17,18,19,40,41,42,43,56,57,58,59},{8,9,10,11,24,25,26,27,32..., dimensions={0} | all-to-all | bytes 262144 | tf_op jit(solution)/shard_map/all_to_all | solution.py:317
  67.3 0.1 collective-permute-start.7
  67.4 1.0 %shard_map.75 = (f32[32,128]{1,0:T(8,128)S(1)}, f32[2,32,512]{2,1,0:T(8,128)S(1)}) custom-call(f32[16,128]{1,0:T(8,128)S(1)} %get-tuple-element.24.gram_ref, f32[16,8,128]{2,1,0:T(8,128)S(1)} %add.19.left_ref.mine_ref, f32[16,8,128]{2,1,0:T(8,128)S(1)} %collective-permute-done.5.left_ref.other_ref), custom_call_target="tpu_custom_call" | custom-call | flops 1048576 | bytes 262144 | tf_op jit(solution)/shard_map/pallas_call | solution.py:30
  68.5 0.0 copy-done
  68.5 0.0 copy-done.1
  68.5 0.5 shard_map.76
  69.1 0.0 collective-permute-done.7.right_ref
  69.1 1.3 %shard_map.77 = (f32[2,32,1024]{2,1,0:T(8,128)}, f32[2,32,512]{2,1,0:T(8,128)}, f32[2,32,512]{2,1,0:T(8,128)}) custom-call(f32[32,8,128]{2,1,0:T(8,128)S(1)} %collective-permute-done.7.right_ref, f32[32,128]{1,0:T(8,128)S(1)} %get-tuple-element.25.inverse_ref, f32[2,32,512]{2,1,0:T(8,128)S(1)} %get-tuple-element.26.frame_ref, f32[2,32,512]{2,1,0:T(8,128)S(1)} %bitcast.15, ...), custom_call_target="tpu_custom_call" | custom-call | flops 1048576 | bytes 262144 | tf_op jit(solution)/shard_map/pallas_call | solution.py:30
  (8 shorter events, 0.1 us)
Async XLA Ops:
  2.3 4.2 %collective-permute-start = (f32[16,8,128]{2,1,0:T(8,128)S(1)}, f32[16,8,128]{2,1,0:T(8,128)S(1)}, u32[]{:S(2)}, u32[]{:S(2)}) collective-permute-start(f32[16,8,128]{2,1,0:T(8,128)S(1)} %get-tuple-element.20), channel_id=1, source_target_pairs={{0,8},{8,0},{1,9},{9,1},{2,10},{10,2},{3,11},{11,3},{4,12},{12,4},... | collective-permute-start | bytes 196616 | tf_op jit(solution)/shard_map/ppermute | solution.py:309
  6.5 3.2 %collective-permute-start.1 = (f32[16,8,128]{2,1,0:T(8,128)S(1)}, f32[16,8,128]{2,1,0:T(8,128)S(1)}, u32[]{:S(2)}, u32[]{:S(2)}) collective-permute-start(f32[16,8,128]{2,1,0:T(8,128)S(1)} %add.15), channel_id=1, source_target_pairs={{0,16},{8,24},{16,0},{24,8},{32,48},{40,56},{48,32},{56,40},{64,80... | collective-permute-start | bytes 196616 | tf_op jit(solution)/shard_map/ppermute | solution.py:342
  9.8 5.0 %collective-permute-start.2 = (f32[16,8,128]{2,1,0:T(8,128)S(1)}, f32[16,8,128]{2,1,0:T(8,128)S(1)}, u32[]{:S(2)}, u32[]{:S(2)}) collective-permute-start(f32[16,8,128]{2,1,0:T(8,128)S(1)} %add.16), channel_id=1, source_target_pairs={{0,56},{8,48},{16,40},{24,32},{32,24},{40,16},{48,8},{56,0},{64,12... | collective-permute-start | bytes 196616 | tf_op jit(solution)/shard_map/ppermute | solution.py:342
  14.8 3.8 %collective-permute-start.3 = (f32[16,8,128]{2,1,0:T(8,128)S(1)}, f32[16,8,128]{2,1,0:T(8,128)S(1)}, u32[]{:S(2)}, u32[]{:S(2)}) collective-permute-start(f32[16,8,128]{2,1,0:T(8,128)S(1)} %add.17), channel_id=1, source_target_pairs={{0,72},{8,64},{16,88},{24,80},{32,104},{40,96},{48,120},{56,112},{... | collective-permute-start | bytes 196616 | tf_op jit(solution)/shard_map/ppermute | solution.py:342
  18.5 4.9 %collective-permute-start.4 = (f32[16,8,128]{2,1,0:T(8,128)S(1)}, f32[16,8,128]{2,1,0:T(8,128)S(1)}, u32[]{:S(2)}, u32[]{:S(2)}) collective-permute-start(f32[16,8,128]{2,1,0:T(8,128)S(1)} %add.18), channel_id=1, source_target_pairs={{0,128},{8,136},{16,144},{24,152},{32,160},{40,168},{48,176},{56,1... | collective-permute-start | bytes 196616 | tf_op jit(solution)/shard_map/ppermute | solution.py:342
  23.7 44.7 %copy-start = (f32[2,512,32]{1,2,0:T(8,128)S(1)}, f32[2,512,32]{1,2,0:T(8,128)}, u32[]{:S(2)}) copy-start(f32[2,512,32]{1,2,0:T(8,128)} %param.6) | copy-start | bytes 393220
  23.7 44.7 %copy-start.1 = (f32[2,512,32]{1,2,0:T(8,128)S(1)}, f32[2,512,32]{1,2,0:T(8,128)}, u32[]{:S(2)}) copy-start(f32[2,512,32]{1,2,0:T(8,128)} %param.7) | copy-start | bytes 393220
  23.8 5.3 %collective-permute-start.6 = (f32[16,16,128]{2,1,0:T(8,128)S(1)}, f32[16,16,128]{2,1,0:T(8,128)S(1)}, u32[]{:S(2)}, u32[]{:S(2)}) collective-permute-start(f32[16,16,128]{2,1,0:T(8,128)S(1)} %shard_map.70), channel_id=1, source_target_pairs={{0,8},{8,0},{1,9},{9,1},{2,10},{10,2},{3,11},{11,3},{4,12},{12,4},... | collective-permute-start | bytes 393224 | tf_op jit(solution)/shard_map/ppermute | solution.py:309
  27.1 1.3 %collective-permute-start.5 = (f32[16,8,128]{2,1,0:T(8,128)S(1)}, f32[16,8,128]{2,1,0:T(8,128)S(1)}, u32[]{:S(2)}, u32[]{:S(2)}) collective-permute-start(f32[16,8,128]{2,1,0:T(8,128)S(1)} %add.19.left_ref.mine_ref), channel_id=1, source_target_pairs={{0,8},{8,0},{1,9},{9,1},{2,10},{10,2},{3,11},{11,3},{4,12},{12,4},... | collective-permute-start | bytes 196616 | tf_op jit(solution)/shard_map/ppermute | solution.py:309
  67.3 1.7 %collective-permute-start.7 = (f32[32,8,128]{2,1,0:T(8,128)S(1)}, f32[32,8,128]{2,1,0:T(8,128)S(1)}, u32[]{:S(2)}, u32[]{:S(2)}) collective-permute-start(f32[32,8,128]{2,1,0:T(8,128)S(1)} %bitcast.18), channel_id=1, source_target_pairs={{0,8},{8,0},{1,9},{9,1},{2,10},{10,2},{3,11},{11,3},{4,12},{12,4},... | collective-permute-start | bytes 393224 | tf_op jit(solution)/shard_map/ppermute | solution.py:309

commit v9 on v8

--- a/solution.py
+++ b/solution.py
@@ -1,4 +1,3 @@
-import functools
 import itertools
 
 import jax
@@ -8,6 +7,7 @@
 from jax.experimental.pallas import tpu as pltpu
 from jax.sharding import Mesh
 from jax.sharding import PartitionSpec as P
+
 
 RANK = 32
 LANES = 128
@@ -118,37 +118,44 @@
     put_left(left_of(basis_ref[h], grads_ref[h]), out_ref)
 
 
-def right_body(kept, left_ref, grads_ref, out_ref):
-    right = jnp.dot(
-        joined(left_ref, 4, 4).astype(jnp.bfloat16),
-        grads_ref[owned() if kept else held()],
-        preferred_element_type=jnp.float32,
-    )
+def put_right(left, grads, out_ref):
+    right = jnp.dot(left.astype(jnp.bfloat16), grads, preferred_element_type=jnp.float32)
     for t in range(4):
         for j in range(8):
             d, h = divmod(8 * t + j, 2)
             out_ref[d, 8 * h : 8 * h + 8] = right[8 * t : 8 * t + 8, LANES * j : LANES * j + LANES]
 
 
+def packed_gram(left):
+    gram = lax.dot_general(
+        left,
+        jnp.concatenate([left] * 4, axis=0),
+        (((1,), (1,)), ((), ())),
+        precision=EXACT,
+        preferred_element_type=jnp.float32,
+    )
+    return jnp.where(lane_of((16, LANES)) < 64, gram[:16], gram[16:])
+
+
+def sent_body(left_ref, grads_ref, out_ref, gram_ref):
+    left = joined(left_ref, 4, 4)
+    put_right(left, grads_ref[held()], out_ref)
+    gram_ref[...] = packed_gram(left)
+
+
+def kept_body(left_ref, grads_ref, gram_ref, out_ref, share_ref):
+    layer = owned()
+    left = joined(left_ref, 4, 4)
+    put_right(left, grads_ref[layer], out_ref)
+    group = lane_of((16, LANES)) // RANK % 2
+    packed = jnp.where(group == layer, packed_gram(left), gram_ref[...])
+    share_ref[...] = picked([packed[4 * s : 4 * s + 4] for s in range(4)], lax.axis_index("y"))
+
+
 def by_layer(mine_ref, other_ref):
     mine, other = joined(mine_ref, 4, 4), joined(other_ref, 4, 4)
     first = held() == 0
     return jnp.where(first, mine, other), jnp.where(first, other, mine)
-
-
-def gram_body(mine_ref, other_ref, share_ref):
-    left = jnp.concatenate(by_layer(mine_ref, other_ref), axis=0)
-    twice = jnp.concatenate([left, left], axis=0)
-    gram = lax.dot_general(
-        left, twice, (((1,), (1,)), ((), ())), precision=EXACT, preferred_element_type=jnp.float32
-    )
-    lane = lane_of((16, LANES))
-    packed = jnp.where(
-        lane < 32,
-        gram[0:16],
-        jnp.where(lane < 64, gram[32:48], jnp.where(lane < 96, gram[16:32], gram[48:64])),
-    )
-    share_ref[...] = picked([packed[4 * s : 4 * s + 4] for s in range(4)], lax.axis_index("y"))
 
 
 def picked(values, index):
@@ -341,9 +348,9 @@
         pairs = [(2 * p + c, 2 * (p ^ flip) + (c ^ cross)) for p in range(16) for c in range(2)]
         mine = mine + lax.ppermute(mine, REPLICA, pairs)
     other = swapped(mine)
-    away = swapped(kernel_call(functools.partial(right_body, False), rights)(mine, grads))
-    kept = kernel_call(functools.partial(right_body, True), rights)(other, grads)
-    share = kernel_call(gram_body, f32(4, LANES))(mine, other)
+    away, gram = kernel_call(sent_body, [rights, f32(16, LANES)])(mine, grads)
+    away = swapped(away)
+    kept, share = kernel_call(kept_body, [rights, f32(4, LANES)])(other, grads, gram)
 
     sent = kernel_call(pack_body, f32(PEERS * CHUNK, LANES))(kept, away, share)
     came = all_to_all(sent.reshape(PEERS * CHUNK // 4, 4, LANES), PLANE)

time: 70.6 us -> 70.6 us (level)
    pallas_call x10 -> x9, Pallas kernels: 4.36 us -> 4.31 us  [kernel_call(): pl.pallas_call(body, out_shape=outs, in_specs=[spec] * len(args), out_spe...]
where the time goes in v9:
time: 70.6 us; the launch traced here: 70.4 us
  blocking collectives  38.1 us (54%)
  starting transfers between devices  14.4 us (20%)
  waiting for transfers between devices  11 us (16%)
  Pallas kernels  6.01 us (9%)
  between operations  0.76 us (1%)
    all_to_all x3, blocking collectives, all_to_all(): lax.all_to_all(value, axes, 0, 0, axis_index_groups=groups, tiled=True)  38.1 us
    ppermute x4, waiting for transfers between devices, shards(): mine = mine + lax.ppermute(mine, REPLICA, pairs)  9.28 us
    ppermute x4, starting transfers between devices, shards(): mine = mine + lax.ppermute(mine, REPLICA, pairs)  7.56 us
    ppermute x4, starting transfers between devices, swapped(): return lax.ppermute(value, 'core', [(0, 1), (1, 0)])  6.87 us
    pallas_call x9, Pallas kernels, kernel_call(): pl.pallas_call(body, out_shape=outs, in_specs=[spec] * len(args), out_spe...  4.31 us
    pallas_call x1, Pallas kernels, shards(): pl.pallas_call(first_body, out_shape=[lefts, jax.ShapeDtypeStruct(grads.s...  1.7 us
    ppermute x4, waiting for transfers between devices, swapped(): return lax.ppermute(value, 'core', [(0, 1), (1, 0)])  1.68 us
  transfers between devices with their start and end apart: 8, of which 6 were waited for; matrix products, arithmetic and copies ran while one was open for 0% of the time, Pallas kernels for 4%

profile of v9, /device:TPU:1, one launch (start us, length us, event | category | flops | bytes accessed | tf_op | source)
XLA Modules:
  0.0 70.4 jit_solution(909620523559661865)
XLA Ops:
  0.6 1.7 %shard_map.67 = (f32[16,8,128]{2,1,0:T(8,128)S(1)}, bf16[2,512,1024]{2,1,0:T(8,128)(2,1)S(1)}, f32[2,32,1024]{2,1,0:T(8,128)S(1)}) custom-call(f32[2,32,1024]{2,1,0:T(8,128)} %bitcast.23, bf16[2,512,1024]{2,1,0:T(8,128)(2,1)} %bitcast.22), custom_call_target="tpu_custom_call" | custom-call | flops 1048576 | bytes 262144 | tf_op jit(solution)/shard_map/pallas_call | solution.py:336
  2.3 3.3 %collective-permute-start = (f32[16,8,128]{2,1,0:T(8,128)S(1)}, f32[16,8,128]{2,1,0:T(8,128)S(1)}, u32[]{:S(2)}, u32[]{:S(2)}) collective-permute-start(f32[16,8,128]{2,1,0:T(8,128)S(1)} %get-tuple-element.24), channel_id=1, source_target_pairs={{0,8},{8,0},{1,9},{9,1},{2,10},{10,2},{3,11},{11,3},{4,12},{12,4},... | collective-permute-start | bytes 196616 | tf_op jit(solution)/shard_map/ppermute | solution.py:316
  5.6 0.4 shard_map.68
  6.0 0.5 collective-permute-done
  6.5 0.1 collective-permute-start.1
  6.6 3.1 %collective-permute-done.1 = f32[16,8,128]{2,1,0:T(8,128)S(1)} collective-permute-done((f32[16,8,128]{2,1,0:T(8,128)S(1)}, f32[16,8,128]{2,1,0:T(8,128)S(1)}, u32[]{:S(2)}, u32[]{:S(2)}) %collective-permute-start.1) | collective-permute-done | bytes 65568 | tf_op jit(solution)/shard_map/ppermute | solution.py:349
  9.8 2.5 %collective-permute-start.2 = (f32[16,8,128]{2,1,0:T(8,128)S(1)}, f32[16,8,128]{2,1,0:T(8,128)S(1)}, u32[]{:S(2)}, u32[]{:S(2)}) collective-permute-start(f32[16,8,128]{2,1,0:T(8,128)S(1)} %add.16), channel_id=1, source_target_pairs={{0,56},{8,48},{16,40},{24,32},{32,24},{40,16},{48,8},{56,0},{64,12... | collective-permute-start | bytes 196616 | tf_op jit(solution)/shard_map/ppermute | solution.py:349
  12.3 2.5 %collective-permute-done.2 = f32[16,8,128]{2,1,0:T(8,128)S(1)} collective-permute-done((f32[16,8,128]{2,1,0:T(8,128)S(1)}, f32[16,8,128]{2,1,0:T(8,128)S(1)}, u32[]{:S(2)}, u32[]{:S(2)}) %collective-permute-start.2) | collective-permute-done | bytes 65568 | tf_op jit(solution)/shard_map/ppermute | solution.py:349
  14.8 1.7 %collective-permute-start.3 = (f32[16,8,128]{2,1,0:T(8,128)S(1)}, f32[16,8,128]{2,1,0:T(8,128)S(1)}, u32[]{:S(2)}, u32[]{:S(2)}) collective-permute-start(f32[16,8,128]{2,1,0:T(8,128)S(1)} %add.17), channel_id=1, source_target_pairs={{0,72},{8,64},{16,88},{24,80},{32,104},{40,96},{48,120},{56,112},{... | collective-permute-start | bytes 196616 | tf_op jit(solution)/shard_map/ppermute | solution.py:349
  16.5 2.0 %collective-permute-done.3 = f32[16,8,128]{2,1,0:T(8,128)S(1)} collective-permute-done((f32[16,8,128]{2,1,0:T(8,128)S(1)}, f32[16,8,128]{2,1,0:T(8,128)S(1)}, u32[]{:S(2)}, u32[]{:S(2)}) %collective-permute-start.3) | collective-permute-done | bytes 65568 | tf_op jit(solution)/shard_map/ppermute | solution.py:349
  18.5 3.2 %collective-permute-start.4 = (f32[16,8,128]{2,1,0:T(8,128)S(1)}, f32[16,8,128]{2,1,0:T(8,128)S(1)}, u32[]{:S(2)}, u32[]{:S(2)}) collective-permute-start(f32[16,8,128]{2,1,0:T(8,128)S(1)} %add.18), channel_id=1, source_target_pairs={{0,128},{8,136},{16,144},{24,152},{32,160},{40,168},{48,176},{56,1... | collective-permute-start | bytes 196616 | tf_op jit(solution)/shard_map/ppermute | solution.py:349
  21.8 1.7 %collective-permute-done.4 = f32[16,8,128]{2,1,0:T(8,128)S(1)} collective-permute-done((f32[16,8,128]{2,1,0:T(8,128)S(1)}, f32[16,8,128]{2,1,0:T(8,128)S(1)}, u32[]{:S(2)}, u32[]{:S(2)}) %collective-permute-start.4) | collective-permute-done | bytes 65568 | tf_op jit(solution)/shard_map/ppermute | solution.py:349
  23.4 0.5 shard_map.69
  23.9 0.0 copy-start
  23.9 0.0 copy-start.1
  24.0 3.4 %collective-permute-start.6 = (f32[16,16,128]{2,1,0:T(8,128)S(1)}, f32[16,16,128]{2,1,0:T(8,128)S(1)}, u32[]{:S(2)}, u32[]{:S(2)}) collective-permute-start(f32[16,16,128]{2,1,0:T(8,128)S(1)} %get-tuple-element.27), channel_id=1, source_target_pairs={{0,8},{8,0},{1,9},{9,1},{2,10},{10,2},{3,11},{11,3},{4,12},{12,4},... | collective-permute-start | bytes 393224 | tf_op jit(solution)/shard_map/ppermute | solution.py:316
  27.3 0.1 collective-permute-start.5
  27.4 1.2 %collective-permute-done.5.left_ref.other_ref = f32[16,8,128]{2,1,0:T(8,128)S(1)} collective-permute-done((f32[16,8,128]{2,1,0:T(8,128)S(1)}, f32[16,8,128]{2,1,0:T(8,128)S(1)}, u32[]{:S(2)}, u32[]{:S(2)}) %collective-permute-start.5) | collective-permute-done | bytes 65568 | tf_op jit(solution)/shard_map/ppermute | solution.py:316
  28.6 0.5 shard_map.70
  29.1 0.0 collective-permute-done.6.other_ref
  29.1 13.6 %all_to_all.15 = f32[80,4,128]{2,1,0:T(4,128)S(1)} all-to-all(f32[80,4,128]{2,1,0:T(4,128)S(1)} %bitcast.12), channel_id=1, replica_groups={{0,1,2,3,16,17,18,19,40,41,42,43,56,57,58,59},{8,9,10,11,24,25,26,27,32..., dimensions={0} | all-to-all | bytes 327680 | tf_op jit(solution)/shard_map/all_to_all | solution.py:324
  42.7 11.3 %all_to_all.16 = f32[40,4,128]{2,1,0:T(4,128)S(1)} all-to-all(f32[40,4,128]{2,1,0:T(4,128)S(1)} %bitcast.21), channel_id=1, replica_groups={{0,12,68,72,128,140,196,200},{4,8,64,76,132,136,192,204},{1,13,69,73,12..., dimensions={0} | all-to-all | bytes 163840 | tf_op jit(solution)/shard_map/all_to_all | solution.py:324
  54.0 13.3 %all_to_all.17 = f32[16,16,128]{2,1,0:T(8,128)S(1)} all-to-all(f32[16,16,128]{2,1,0:T(8,128)S(1)} %get-tuple-element.29), channel_id=1, replica_groups={{0,1,2,3,16,17,18,19,40,41,42,43,56,57,58,59},{8,9,10,11,24,25,26,27,32..., dimensions={0} | all-to-all | bytes 262144 | tf_op jit(solution)/shard_map/all_to_all | solution.py:324
  67.3 0.1 collective-permute-start.7
  67.4 1.0 %shard_map.74 = (f32[32,128]{1,0:T(8,128)S(1)}, f32[2,32,512]{2,1,0:T(8,128)S(1)}) custom-call(f32[16,128]{1,0:T(8,128)S(1)} %get-tuple-element.32.gram_ref, f32[16,8,128]{2,1,0:T(8,128)S(1)} %add.19.left_ref.mine_ref, f32[16,8,128]{2,1,0:T(8,128)S(1)} %collective-permute-done.5.left_ref.other_ref), custom_call_target="tpu_custom_call" | custom-call | flops 1048576 | bytes 262144 | tf_op jit(solution)/shard_map/pallas_call | solution.py:30
  68.5 0.0 copy-done
  68.5 0.0 copy-done.1
  68.5 0.5 shard_map.75
  69.1 0.0 collective-permute-done.7.right_ref
  69.1 1.3 %shard_map.76 = (f32[2,32,1024]{2,1,0:T(8,128)}, f32[2,32,512]{2,1,0:T(8,128)}, f32[2,32,512]{2,1,0:T(8,128)}) custom-call(f32[32,8,128]{2,1,0:T(8,128)S(1)} %collective-permute-done.7.right_ref, f32[32,128]{1,0:T(8,128)S(1)} %get-tuple-element.33.inverse_ref, f32[2,32,512]{2,1,0:T(8,128)S(1)} %get-tuple-element.34.frame_ref, f32[2,32,512]{2,1,0:T(8,128)S(1)} %bitcast.15, ...), custom_call_target="tpu_custom_call" | custom-call | flops 1048576 | bytes 262144 | tf_op jit(solution)/shard_map/pallas_call | solution.py:30
  (8 shorter events, 0.1 us)
Async XLA Ops:
  2.3 4.2 %collective-permute-start = (f32[16,8,128]{2,1,0:T(8,128)S(1)}, f32[16,8,128]{2,1,0:T(8,128)S(1)}, u32[]{:S(2)}, u32[]{:S(2)}) collective-permute-start(f32[16,8,128]{2,1,0:T(8,128)S(1)} %get-tuple-element.24), channel_id=1, source_target_pairs={{0,8},{8,0},{1,9},{9,1},{2,10},{10,2},{3,11},{11,3},{4,12},{12,4},... | collective-permute-start | bytes 196616 | tf_op jit(solution)/shard_map/ppermute | solution.py:316
  6.5 3.2 %collective-permute-start.1 = (f32[16,8,128]{2,1,0:T(8,128)S(1)}, f32[16,8,128]{2,1,0:T(8,128)S(1)}, u32[]{:S(2)}, u32[]{:S(2)}) collective-permute-start(f32[16,8,128]{2,1,0:T(8,128)S(1)} %add.15), channel_id=1, source_target_pairs={{0,16},{8,24},{16,0},{24,8},{32,48},{40,56},{48,32},{56,40},{64,80... | collective-permute-start | bytes 196616 | tf_op jit(solution)/shard_map/ppermute | solution.py:349
  9.8 5.0 %collective-permute-start.2 = (f32[16,8,128]{2,1,0:T(8,128)S(1)}, f32[16,8,128]{2,1,0:T(8,128)S(1)}, u32[]{:S(2)}, u32[]{:S(2)}) collective-permute-start(f32[16,8,128]{2,1,0:T(8,128)S(1)} %add.16), channel_id=1, source_target_pairs={{0,56},{8,48},{16,40},{24,32},{32,24},{40,16},{48,8},{56,0},{64,12... | collective-permute-start | bytes 196616 | tf_op jit(solution)/shard_map/ppermute | solution.py:349
  14.8 3.8 %collective-permute-start.3 = (f32[16,8,128]{2,1,0:T(8,128)S(1)}, f32[16,8,128]{2,1,0:T(8,128)S(1)}, u32[]{:S(2)}, u32[]{:S(2)}) collective-permute-start(f32[16,8,128]{2,1,0:T(8,128)S(1)} %add.17), channel_id=1, source_target_pairs={{0,72},{8,64},{16,88},{24,80},{32,104},{40,96},{48,120},{56,112},{... | collective-permute-start | bytes 196616 | tf_op jit(solution)/shard_map/ppermute | solution.py:349
  18.5 4.9 %collective-permute-start.4 = (f32[16,8,128]{2,1,0:T(8,128)S(1)}, f32[16,8,128]{2,1,0:T(8,128)S(1)}, u32[]{:S(2)}, u32[]{:S(2)}) collective-permute-start(f32[16,8,128]{2,1,0:T(8,128)S(1)} %add.18), channel_id=1, source_target_pairs={{0,128},{8,136},{16,144},{24,152},{32,160},{40,168},{48,176},{56,1... | collective-permute-start | bytes 196616 | tf_op jit(solution)/shard_map/ppermute | solution.py:349
  23.9 44.6 %copy-start = (f32[2,512,32]{1,2,0:T(8,128)S(1)}, f32[2,512,32]{1,2,0:T(8,128)}, u32[]{:S(2)}) copy-start(f32[2,512,32]{1,2,0:T(8,128)} %param.6) | copy-start | bytes 393220
  23.9 44.6 %copy-start.1 = (f32[2,512,32]{1,2,0:T(8,128)S(1)}, f32[2,512,32]{1,2,0:T(8,128)}, u32[]{:S(2)}) copy-start(f32[2,512,32]{1,2,0:T(8,128)} %param.7) | copy-start | bytes 393220
  24.0 5.1 %collective-permute-start.6 = (f32[16,16,128]{2,1,0:T(8,128)S(1)}, f32[16,16,128]{2,1,0:T(8,128)S(1)}, u32[]{:S(2)}, u32[]{:S(2)}) collective-permute-start(f32[16,16,128]{2,1,0:T(8,128)S(1)} %get-tuple-element.27), channel_id=1, source_target_pairs={{0,8},{8,0},{1,9},{9,1},{2,10},{10,2},{3,11},{11,3},{4,12},{12,4},... | collective-permute-start | bytes 393224 | tf_op jit(solution)/shard_map/ppermute | solution.py:316
  27.3 1.3 %collective-permute-start.5 = (f32[16,8,128]{2,1,0:T(8,128)S(1)}, f32[16,8,128]{2,1,0:T(8,128)S(1)}, u32[]{:S(2)}, u32[]{:S(2)}) collective-permute-start(f32[16,8,128]{2,1,0:T(8,128)S(1)} %add.19.left_ref.mine_ref), channel_id=1, source_target_pairs={{0,8},{8,0},{1,9},{9,1},{2,10},{10,2},{3,11},{11,3},{4,12},{12,4},... | collective-permute-start | bytes 196616 | tf_op jit(solution)/shard_map/ppermute | solution.py:316
  67.3 1.7 %collective-permute-start.7 = (f32[32,8,128]{2,1,0:T(8,128)S(1)}, f32[32,8,128]{2,1,0:T(8,128)S(1)}, u32[]{:S(2)}, u32[]{:S(2)}) collective-permute-start(f32[32,8,128]{2,1,0:T(8,128)S(1)} %bitcast.18), channel_id=1, source_target_pairs={{0,8},{8,0},{1,9},{9,1},{2,10},{10,2},{3,11},{11,3},{4,12},{12,4},... | collective-permute-start | bytes 393224 | tf_op jit(solution)/shard_map/ppermute | solution.py:316

commit v10 on v9

--- a/solution.py
+++ b/solution.py
@@ -152,12 +152,6 @@
     share_ref[...] = picked([packed[4 * s : 4 * s + 4] for s in range(4)], lax.axis_index("y"))
 
 
-def by_layer(mine_ref, other_ref):
-    mine, other = joined(mine_ref, 4, 4), joined(other_ref, 4, 4)
-    first = held() == 0
-    return jnp.where(first, mine, other), jnp.where(first, other, mine)
-
-
 def picked(values, index):
     out = values[0]
     for s in range(1, len(values)):
@@ -201,8 +195,7 @@
         gram_ref[4 * q : 4 * q + 4] = in_ref[at : at + 4] + in_ref[at + CHUNK : at + CHUNK + 4]
 
 
-def factor_body(gram_ref, mine_ref, other_ref, inverse_ref, frame_ref):
-    packed = gram_ref[...]
+def inverse_factors(packed):
     turned = pltpu.roll(packed, 64, 1)
     grams = [packed[0:8], packed[8:16], turned[0:8], turned[8:16]]
     shape = (8, LANES)
@@ -239,74 +232,105 @@
                 for j in ahead:
                     columns[j][r] = columns[j][r] - factor * ahead[j]
             work[at] = jnp.where(row == s, work[at] * lax.rsqrt(pivot), work[at])
-    inverse = pltpu.roll(jnp.concatenate(work, axis=0), 64, 1)
-    inverse_ref[...] = inverse
-    left = by_layer(mine_ref, other_ref)
-    for l in range(2):
-        frame_ref[l] = (
-            jnp.dot(
-                inverse[:, l * RANK : (l + 1) * RANK],
-                left[l],
-                precision=EXACT,
-                preferred_element_type=jnp.float32,
-            )
-            * (1.0 / REPLICAS)
-        )
-
-
-def settle(layer, right_ref, inverse_ref, frame_ref, weights_ref, momentum_ref):
+    return pltpu.roll(jnp.concatenate(work, axis=0), 64, 1)
+
+
+def settled(layer, right_ref, inverse, left_ref, weights_ref, momentum_ref):
     place = (lax.axis_index("zlo") * 4 + lax.axis_index("y")) * 2 + core()
     block = place // 4
     shift = (4 - place % 4) * 32
-    square = jnp.zeros((8, LANES), jnp.float32)
+    own = jnp.concatenate([right_ref[8 * t + block] for t in range(4)], axis=0)
+    own = pltpu.roll(own, shift, 1)[:, :RANK]
+    inverse = jnp.where(layer == 0, inverse[:, :RANK], inverse[:, RANK : 2 * RANK])
+    half = jnp.dot(inverse, own, precision=EXACT, preferred_element_type=jnp.float32)
+    columns = (((0,), (0,)), ((), ()))
+    mixed = lax.dot_general(
+        inverse, half, columns, precision=EXACT, preferred_element_type=jnp.float32
+    )
+    change = lax.dot_general(
+        mixed,
+        joined(left_ref, 4, 4),
+        columns,
+        precision=EXACT,
+        preferred_element_type=jnp.float32,
+    )
+    new = 0.9 * momentum_ref[layer] + change * (1.0 / REPLICAS)
+    return new, weights_ref[layer] - 0.02 * new
+
+
+def scale_of(right_ref):
+    squares = [jnp.zeros((8, LANES), jnp.float32)] * 4
     for i in range(32):
         tile = right_ref[i]
-        square = square + tile * tile
-    scale = lax.rsqrt(jnp.sum(square) * (1.0 / (RANK * 1024)) + 1e-12)
-    own = jnp.concatenate([right_ref[8 * t + block] for t in range(4)], axis=0)
-    inverse = inverse_ref[...]
-    inverse = jnp.where(layer == 0, inverse[:, :RANK], inverse[:, RANK : 2 * RANK])
-    half = jnp.dot(inverse, own, precision=EXACT, preferred_element_type=jnp.float32)
-    half = pltpu.roll(half, shift, 1)[:, :RANK]
-    change = lax.dot_general(
-        half,
-        frame_ref[layer],
-        (((0,), (0,)), ((), ())),
-        precision=EXACT,
-        preferred_element_type=jnp.float32,
-    )
-    new = 0.9 * momentum_ref[layer] + change
-    return scale, new, weights_ref[layer] - 0.02 * new
-
-
-def scaled(right_ref, scale, basis_ref, layer):
+        squares[i % 4] = squares[i % 4] + tile * tile
+    square = (squares[0] + squares[1]) + (squares[2] + squares[3])
+    return lax.rsqrt(jnp.sum(square) * (1.0 / (RANK * 1024)) + 1e-12)
+
+
+def put_scaled(right_ref, scale, t, basis_ref):
+    for j in range(8):
+        at = (slice(8 * t, 8 * t + 8), slice(LANES * j, LANES * j + LANES))
+        basis_ref[at] = right_ref[8 * t + j] * scale
+
+
+def early_body(
+    gram_ref, right_ref, left_ref, weights_ref, momentum_ref, inverse_ref, basis_ref, w_ref, m_ref
+):
+    inverse = inverse_factors(gram_ref[...])
+    inverse_ref[...] = inverse
+    scale = scale_of(right_ref)
     for t in range(4):
-        for j in range(8):
-            at = (slice(8 * t, 8 * t + 8), slice(LANES * j, LANES * j + LANES))
-            at = at if layer is None else (layer, *at)
-            basis_ref[at] = right_ref[8 * t + j] * scale
-
-
-def early_body(right_ref, inverse_ref, frame_ref, weights_ref, momentum_ref, basis_ref, w_ref, m_ref):
-    scale, new, weights = settle(owned(), right_ref, inverse_ref, frame_ref, weights_ref, momentum_ref)
-    scaled(right_ref, scale, basis_ref, None)
-    m_ref[...] = new
-    w_ref[...] = weights
+        put_scaled(right_ref, scale, t, basis_ref)
+    m_ref[...], w_ref[...] = settled(
+        owned(), right_ref, inverse, left_ref, weights_ref, momentum_ref
+    )
 
 
 def late_body(
-    right_ref, inverse_ref, frame_ref, weights_ref, momentum_ref, b_ref, w_ref, m_ref,
-    basis_ref, new_w_ref, new_m_ref,
+    right_ref, left_ref, weights_ref, momentum_ref, inverse_ref, b_ref, w_ref, m_ref,
+    basis_hbm, w_hbm, m_hbm, basis_ref, new_w_ref, new_m_ref, sems,
 ):
-    c = owned()
-    basis_ref[c] = b_ref[...]
-    new_w_ref[c] = w_ref[...]
-    new_m_ref[c] = m_ref[...]
-    layer = 1 - c
-    scale, new, weights = settle(layer, right_ref, inverse_ref, frame_ref, weights_ref, momentum_ref)
-    scaled(right_ref, scale, basis_ref, layer)
-    new_m_ref[layer] = new
-    new_w_ref[layer] = weights
+    layer = held()
+    copies = []
+
+    def send(source, target):
+        copies.append(pltpu.make_async_copy(source, target, sems.at[len(copies)]))
+        copies[-1].start()
+
+    send(b_ref, basis_hbm.at[1 - layer])
+    send(w_ref, w_hbm.at[1 - layer])
+    send(m_ref, m_hbm.at[1 - layer])
+    new, weights = settled(
+        layer, right_ref, inverse_ref[...], left_ref, weights_ref, momentum_ref
+    )
+    scale = scale_of(right_ref)
+    for t in range(4):
+        put_scaled(right_ref, scale, t, basis_ref)
+        rows = slice(8 * t, 8 * t + 8)
+        send(basis_ref.at[rows], basis_hbm.at[layer, rows])
+    new_m_ref[...] = new
+    send(new_m_ref, m_hbm.at[layer])
+    new_w_ref[...] = weights
+    send(new_w_ref, w_hbm.at[layer])
+    for copy in copies:
+        copy.wait()
+
+
+def last(right, left, weights, momentum, early):
+    local, far = pl.BlockSpec(memory_space=pltpu.VMEM), pl.BlockSpec(memory_space=pltpu.HBM)
+    shapes = [early[1].shape, early[2].shape, early[3].shape]
+    return pl.pallas_call(
+        late_body,
+        out_shape=[f32(2, *shape) for shape in shapes],
+        in_specs=[local] * 8,
+        out_specs=[far] * 3,
+        scratch_shapes=[
+            *(pltpu.VMEM(shape, jnp.float32) for shape in shapes),
+            pltpu.SemaphoreType.DMA((9,)),
+        ],
+        compiler_params=pltpu.CompilerParams(vmem_limit_bytes=VMEM_LIMIT),
+        cost_estimate=pl.CostEstimate(flops=1 << 20, bytes_accessed=1 << 18, transcendentals=0),
+    )(right, left, weights, momentum, *early)
 
 
 DOUBLING = ((1, 0), (3, 1), (4, 1), (8, 0))
@@ -326,7 +350,7 @@
 
 def shards(layer_grads, last_basis, layer_weights, momentum):
     grads = layer_grads[0]
-    layers, rows, width = grads.shape
+    _, rows, width = grads.shape
     basis = jnp.swapaxes(last_basis, 1, 2)
     weights, momentum = jnp.swapaxes(layer_weights, 1, 2), jnp.swapaxes(momentum, 1, 2)
     lefts, rights = f32(PEERS, 8, LANES), f32(PEERS, 16, LANES)
@@ -360,17 +384,10 @@
     right = all_to_all(sent, PLANE)
     right, gram = lax.optimization_barrier((right.reshape(32, 8, LANES), gram))
     late = swapped(right)
-    inverse, frame = kernel_call(factor_body, [f32(RANK, LANES), f32(layers, RANK, rows)])(
-        gram, mine, other
-    )
-    solved = (inverse, frame, weights, momentum)
     early = kernel_call(
-        early_body, [f32(RANK, width), f32(RANK, rows), f32(RANK, rows)]
-    )(right, *solved)
-    new_basis, new_weights, new_momentum = kernel_call(
-        late_body,
-        [f32(layers, RANK, width), f32(layers, RANK, rows), f32(layers, RANK, rows)],
-    )(late, *solved, *early)
+        early_body, [f32(RANK, LANES), f32(RANK, width), f32(RANK, rows), f32(RANK, rows)]
+    )(gram, right, other, weights, momentum)
+    new_basis, new_weights, new_momentum = last(late, mine, weights, momentum, early)
     return tuple(jnp.swapaxes(a, 1, 2) for a in (new_weights, new_basis, new_momentum))
 
 

time: 70.6 us -> 70.5 us (level)
    pallas_call x9 -> x7, Pallas kernels: 4.31 us -> 2.87 us  [kernel_call(): pl.pallas_call(body, out_shape=outs, in_specs=[spec] * len(args), out_spe...]
    pallas_call x0 -> x1, Pallas kernels: none -> 1.4 us  [last(): pl.pallas_call(late_body, out_shape=[f32(2, *shape) for shape in shapes],...]
  transfers between devices with their start and end apart: 8 -> 8, of which waited for: 6 -> 6; matrix products, arithmetic and copies ran while one was open for 0% -> 0% of each run, Pallas kernels for 4% -> 3%
where the time goes in v10:
time: 70.5 us; the launch traced here: 70.3 us
  blocking collectives  38.1 us (54%)
  starting transfers between devices  14.4 us (20%)
  waiting for transfers between devices  11 us (16%)
  Pallas kernels  5.96 us (8%)
  between operations  0.74 us (1%)
    all_to_all x3, blocking collectives, all_to_all(): lax.all_to_all(value, axes, 0, 0, axis_index_groups=groups, tiled=True)  38.1 us
    ppermute x4, waiting for transfers between devices, shards(): mine = mine + lax.ppermute(mine, REPLICA, pairs)  9.28 us
    ppermute x4, starting transfers between devices, shards(): mine = mine + lax.ppermute(mine, REPLICA, pairs)  7.56 us
    ppermute x4, starting transfers between devices, swapped(): return lax.ppermute(value, 'core', [(0, 1), (1, 0)])  6.87 us
    pallas_call x7, Pallas kernels, kernel_call(): pl.pallas_call(body, out_shape=outs, in_specs=[spec] * len(args), out_spe...  2.87 us
    pallas_call x1, Pallas kernels, shards(): pl.pallas_call(first_body, out_shape=[lefts, jax.ShapeDtypeStruct(grads.s...  1.7 us
    ppermute x4, waiting for transfers between devices, swapped(): return lax.ppermute(value, 'core', [(0, 1), (1, 0)])  1.68 us
  transfers between devices with their start and end apart: 8, of which 6 were waited for; matrix products, arithmetic and copies ran while one was open for 0% of the time, Pallas kernels for 3%

profile of v10, /device:TPU:1, one launch (start us, length us, event | category | flops | bytes accessed | tf_op | source)
XLA Modules:
  0.0 70.3 jit_solution(16288661583777030703)
XLA Ops:
  0.6 1.7 %shard_map.67 = (f32[16,8,128]{2,1,0:T(8,128)S(1)}, bf16[2,512,1024]{2,1,0:T(8,128)(2,1)S(1)}, f32[2,32,1024]{2,1,0:T(8,128)S(1)}) custom-call(f32[2,32,1024]{2,1,0:T(8,128)} %bitcast.23, bf16[2,512,1024]{2,1,0:T(8,128)(2,1)} %bitcast.22), custom_call_target="tpu_custom_call" | custom-call | flops 1048576 | bytes 262144 | tf_op jit(solution)/shard_map/pallas_call | solution.py:360
  2.3 3.3 %collective-permute-start = (f32[16,8,128]{2,1,0:T(8,128)S(1)}, f32[16,8,128]{2,1,0:T(8,128)S(1)}, u32[]{:S(2)}, u32[]{:S(2)}) collective-permute-start(f32[16,8,128]{2,1,0:T(8,128)S(1)} %get-tuple-element.23), channel_id=1, source_target_pairs={{0,8},{8,0},{1,9},{9,1},{2,10},{10,2},{3,11},{11,3},{4,12},{12,4},... | collective-permute-start | bytes 196616 | tf_op jit(solution)/shard_map/ppermute | solution.py:340
  5.6 0.4 shard_map.68
  6.0 0.5 collective-permute-done
  6.5 0.1 collective-permute-start.1
  6.6 3.1 %collective-permute-done.1 = f32[16,8,128]{2,1,0:T(8,128)S(1)} collective-permute-done((f32[16,8,128]{2,1,0:T(8,128)S(1)}, f32[16,8,128]{2,1,0:T(8,128)S(1)}, u32[]{:S(2)}, u32[]{:S(2)}) %collective-permute-start.1) | collective-permute-done | bytes 65568 | tf_op jit(solution)/shard_map/ppermute | solution.py:373
  9.8 2.5 %collective-permute-start.2 = (f32[16,8,128]{2,1,0:T(8,128)S(1)}, f32[16,8,128]{2,1,0:T(8,128)S(1)}, u32[]{:S(2)}, u32[]{:S(2)}) collective-permute-start(f32[16,8,128]{2,1,0:T(8,128)S(1)} %add.16), channel_id=1, source_target_pairs={{0,56},{8,48},{16,40},{24,32},{32,24},{40,16},{48,8},{56,0},{64,12... | collective-permute-start | bytes 196616 | tf_op jit(solution)/shard_map/ppermute | solution.py:373
  12.3 2.5 %collective-permute-done.2 = f32[16,8,128]{2,1,0:T(8,128)S(1)} collective-permute-done((f32[16,8,128]{2,1,0:T(8,128)S(1)}, f32[16,8,128]{2,1,0:T(8,128)S(1)}, u32[]{:S(2)}, u32[]{:S(2)}) %collective-permute-start.2) | collective-permute-done | bytes 65568 | tf_op jit(solution)/shard_map/ppermute | solution.py:373
  14.8 1.7 %collective-permute-start.3 = (f32[16,8,128]{2,1,0:T(8,128)S(1)}, f32[16,8,128]{2,1,0:T(8,128)S(1)}, u32[]{:S(2)}, u32[]{:S(2)}) collective-permute-start(f32[16,8,128]{2,1,0:T(8,128)S(1)} %add.17), channel_id=1, source_target_pairs={{0,72},{8,64},{16,88},{24,80},{32,104},{40,96},{48,120},{56,112},{... | collective-permute-start | bytes 196616 | tf_op jit(solution)/shard_map/ppermute | solution.py:373
  16.5 2.0 %collective-permute-done.3 = f32[16,8,128]{2,1,0:T(8,128)S(1)} collective-permute-done((f32[16,8,128]{2,1,0:T(8,128)S(1)}, f32[16,8,128]{2,1,0:T(8,128)S(1)}, u32[]{:S(2)}, u32[]{:S(2)}) %collective-permute-start.3) | collective-permute-done | bytes 65568 | tf_op jit(solution)/shard_map/ppermute | solution.py:373
  18.5 3.2 %collective-permute-start.4 = (f32[16,8,128]{2,1,0:T(8,128)S(1)}, f32[16,8,128]{2,1,0:T(8,128)S(1)}, u32[]{:S(2)}, u32[]{:S(2)}) collective-permute-start(f32[16,8,128]{2,1,0:T(8,128)S(1)} %add.18), channel_id=1, source_target_pairs={{0,128},{8,136},{16,144},{24,152},{32,160},{40,168},{48,176},{56,1... | collective-permute-start | bytes 196616 | tf_op jit(solution)/shard_map/ppermute | solution.py:373
  21.8 1.7 %collective-permute-done.4 = f32[16,8,128]{2,1,0:T(8,128)S(1)} collective-permute-done((f32[16,8,128]{2,1,0:T(8,128)S(1)}, f32[16,8,128]{2,1,0:T(8,128)S(1)}, u32[]{:S(2)}, u32[]{:S(2)}) %collective-permute-start.4) | collective-permute-done | bytes 65568 | tf_op jit(solution)/shard_map/ppermute | solution.py:373
  23.4 0.5 shard_map.69
  23.9 0.0 copy-start
  23.9 0.0 copy-start.1
  24.0 3.4 %collective-permute-start.6 = (f32[16,16,128]{2,1,0:T(8,128)S(1)}, f32[16,16,128]{2,1,0:T(8,128)S(1)}, u32[]{:S(2)}, u32[]{:S(2)}) collective-permute-start(f32[16,16,128]{2,1,0:T(8,128)S(1)} %get-tuple-element.26), channel_id=1, source_target_pairs={{0,8},{8,0},{1,9},{9,1},{2,10},{10,2},{3,11},{11,3},{4,12},{12,4},... | collective-permute-start | bytes 393224 | tf_op jit(solution)/shard_map/ppermute | solution.py:340
  27.3 0.1 collective-permute-start.5
  27.4 1.2 %collective-permute-done.5.left_ref = f32[16,8,128]{2,1,0:T(8,128)S(1)} collective-permute-done((f32[16,8,128]{2,1,0:T(8,128)S(1)}, f32[16,8,128]{2,1,0:T(8,128)S(1)}, u32[]{:S(2)}, u32[]{:S(2)}) %collective-permute-start.5) | collective-permute-done | bytes 65568 | tf_op jit(solution)/shard_map/ppermute | solution.py:340
  28.6 0.5 shard_map.70
  29.1 0.0 collective-permute-done.6.other_ref
  29.1 13.6 %all_to_all.15 = f32[80,4,128]{2,1,0:T(4,128)S(1)} all-to-all(f32[80,4,128]{2,1,0:T(4,128)S(1)} %bitcast.12), channel_id=1, replica_groups={{0,1,2,3,16,17,18,19,40,41,42,43,56,57,58,59},{8,9,10,11,24,25,26,27,32..., dimensions={0} | all-to-all | bytes 327680 | tf_op jit(solution)/shard_map/all_to_all | solution.py:348
  42.7 11.3 %all_to_all.16 = f32[40,4,128]{2,1,0:T(4,128)S(1)} all-to-all(f32[40,4,128]{2,1,0:T(4,128)S(1)} %bitcast.21), channel_id=1, replica_groups={{0,12,68,72,128,140,196,200},{4,8,64,76,132,136,192,204},{1,13,69,73,12..., dimensions={0} | all-to-all | bytes 163840 | tf_op jit(solution)/shard_map/all_to_all | solution.py:348
  54.0 13.3 %all_to_all.17 = f32[16,16,128]{2,1,0:T(8,128)S(1)} all-to-all(f32[16,16,128]{2,1,0:T(8,128)S(1)} %get-tuple-element.28), channel_id=1, replica_groups={{0,1,2,3,16,17,18,19,40,41,42,43,56,57,58,59},{8,9,10,11,24,25,26,27,32..., dimensions={0} | all-to-all | bytes 262144 | tf_op jit(solution)/shard_map/all_to_all | solution.py:348
  67.3 0.1 collective-permute-start.7
  67.4 0.0 copy-done
  67.4 0.0 copy-done.1
  67.4 1.4 %shard_map.74 = (f32[32,128]{1,0:T(8,128)S(1)}, f32[32,1024]{1,0:T(8,128)S(1)}, f32[32,512]{1,0:T(8,128)S(1)}, f32[32,512]{1,0:T(8,128)S(1)}) custom-call(f32[16,128]{1,0:T(8,128)S(1)} %get-tuple-element.31.gram_ref, f32[32,8,128]{2,1,0:T(8,128)S(1)} %bitcast.15, f32[16,8,128]{2,1,0:T(8,128)S(1)} %collective-permute-done.5.left_ref, ...), custom_call_target="tpu_custom_call" | custom-call | flops 1048576 | bytes 262144 | tf_op jit(solution)/shard_map/pallas_call | solution.py:30
  68.9 0.0 collective-permute-done.7.right_ref
  68.9 1.4 %shard_map.75 = (f32[2,32,1024]{2,1,0:T(8,128)}, f32[2,32,512]{2,1,0:T(8,128)}, f32[2,32,512]{2,1,0:T(8,128)}) custom-call(f32[32,8,128]{2,1,0:T(8,128)S(1)} %collective-permute-done.7.right_ref, f32[16,8,128]{2,1,0:T(8,128)S(1)} %add.19.left_ref, f32[2,32,512]{2,1,0:T(8,128)S(1)} %bitcast.17, f32[2,32,512]{2,1,0:T(8,128)S(1)} %bitcast.19, ...), custom_call_target="tpu_custom_call" | custom-call | flops 1048576 | bytes 262144 | tf_op jit(solution)/shard_map/pallas_call | solution.py:322
  (8 shorter events, 0.1 us)
Async XLA Ops:
  2.3 4.2 %collective-permute-start = (f32[16,8,128]{2,1,0:T(8,128)S(1)}, f32[16,8,128]{2,1,0:T(8,128)S(1)}, u32[]{:S(2)}, u32[]{:S(2)}) collective-permute-start(f32[16,8,128]{2,1,0:T(8,128)S(1)} %get-tuple-element.23), channel_id=1, source_target_pairs={{0,8},{8,0},{1,9},{9,1},{2,10},{10,2},{3,11},{11,3},{4,12},{12,4},... | collective-permute-start | bytes 196616 | tf_op jit(solution)/shard_map/ppermute | solution.py:340
  6.5 3.2 %collective-permute-start.1 = (f32[16,8,128]{2,1,0:T(8,128)S(1)}, f32[16,8,128]{2,1,0:T(8,128)S(1)}, u32[]{:S(2)}, u32[]{:S(2)}) collective-permute-start(f32[16,8,128]{2,1,0:T(8,128)S(1)} %add.15), channel_id=1, source_target_pairs={{0,16},{8,24},{16,0},{24,8},{32,48},{40,56},{48,32},{56,40},{64,80... | collective-permute-start | bytes 196616 | tf_op jit(solution)/shard_map/ppermute | solution.py:373
  9.8 5.0 %collective-permute-start.2 = (f32[16,8,128]{2,1,0:T(8,128)S(1)}, f32[16,8,128]{2,1,0:T(8,128)S(1)}, u32[]{:S(2)}, u32[]{:S(2)}) collective-permute-start(f32[16,8,128]{2,1,0:T(8,128)S(1)} %add.16), channel_id=1, source_target_pairs={{0,56},{8,48},{16,40},{24,32},{32,24},{40,16},{48,8},{56,0},{64,12... | collective-permute-start | bytes 196616 | tf_op jit(solution)/shard_map/ppermute | solution.py:373
  14.8 3.8 %collective-permute-start.3 = (f32[16,8,128]{2,1,0:T(8,128)S(1)}, f32[16,8,128]{2,1,0:T(8,128)S(1)}, u32[]{:S(2)}, u32[]{:S(2)}) collective-permute-start(f32[16,8,128]{2,1,0:T(8,128)S(1)} %add.17), channel_id=1, source_target_pairs={{0,72},{8,64},{16,88},{24,80},{32,104},{40,96},{48,120},{56,112},{... | collective-permute-start | bytes 196616 | tf_op jit(solution)/shard_map/ppermute | solution.py:373
  18.5 4.9 %collective-permute-start.4 = (f32[16,8,128]{2,1,0:T(8,128)S(1)}, f32[16,8,128]{2,1,0:T(8,128)S(1)}, u32[]{:S(2)}, u32[]{:S(2)}) collective-permute-start(f32[16,8,128]{2,1,0:T(8,128)S(1)} %add.18), channel_id=1, source_target_pairs={{0,128},{8,136},{16,144},{24,152},{32,160},{40,168},{48,176},{56,1... | collective-permute-start | bytes 196616 | tf_op jit(solution)/shard_map/ppermute | solution.py:373
  23.9 43.5 %copy-start = (f32[2,512,32]{1,2,0:T(8,128)S(1)}, f32[2,512,32]{1,2,0:T(8,128)}, u32[]{:S(2)}) copy-start(f32[2,512,32]{1,2,0:T(8,128)} %param.6) | copy-start | bytes 393220
  23.9 43.5 %copy-start.1 = (f32[2,512,32]{1,2,0:T(8,128)S(1)}, f32[2,512,32]{1,2,0:T(8,128)}, u32[]{:S(2)}) copy-start(f32[2,512,32]{1,2,0:T(8,128)} %param.7) | copy-start | bytes 393220
  24.0 5.1 %collective-permute-start.6 = (f32[16,16,128]{2,1,0:T(8,128)S(1)}, f32[16,16,128]{2,1,0:T(8,128)S(1)}, u32[]{:S(2)}, u32[]{:S(2)}) collective-permute-start(f32[16,16,128]{2,1,0:T(8,128)S(1)} %get-tuple-element.26), channel_id=1, source_target_pairs={{0,8},{8,0},{1,9},{9,1},{2,10},{10,2},{3,11},{11,3},{4,12},{12,4},... | collective-permute-start | bytes 393224 | tf_op jit(solution)/shard_map/ppermute | solution.py:340
  27.3 1.3 %collective-permute-start.5 = (f32[16,8,128]{2,1,0:T(8,128)S(1)}, f32[16,8,128]{2,1,0:T(8,128)S(1)}, u32[]{:S(2)}, u32[]{:S(2)}) collective-permute-start(f32[16,8,128]{2,1,0:T(8,128)S(1)} %add.19.left_ref), channel_id=1, source_target_pairs={{0,8},{8,0},{1,9},{9,1},{2,10},{10,2},{3,11},{11,3},{4,12},{12,4},... | collective-permute-start | bytes 196616 | tf_op jit(solution)/shard_map/ppermute | solution.py:340
  67.3 1.6 %collective-permute-start.7 = (f32[32,8,128]{2,1,0:T(8,128)S(1)}, f32[32,8,128]{2,1,0:T(8,128)S(1)}, u32[]{:S(2)}, u32[]{:S(2)}) collective-permute-start(f32[32,8,128]{2,1,0:T(8,128)S(1)} %bitcast.14), channel_id=1, source_target_pairs={{0,8},{8,0},{1,9},{9,1},{2,10},{10,2},{3,11},{11,3},{4,12},{12,4},... | collective-permute-start | bytes 393224 | tf_op jit(solution)/shard_map/ppermute | solution.py:340

commit v11 on v10

--- a/solution.py
+++ b/solution.py
@@ -137,18 +137,16 @@
     return jnp.where(lane_of((16, LANES)) < 64, gram[:16], gram[16:])
 
 
-def sent_body(left_ref, grads_ref, out_ref, gram_ref):
-    left = joined(left_ref, 4, 4)
-    put_right(left, grads_ref[held()], out_ref)
-    gram_ref[...] = packed_gram(left)
-
-
-def kept_body(left_ref, grads_ref, gram_ref, out_ref, share_ref):
+def sent_body(left_ref, grads_ref, out_ref):
+    put_right(joined(left_ref, 4, 4), grads_ref[held()], out_ref)
+
+
+def kept_body(mine_ref, other_ref, grads_ref, out_ref, share_ref):
     layer = owned()
-    left = joined(left_ref, 4, 4)
+    left = joined(other_ref, 4, 4)
     put_right(left, grads_ref[layer], out_ref)
     group = lane_of((16, LANES)) // RANK % 2
-    packed = jnp.where(group == layer, packed_gram(left), gram_ref[...])
+    packed = jnp.where(group == layer, packed_gram(left), packed_gram(joined(mine_ref, 4, 4)))
     share_ref[...] = picked([packed[4 * s : 4 * s + 4] for s in range(4)], lax.axis_index("y"))
 
 
@@ -372,9 +370,9 @@
         pairs = [(2 * p + c, 2 * (p ^ flip) + (c ^ cross)) for p in range(16) for c in range(2)]
         mine = mine + lax.ppermute(mine, REPLICA, pairs)
     other = swapped(mine)
-    away, gram = kernel_call(sent_body, [rights, f32(16, LANES)])(mine, grads)
+    away = kernel_call(sent_body, rights)(mine, grads)
     away = swapped(away)
-    kept, share = kernel_call(kept_body, [rights, f32(4, LANES)])(other, grads, gram)
+    kept, share = kernel_call(kept_body, [rights, f32(4, LANES)])(mine, other, grads)
 
     sent = kernel_call(pack_body, f32(PEERS * CHUNK, LANES))(kept, away, share)
     came = all_to_all(sent.reshape(PEERS * CHUNK // 4, 4, LANES), PLANE)

time: 70.5 us -> 70.6 us (level)
  transfers between devices with their start and end apart: 8 -> 8, of which waited for: 6 -> 6; matrix products, arithmetic and copies ran while one was open for 0% -> 0% of each run, Pallas kernels for 3% -> 4%
where the time goes in v11:
time: 70.6 us; the launch traced here: 70.4 us
  blocking collectives  38.1 us (54%)
  starting transfers between devices  14.4 us (20%)
  waiting for transfers between devices  10.9 us (15%)
  Pallas kernels  6.08 us (9%)
  between operations  0.72 us (1%)
    all_to_all x3, blocking collectives, all_to_all(): lax.all_to_all(value, axes, 0, 0, axis_index_groups=groups, tiled=True)  38.1 us
    ppermute x4, waiting for transfers between devices, shards(): mine = mine + lax.ppermute(mine, REPLICA, pairs)  9.28 us
    ppermute x4, starting transfers between devices, shards(): mine = mine + lax.ppermute(mine, REPLICA, pairs)  7.56 us
    ppermute x4, starting transfers between devices, swapped(): return lax.ppermute(value, 'core', [(0, 1), (1, 0)])  6.87 us
    pallas_call x7, Pallas kernels, kernel_call(): pl.pallas_call(body, out_shape=outs, in_specs=[spec] * len(args), out_spe...  2.98 us
    pallas_call x1, Pallas kernels, shards(): pl.pallas_call(first_body, out_shape=[lefts, jax.ShapeDtypeStruct(grads.s...  1.7 us
    ppermute x4, waiting for transfers between devices, swapped(): return lax.ppermute(value, 'core', [(0, 1), (1, 0)])  1.67 us
  transfers between devices with their start and end apart: 8, of which 6 were waited for; matrix products, arithmetic and copies ran while one was open for 0% of the time, Pallas kernels for 4%

profile of v11, /device:TPU:1, one launch (start us, length us, event | category | flops | bytes accessed | tf_op | source)
XLA Modules:
  0.0 70.4 jit_solution(10878637172725819632)
XLA Ops:
  0.6 1.7 %shard_map.67 = (f32[16,8,128]{2,1,0:T(8,128)S(1)}, bf16[2,512,1024]{2,1,0:T(8,128)(2,1)S(1)}, f32[2,32,1024]{2,1,0:T(8,128)S(1)}) custom-call(f32[2,32,1024]{2,1,0:T(8,128)} %bitcast.23, bf16[2,512,1024]{2,1,0:T(8,128)(2,1)} %bitcast.22), custom_call_target="tpu_custom_call" | custom-call | flops 1048576 | bytes 262144 | tf_op jit(solution)/shard_map/pallas_call | solution.py:358
  2.3 3.3 %collective-permute-start = (f32[16,8,128]{2,1,0:T(8,128)S(1)}, f32[16,8,128]{2,1,0:T(8,128)S(1)}, u32[]{:S(2)}, u32[]{:S(2)}) collective-permute-start(f32[16,8,128]{2,1,0:T(8,128)S(1)} %get-tuple-element.21), channel_id=1, source_target_pairs={{0,8},{8,0},{1,9},{9,1},{2,10},{10,2},{3,11},{11,3},{4,12},{12,4},... | collective-permute-start | bytes 196616 | tf_op jit(solution)/shard_map/ppermute | solution.py:338
  5.6 0.4 shard_map.68
  6.0 0.5 collective-permute-done
  6.5 0.1 collective-permute-start.1
  6.6 3.1 %collective-permute-done.1 = f32[16,8,128]{2,1,0:T(8,128)S(1)} collective-permute-done((f32[16,8,128]{2,1,0:T(8,128)S(1)}, f32[16,8,128]{2,1,0:T(8,128)S(1)}, u32[]{:S(2)}, u32[]{:S(2)}) %collective-permute-start.1) | collective-permute-done | bytes 65568 | tf_op jit(solution)/shard_map/ppermute | solution.py:371
  9.8 2.5 %collective-permute-start.2 = (f32[16,8,128]{2,1,0:T(8,128)S(1)}, f32[16,8,128]{2,1,0:T(8,128)S(1)}, u32[]{:S(2)}, u32[]{:S(2)}) collective-permute-start(f32[16,8,128]{2,1,0:T(8,128)S(1)} %add.16), channel_id=1, source_target_pairs={{0,56},{8,48},{16,40},{24,32},{32,24},{40,16},{48,8},{56,0},{64,12... | collective-permute-start | bytes 196616 | tf_op jit(solution)/shard_map/ppermute | solution.py:371
  12.3 2.5 %collective-permute-done.2 = f32[16,8,128]{2,1,0:T(8,128)S(1)} collective-permute-done((f32[16,8,128]{2,1,0:T(8,128)S(1)}, f32[16,8,128]{2,1,0:T(8,128)S(1)}, u32[]{:S(2)}, u32[]{:S(2)}) %collective-permute-start.2) | collective-permute-done | bytes 65568 | tf_op jit(solution)/shard_map/ppermute | solution.py:371
  14.8 1.7 %collective-permute-start.3 = (f32[16,8,128]{2,1,0:T(8,128)S(1)}, f32[16,8,128]{2,1,0:T(8,128)S(1)}, u32[]{:S(2)}, u32[]{:S(2)}) collective-permute-start(f32[16,8,128]{2,1,0:T(8,128)S(1)} %add.17), channel_id=1, source_target_pairs={{0,72},{8,64},{16,88},{24,80},{32,104},{40,96},{48,120},{56,112},{... | collective-permute-start | bytes 196616 | tf_op jit(solution)/shard_map/ppermute | solution.py:371
  16.5 2.0 %collective-permute-done.3 = f32[16,8,128]{2,1,0:T(8,128)S(1)} collective-permute-done((f32[16,8,128]{2,1,0:T(8,128)S(1)}, f32[16,8,128]{2,1,0:T(8,128)S(1)}, u32[]{:S(2)}, u32[]{:S(2)}) %collective-permute-start.3) | collective-permute-done | bytes 65568 | tf_op jit(solution)/shard_map/ppermute | solution.py:371
  18.5 3.2 %collective-permute-start.4 = (f32[16,8,128]{2,1,0:T(8,128)S(1)}, f32[16,8,128]{2,1,0:T(8,128)S(1)}, u32[]{:S(2)}, u32[]{:S(2)}) collective-permute-start(f32[16,8,128]{2,1,0:T(8,128)S(1)} %add.18), channel_id=1, source_target_pairs={{0,128},{8,136},{16,144},{24,152},{32,160},{40,168},{48,176},{56,1... | collective-permute-start | bytes 196616 | tf_op jit(solution)/shard_map/ppermute | solution.py:371
  21.8 1.7 %collective-permute-done.4 = f32[16,8,128]{2,1,0:T(8,128)S(1)} collective-permute-done((f32[16,8,128]{2,1,0:T(8,128)S(1)}, f32[16,8,128]{2,1,0:T(8,128)S(1)}, u32[]{:S(2)}, u32[]{:S(2)}) %collective-permute-start.4) | collective-permute-done | bytes 65568 | tf_op jit(solution)/shard_map/ppermute | solution.py:371
  23.4 0.3 shard_map.70
  23.7 0.0 copy-start
  23.7 0.0 copy-start.1
  23.8 3.4 %collective-permute-start.6 = (f32[16,16,128]{2,1,0:T(8,128)S(1)}, f32[16,16,128]{2,1,0:T(8,128)S(1)}, u32[]{:S(2)}, u32[]{:S(2)}) collective-permute-start(f32[16,16,128]{2,1,0:T(8,128)S(1)} %shard_map.70), channel_id=1, source_target_pairs={{0,8},{8,0},{1,9},{9,1},{2,10},{10,2},{3,11},{11,3},{4,12},{12,4},... | collective-permute-start | bytes 393224 | tf_op jit(solution)/shard_map/ppermute | solution.py:338
  27.1 0.1 collective-permute-start.5
  27.2 1.2 %collective-permute-done.5.other_ref.left_ref = f32[16,8,128]{2,1,0:T(8,128)S(1)} collective-permute-done((f32[16,8,128]{2,1,0:T(8,128)S(1)}, f32[16,8,128]{2,1,0:T(8,128)S(1)}, u32[]{:S(2)}, u32[]{:S(2)}) %collective-permute-start.5) | collective-permute-done | bytes 65568 | tf_op jit(solution)/shard_map/ppermute | solution.py:338
  28.4 0.8 %shard_map.69 = (f32[16,16,128]{2,1,0:T(8,128)S(1)}, f32[4,128]{1,0:T(4,128)S(1)}) custom-call(f32[16,8,128]{2,1,0:T(8,128)S(1)} %add.19.mine_ref.left_ref, f32[16,8,128]{2,1,0:T(8,128)S(1)} %collective-permute-done.5.other_ref.left_ref, bf16[2,512,1024]{2,1,0:T(8,128)(2,1)S(1)} %get-tuple-element.20.grads_ref), custom_call_target="tpu_custom_call" | custom-call | flops 1048576 | bytes 262144 | tf_op jit(solution)/shard_map/pallas_call | solution.py:30
  29.2 0.0 collective-permute-done.6.other_ref
  29.2 13.6 %all_to_all.15 = f32[80,4,128]{2,1,0:T(4,128)S(1)} all-to-all(f32[80,4,128]{2,1,0:T(4,128)S(1)} %bitcast.12), channel_id=1, replica_groups={{0,1,2,3,16,17,18,19,40,41,42,43,56,57,58,59},{8,9,10,11,24,25,26,27,32..., dimensions={0} | all-to-all | bytes 327680 | tf_op jit(solution)/shard_map/all_to_all | solution.py:346
  42.8 11.3 %all_to_all.16 = f32[40,4,128]{2,1,0:T(4,128)S(1)} all-to-all(f32[40,4,128]{2,1,0:T(4,128)S(1)} %bitcast.21), channel_id=1, replica_groups={{0,12,68,72,128,140,196,200},{4,8,64,76,132,136,192,204},{1,13,69,73,12..., dimensions={0} | all-to-all | bytes 163840 | tf_op jit(solution)/shard_map/all_to_all | solution.py:346
  54.1 13.3 %all_to_all.17 = f32[16,16,128]{2,1,0:T(8,128)S(1)} all-to-all(f32[16,16,128]{2,1,0:T(8,128)S(1)} %get-tuple-element.24), channel_id=1, replica_groups={{0,1,2,3,16,17,18,19,40,41,42,43,56,57,58,59},{8,9,10,11,24,25,26,27,32..., dimensions={0} | all-to-all | bytes 262144 | tf_op jit(solution)/shard_map/all_to_all | solution.py:346
  67.4 0.1 collective-permute-start.7
  67.5 0.0 copy-done
  67.5 0.0 copy-done.1
  67.5 1.4 %shard_map.74 = (f32[32,128]{1,0:T(8,128)S(1)}, f32[32,1024]{1,0:T(8,128)S(1)}, f32[32,512]{1,0:T(8,128)S(1)}, f32[32,512]{1,0:T(8,128)S(1)}) custom-call(f32[16,128]{1,0:T(8,128)S(1)} %get-tuple-element.27.gram_ref, f32[32,8,128]{2,1,0:T(8,128)S(1)} %bitcast.15, f32[16,8,128]{2,1,0:T(8,128)S(1)} %collective-permute-done.5.other_ref.left_ref, ...), custom_call_target="tpu_custom_call" | custom-call | flops 1048576 | bytes 262144 | tf_op jit(solution)/shard_map/pallas_call | solution.py:30
  69.0 0.0 collective-permute-done.7.right_ref
  69.0 1.4 %shard_map.75 = (f32[2,32,1024]{2,1,0:T(8,128)}, f32[2,32,512]{2,1,0:T(8,128)}, f32[2,32,512]{2,1,0:T(8,128)}) custom-call(f32[32,8,128]{2,1,0:T(8,128)S(1)} %collective-permute-done.7.right_ref, f32[16,8,128]{2,1,0:T(8,128)S(1)} %add.19.mine_ref.left_ref, f32[2,32,512]{2,1,0:T(8,128)S(1)} %bitcast.17, f32[2,32,512]{2,1,0:T(8,128)S(1)} %bitcast.19, ...), custom_call_target="tpu_custom_call" | custom-call | flops 1048576 | bytes 262144 | tf_op jit(solution)/shard_map/pallas_call | solution.py:320
  (8 shorter events, 0.1 us)
Async XLA Ops:
  2.3 4.2 %collective-permute-start = (f32[16,8,128]{2,1,0:T(8,128)S(1)}, f32[16,8,128]{2,1,0:T(8,128)S(1)}, u32[]{:S(2)}, u32[]{:S(2)}) collective-permute-start(f32[16,8,128]{2,1,0:T(8,128)S(1)} %get-tuple-element.21), channel_id=1, source_target_pairs={{0,8},{8,0},{1,9},{9,1},{2,10},{10,2},{3,11},{11,3},{4,12},{12,4},... | collective-permute-start | bytes 196616 | tf_op jit(solution)/shard_map/ppermute | solution.py:338
  6.5 3.2 %collective-permute-start.1 = (f32[16,8,128]{2,1,0:T(8,128)S(1)}, f32[16,8,128]{2,1,0:T(8,128)S(1)}, u32[]{:S(2)}, u32[]{:S(2)}) collective-permute-start(f32[16,8,128]{2,1,0:T(8,128)S(1)} %add.15), channel_id=1, source_target_pairs={{0,16},{8,24},{16,0},{24,8},{32,48},{40,56},{48,32},{56,40},{64,80... | collective-permute-start | bytes 196616 | tf_op jit(solution)/shard_map/ppermute | solution.py:371
  9.8 5.0 %collective-permute-start.2 = (f32[16,8,128]{2,1,0:T(8,128)S(1)}, f32[16,8,128]{2,1,0:T(8,128)S(1)}, u32[]{:S(2)}, u32[]{:S(2)}) collective-permute-start(f32[16,8,128]{2,1,0:T(8,128)S(1)} %add.16), channel_id=1, source_target_pairs={{0,56},{8,48},{16,40},{24,32},{32,24},{40,16},{48,8},{56,0},{64,12... | collective-permute-start | bytes 196616 | tf_op jit(solution)/shard_map/ppermute | solution.py:371
  14.8 3.8 %collective-permute-start.3 = (f32[16,8,128]{2,1,0:T(8,128)S(1)}, f32[16,8,128]{2,1,0:T(8,128)S(1)}, u32[]{:S(2)}, u32[]{:S(2)}) collective-permute-start(f32[16,8,128]{2,1,0:T(8,128)S(1)} %add.17), channel_id=1, source_target_pairs={{0,72},{8,64},{16,88},{24,80},{32,104},{40,96},{48,120},{56,112},{... | collective-permute-start | bytes 196616 | tf_op jit(solution)/shard_map/ppermute | solution.py:371
  18.5 4.9 %collective-permute-start.4 = (f32[16,8,128]{2,1,0:T(8,128)S(1)}, f32[16,8,128]{2,1,0:T(8,128)S(1)}, u32[]{:S(2)}, u32[]{:S(2)}) collective-permute-start(f32[16,8,128]{2,1,0:T(8,128)S(1)} %add.18), channel_id=1, source_target_pairs={{0,128},{8,136},{16,144},{24,152},{32,160},{40,168},{48,176},{56,1... | collective-permute-start | bytes 196616 | tf_op jit(solution)/shard_map/ppermute | solution.py:371
  23.7 43.8 %copy-start = (f32[2,512,32]{1,2,0:T(8,128)S(1)}, f32[2,512,32]{1,2,0:T(8,128)}, u32[]{:S(2)}) copy-start(f32[2,512,32]{1,2,0:T(8,128)} %param.6) | copy-start | bytes 393220
  23.7 43.8 %copy-start.1 = (f32[2,512,32]{1,2,0:T(8,128)S(1)}, f32[2,512,32]{1,2,0:T(8,128)}, u32[]{:S(2)}) copy-start(f32[2,512,32]{1,2,0:T(8,128)} %param.7) | copy-start | bytes 393220
  23.8 5.4 %collective-permute-start.6 = (f32[16,16,128]{2,1,0:T(8,128)S(1)}, f32[16,16,128]{2,1,0:T(8,128)S(1)}, u32[]{:S(2)}, u32[]{:S(2)}) collective-permute-start(f32[16,16,128]{2,1,0:T(8,128)S(1)} %shard_map.70), channel_id=1, source_target_pairs={{0,8},{8,0},{1,9},{9,1},{2,10},{10,2},{3,11},{11,3},{4,12},{12,4},... | collective-permute-start | bytes 393224 | tf_op jit(solution)/shard_map/ppermute | solution.py:338
  27.1 1.3 %collective-permute-start.5 = (f32[16,8,128]{2,1,0:T(8,128)S(1)}, f32[16,8,128]{2,1,0:T(8,128)S(1)}, u32[]{:S(2)}, u32[]{:S(2)}) collective-permute-start(f32[16,8,128]{2,1,0:T(8,128)S(1)} %add.19.mine_ref.left_ref), channel_id=1, source_target_pairs={{0,8},{8,0},{1,9},{9,1},{2,10},{10,2},{3,11},{11,3},{4,12},{12,4},... | collective-permute-start | bytes 196616 | tf_op jit(solution)/shard_map/ppermute | solution.py:338
  67.4 1.6 %collective-permute-start.7 = (f32[32,8,128]{2,1,0:T(8,128)S(1)}, f32[32,8,128]{2,1,0:T(8,128)S(1)}, u32[]{:S(2)}, u32[]{:S(2)}) collective-permute-start(f32[32,8,128]{2,1,0:T(8,128)S(1)} %bitcast.14), channel_id=1, source_target_pairs={{0,8},{8,0},{1,9},{9,1},{2,10},{10,2},{3,11},{11,3},{4,12},{12,4},... | collective-permute-start | bytes 393224 | tf_op jit(solution)/shard_map/ppermute | solution.py:338

commit v12 on v11

--- a/solution.py
+++ b/solution.py
@@ -365,10 +365,12 @@
         cost_estimate=pl.CostEstimate(flops=1 << 20, bytes_accessed=1 << 18, transcendentals=0),
     )(*(pltpu.with_memory_space_constraint(a, pltpu.HBM) for a in (basis, grads)))
     away = swapped(away)
-    mine = kernel_call(left_body, lefts)(basis, grads) + away
+    mine = kernel_call(left_body, lefts)(basis, grads)
+    halves = [mine[:8] + away[:8], mine[8:] + away[8:]]
     for flip, cross in DOUBLING:
         pairs = [(2 * p + c, 2 * (p ^ flip) + (c ^ cross)) for p in range(16) for c in range(2)]
-        mine = mine + lax.ppermute(mine, REPLICA, pairs)
+        halves = [half + lax.ppermute(half, REPLICA, pairs) for half in halves]
+    mine = jnp.concatenate(halves, axis=0)
     other = swapped(mine)
     away = kernel_call(sent_body, rights)(mine, grads)
     away = swapped(away)

time: 70.6 us -> 69.4 us (0.983)
  starting transfers between devices: 14.4 us -> 18.4 us
  waiting for transfers between devices: 10.9 us -> 7.14 us
  blocking collectives: 38.1 us -> 36.8 us
    ppermute x4 -> x8, starting transfers between devices: 7.56 us -> 12.3 us  [shards(): halves = [half + lax.ppermute(half, REPLICA, pairs) for half in halves]]
    ppermute x4 -> x8, waiting for transfers between devices: 9.28 us -> 5.48 us  [shards(): halves = [half + lax.ppermute(half, REPLICA, pairs) for half in halves]]
    all_to_all x3, blocking collectives: 38.1 us -> 36.8 us  [all_to_all(): lax.all_to_all(value, axes, 0, 0, axis_index_groups=groups, tiled=True)]
    ppermute x4, starting transfers between devices: 6.87 us -> 6.05 us  [swapped(): return lax.ppermute(value, 'core', [(0, 1), (1, 0)])]
  transfers between devices with their start and end apart: 8 -> 12, of which waited for: 6 -> 7; matrix products, arithmetic and copies ran while one was open for 0% -> 0% of each run, Pallas kernels for 4% -> 4%
where the time goes in v12:
time: 69.4 us; the launch traced here: 69.2 us
  blocking collectives  36.8 us (53%)
  starting transfers between devices  18.4 us (27%)
  waiting for transfers between devices  7.14 us (10%)
  Pallas kernels  6.08 us (9%)
  between operations  0.72 us (1%)
    all_to_all x3, blocking collectives, all_to_all(): lax.all_to_all(value, axes, 0, 0, axis_index_groups=groups, tiled=True)  36.8 us
    ppermute x8, starting transfers between devices, shards(): halves = [half + lax.ppermute(half, REPLICA, pairs) for half in halves]  12.3 us
    ppermute x4, starting transfers between devices, swapped(): return lax.ppermute(value, 'core', [(0, 1), (1, 0)])  6.05 us
    ppermute x8, waiting for transfers between devices, shards(): halves = [half + lax.ppermute(half, REPLICA, pairs) for half in halves]  5.48 us
    pallas_call x7, Pallas kernels, kernel_call(): pl.pallas_call(body, out_shape=outs, in_specs=[spec] * len(args), out_spe...  2.99 us
    pallas_call x1, Pallas kernels, shards(): pl.pallas_call(first_body, out_shape=[lefts, jax.ShapeDtypeStruct(grads.s...  1.7 us
    ppermute x4, waiting for transfers between devices, swapped(): return lax.ppermute(value, 'core', [(0, 1), (1, 0)])  1.67 us
    pallas_call x1, Pallas kernels, last(): pl.pallas_call(late_body, out_shape=[f32(2, *shape) for shape in shapes],...  1.39 us
  transfers between devices with their start and end apart: 12, of which 7 were waited for; matrix products, arithmetic and copies ran while one was open for 0% of the time, Pallas kernels for 4%

profile of v12, /device:TPU:1, one launch (start us, length us, event | category | flops | bytes accessed | tf_op | source)
XLA Modules:
  0.0 69.2 jit_solution(5727787818895175928)
XLA Ops:
  0.6 1.7 %shard_map.67 = (f32[16,8,128]{2,1,0:T(8,128)S(1)}, bf16[2,512,1024]{2,1,0:T(8,128)(2,1)S(1)}, f32[2,32,1024]{2,1,0:T(8,128)S(1)}) custom-call(f32[2,32,1024]{2,1,0:T(8,128)} %bitcast.23, bf16[2,512,1024]{2,1,0:T(8,128)(2,1)} %bitcast.22), custom_call_target="tpu_custom_call" | custom-call | flops 1048576 | bytes 262144 | tf_op jit(solution)/shard_map/pallas_call | solution.py:358
  2.3 3.3 %collective-permute-start = (f32[16,8,128]{2,1,0:T(8,128)S(1)}, f32[16,8,128]{2,1,0:T(8,128)S(1)}, u32[]{:S(2)}, u32[]{:S(2)}) collective-permute-start(f32[16,8,128]{2,1,0:T(8,128)S(1)} %get-tuple-element.21), channel_id=1, source_target_pairs={{0,8},{8,0},{1,9},{9,1},{2,10},{10,2},{3,11},{11,3},{4,12},{12,4},... | collective-permute-start | bytes 196616 | tf_op jit(solution)/shard_map/ppermute | solution.py:338
  5.6 0.4 shard_map.68
  6.0 0.5 collective-permute-done
  6.5 0.1 collective-permute-start.1
  6.6 1.5 %collective-permute-start.5 = (f32[8,8,128]{2,1,0:T(8,128)S(1)}, f32[8,8,128]{2,1,0:T(8,128)S(1)}, u32[]{:S(2)}, u32[]{:S(2)}) collective-permute-start(f32[8,8,128]{2,1,0:T(8,128)S(1)} %get-tuple-element.36), channel_id=1, source_target_pairs={{0,16},{8,24},{16,0},{24,8},{32,48},{40,56},{48,32},{56,40},{64,80... | collective-permute-start | bytes 98312 | tf_op jit(solution)/shard_map/ppermute | solution.py:372
  8.1 1.3 %collective-permute-done.1 = f32[8,8,128]{2,1,0:T(8,128)S(1)} collective-permute-done((f32[8,8,128]{2,1,0:T(8,128)S(1)}, f32[8,8,128]{2,1,0:T(8,128)S(1)}, u32[]{:S(2)}, u32[]{:S(2)}) %collective-permute-start.1) | collective-permute-done | bytes 32800 | tf_op jit(solution)/shard_map/ppermute | solution.py:372
  9.4 2.4 %collective-permute-start.2 = (f32[8,8,128]{2,1,0:T(8,128)S(1)}, f32[8,8,128]{2,1,0:T(8,128)S(1)}, u32[]{:S(2)}, u32[]{:S(2)}) collective-permute-start(f32[8,8,128]{2,1,0:T(8,128)S(1)} %add.31), channel_id=1, source_target_pairs={{0,56},{8,48},{16,40},{24,32},{32,24},{40,16},{48,8},{56,0},{64,12... | collective-permute-start | bytes 98312 | tf_op jit(solution)/shard_map/ppermute | solution.py:372
  11.8 0.0 collective-permute-done.5
  11.8 0.7 %collective-permute-start.6 = (f32[8,8,128]{2,1,0:T(8,128)S(1)}, f32[8,8,128]{2,1,0:T(8,128)S(1)}, u32[]{:S(2)}, u32[]{:S(2)}) collective-permute-start(f32[8,8,128]{2,1,0:T(8,128)S(1)} %add.36), channel_id=1, source_target_pairs={{0,56},{8,48},{16,40},{24,32},{32,24},{40,16},{48,8},{56,0},{64,12... | collective-permute-start | bytes 98312 | tf_op jit(solution)/shard_map/ppermute | solution.py:372
  12.6 1.4 %collective-permute-done.2 = f32[8,8,128]{2,1,0:T(8,128)S(1)} collective-permute-done((f32[8,8,128]{2,1,0:T(8,128)S(1)}, f32[8,8,128]{2,1,0:T(8,128)S(1)}, u32[]{:S(2)}, u32[]{:S(2)}) %collective-permute-start.2) | collective-permute-done | bytes 32800 | tf_op jit(solution)/shard_map/ppermute | solution.py:372
  14.0 1.3 %collective-permute-start.3 = (f32[8,8,128]{2,1,0:T(8,128)S(1)}, f32[8,8,128]{2,1,0:T(8,128)S(1)}, u32[]{:S(2)}, u32[]{:S(2)}) collective-permute-start(f32[8,8,128]{2,1,0:T(8,128)S(1)} %add.32), channel_id=1, source_target_pairs={{0,72},{8,64},{16,88},{24,80},{32,104},{40,96},{48,120},{56,112},{... | collective-permute-start | bytes 98312 | tf_op jit(solution)/shard_map/ppermute | solution.py:372
  15.3 1.2 %collective-permute-done.6 = f32[8,8,128]{2,1,0:T(8,128)S(1)} collective-permute-done((f32[8,8,128]{2,1,0:T(8,128)S(1)}, f32[8,8,128]{2,1,0:T(8,128)S(1)}, u32[]{:S(2)}, u32[]{:S(2)}) %collective-permute-start.6) | collective-permute-done | bytes 32800 | tf_op jit(solution)/shard_map/ppermute | solution.py:372
  16.5 0.5 collective-permute-start.7
  17.0 0.3 collective-permute-done.3
  17.3 2.8 %collective-permute-start.4 = (f32[8,8,128]{2,1,0:T(8,128)S(1)}, f32[8,8,128]{2,1,0:T(8,128)S(1)}, u32[]{:S(2)}, u32[]{:S(2)}) collective-permute-start(f32[8,8,128]{2,1,0:T(8,128)S(1)} %add.33), channel_id=1, source_target_pairs={{0,128},{8,136},{16,144},{24,152},{32,160},{40,168},{48,176},{56,1... | collective-permute-start | bytes 98312 | tf_op jit(solution)/shard_map/ppermute | solution.py:372
  20.1 0.0 collective-permute-done.7
  20.1 3.0 %collective-permute-start.8 = (f32[8,8,128]{2,1,0:T(8,128)S(1)}, f32[8,8,128]{2,1,0:T(8,128)S(1)}, u32[]{:S(2)}, u32[]{:S(2)}) collective-permute-start(f32[8,8,128]{2,1,0:T(8,128)S(1)} %add.38), channel_id=1, source_target_pairs={{0,128},{8,136},{16,144},{24,152},{32,160},{40,168},{48,176},{56,1... | collective-permute-start | bytes 98312 | tf_op jit(solution)/shard_map/ppermute | solution.py:372
  23.1 0.0 collective-permute-done.4
  23.1 1.3 %collective-permute-done.8 = f32[8,8,128]{2,1,0:T(8,128)S(1)} collective-permute-done((f32[8,8,128]{2,1,0:T(8,128)S(1)}, f32[8,8,128]{2,1,0:T(8,128)S(1)}, u32[]{:S(2)}, u32[]{:S(2)}) %collective-permute-start.8) | collective-permute-done | bytes 32800 | tf_op jit(solution)/shard_map/ppermute | solution.py:372
  24.4 0.3 shard_map.70
  24.7 2.7 %collective-permute-start.10 = (f32[16,16,128]{2,1,0:T(8,128)S(1)}, f32[16,16,128]{2,1,0:T(8,128)S(1)}, u32[]{:S(2)}, u32[]{:S(2)}) collective-permute-start(f32[16,16,128]{2,1,0:T(8,128)S(1)} %shard_map.70), channel_id=1, source_target_pairs={{0,8},{8,0},{1,9},{9,1},{2,10},{10,2},{3,11},{11,3},{4,12},{12,4},... | collective-permute-start | bytes 393224 | tf_op jit(solution)/shard_map/ppermute | solution.py:338
  27.4 0.1 collective-permute-start.9
  27.5 1.2 %collective-permute-done.9.other_ref.left_ref = f32[16,8,128]{2,1,0:T(8,128)S(1)} collective-permute-done((f32[16,8,128]{2,1,0:T(8,128)S(1)}, f32[16,8,128]{2,1,0:T(8,128)S(1)}, u32[]{:S(2)}, u32[]{:S(2)}) %collective-permute-start.9) | collective-permute-done | bytes 65568 | tf_op jit(solution)/shard_map/ppermute | solution.py:338
  28.7 0.8 %shard_map.69 = (f32[16,16,128]{2,1,0:T(8,128)S(1)}, f32[4,128]{1,0:T(4,128)S(1)}) custom-call(f32[16,8,128]{2,1,0:T(8,128)S(1)} %pad_maximum_fusion.mine_ref.left_ref, f32[16,8,128]{2,1,0:T(8,128)S(1)} %collective-permute-done.9.other_ref.left_ref, bf16[2,512,1024]{2,1,0:T(8,128)(2,1)S(1)} %get-tuple-element.20.grads_ref), custom_call_target="tpu_custom_call" | custom-call | flops 1048576 | bytes 262144 | tf_op jit(solution)/shard_map/pallas_call | solution.py:30
  29.4 0.0 collective-permute-done.10.other_ref
  29.5 12.8 %all_to_all.15 = f32[80,4,128]{2,1,0:T(4,128)S(1)} all-to-all(f32[80,4,128]{2,1,0:T(4,128)S(1)} %bitcast.12), channel_id=1, replica_groups={{0,1,2,3,16,17,18,19,40,41,42,43,56,57,58,59},{8,9,10,11,24,25,26,27,32..., dimensions={0} | all-to-all | bytes 327680 | tf_op jit(solution)/shard_map/all_to_all | solution.py:346
  42.3 10.5 %all_to_all.16 = f32[40,4,128]{2,1,0:T(4,128)S(1)} all-to-all(f32[40,4,128]{2,1,0:T(4,128)S(1)} %bitcast.21), channel_id=1, replica_groups={{0,12,68,72,128,140,196,200},{4,8,64,76,132,136,192,204},{1,13,69,73,12..., dimensions={0} | all-to-all | bytes 163840 | tf_op jit(solution)/shard_map/all_to_all | solution.py:346
  52.9 13.5 %all_to_all.17 = f32[16,16,128]{2,1,0:T(8,128)S(1)} all-to-all(f32[16,16,128]{2,1,0:T(8,128)S(1)} %get-tuple-element.24), channel_id=1, replica_groups={{0,1,2,3,16,17,18,19,40,41,42,43,56,57,58,59},{8,9,10,11,24,25,26,27,32..., dimensions={0} | all-to-all | bytes 262144 | tf_op jit(solution)/shard_map/all_to_all | solution.py:346
  66.3 0.0 collective-permute-start.11
  66.4 1.4 %shard_map.74 = (f32[32,128]{1,0:T(8,128)S(1)}, f32[32,1024]{1,0:T(8,128)S(1)}, f32[32,512]{1,0:T(8,128)S(1)}, f32[32,512]{1,0:T(8,128)S(1)}) custom-call(f32[16,128]{1,0:T(8,128)S(1)} %get-tuple-element.27.gram_ref, f32[32,8,128]{2,1,0:T(8,128)S(1)} %bitcast.15, f32[16,8,128]{2,1,0:T(8,128)S(1)} %collective-permute-done.9.other_ref.left_ref, ...), custom_call_target="tpu_custom_call" | custom-call | flops 1048576 | bytes 262144 | tf_op jit(solution)/shard_map/pallas_call | solution.py:30
  67.8 1.4 %shard_map.75 = (f32[2,32,1024]{2,1,0:T(8,128)}, f32[2,32,512]{2,1,0:T(8,128)}, f32[2,32,512]{2,1,0:T(8,128)}) custom-call(f32[32,8,128]{2,1,0:T(8,128)S(1)} %collective-permute-done.11.right_ref, f32[16,8,128]{2,1,0:T(8,128)S(1)} %pad_maximum_fusion.mine_ref.left_ref, f32[2,32,512]{2,1,0:T(8,128)S(1)} %bitcast.17, f32[2,32,512]{2,1,0:T(8,128)S(1)} %bitcast.19, ...), custom_call_target="tpu_custom_call" | custom-call | flops 1048576 | bytes 262144 | tf_op jit(solution)/shard_map/pallas_call | solution.py:320
  (18 shorter events, 0.1 us)
Async XLA Ops:
  2.3 4.2 %collective-permute-start = (f32[16,8,128]{2,1,0:T(8,128)S(1)}, f32[16,8,128]{2,1,0:T(8,128)S(1)}, u32[]{:S(2)}, u32[]{:S(2)}) collective-permute-start(f32[16,8,128]{2,1,0:T(8,128)S(1)} %get-tuple-element.21), channel_id=1, source_target_pairs={{0,8},{8,0},{1,9},{9,1},{2,10},{10,2},{3,11},{11,3},{4,12},{12,4},... | collective-permute-start | bytes 196616 | tf_op jit(solution)/shard_map/ppermute | solution.py:338
  6.5 2.9 %collective-permute-start.1 = (f32[8,8,128]{2,1,0:T(8,128)S(1)}, f32[8,8,128]{2,1,0:T(8,128)S(1)}, u32[]{:S(2)}, u32[]{:S(2)}) collective-permute-start(f32[8,8,128]{2,1,0:T(8,128)S(1)} %get-tuple-element.35), channel_id=1, source_target_pairs={{0,16},{8,24},{16,0},{24,8},{32,48},{40,56},{48,32},{56,40},{64,80... | collective-permute-start | bytes 98312 | tf_op jit(solution)/shard_map/ppermute | solution.py:372
  6.6 5.2 %collective-permute-start.5 = (f32[8,8,128]{2,1,0:T(8,128)S(1)}, f32[8,8,128]{2,1,0:T(8,128)S(1)}, u32[]{:S(2)}, u32[]{:S(2)}) collective-permute-start(f32[8,8,128]{2,1,0:T(8,128)S(1)} %get-tuple-element.36), channel_id=1, source_target_pairs={{0,16},{8,24},{16,0},{24,8},{32,48},{40,56},{48,32},{56,40},{64,80... | collective-permute-start | bytes 98312 | tf_op jit(solution)/shard_map/ppermute | solution.py:372
  9.4 4.6 %collective-permute-start.2 = (f32[8,8,128]{2,1,0:T(8,128)S(1)}, f32[8,8,128]{2,1,0:T(8,128)S(1)}, u32[]{:S(2)}, u32[]{:S(2)}) collective-permute-start(f32[8,8,128]{2,1,0:T(8,128)S(1)} %add.31), channel_id=1, source_target_pairs={{0,56},{8,48},{16,40},{24,32},{32,24},{40,16},{48,8},{56,0},{64,12... | collective-permute-start | bytes 98312 | tf_op jit(solution)/shard_map/ppermute | solution.py:372
  11.8 4.6 %collective-permute-start.6 = (f32[8,8,128]{2,1,0:T(8,128)S(1)}, f32[8,8,128]{2,1,0:T(8,128)S(1)}, u32[]{:S(2)}, u32[]{:S(2)}) collective-permute-start(f32[8,8,128]{2,1,0:T(8,128)S(1)} %add.36), channel_id=1, source_target_pairs={{0,56},{8,48},{16,40},{24,32},{32,24},{40,16},{48,8},{56,0},{64,12... | collective-permute-start | bytes 98312 | tf_op jit(solution)/shard_map/ppermute | solution.py:372
  14.0 3.3 %collective-permute-start.3 = (f32[8,8,128]{2,1,0:T(8,128)S(1)}, f32[8,8,128]{2,1,0:T(8,128)S(1)}, u32[]{:S(2)}, u32[]{:S(2)}) collective-permute-start(f32[8,8,128]{2,1,0:T(8,128)S(1)} %add.32), channel_id=1, source_target_pairs={{0,72},{8,64},{16,88},{24,80},{32,104},{40,96},{48,120},{56,112},{... | collective-permute-start | bytes 98312 | tf_op jit(solution)/shard_map/ppermute | solution.py:372
  16.5 3.6 %collective-permute-start.7 = (f32[8,8,128]{2,1,0:T(8,128)S(1)}, f32[8,8,128]{2,1,0:T(8,128)S(1)}, u32[]{:S(2)}, u32[]{:S(2)}) collective-permute-start(f32[8,8,128]{2,1,0:T(8,128)S(1)} %add.37), channel_id=1, source_target_pairs={{0,72},{8,64},{16,88},{24,80},{32,104},{40,96},{48,120},{56,112},{... | collective-permute-start | bytes 98312 | tf_op jit(solution)/shard_map/ppermute | solution.py:372
  17.3 5.8 %collective-permute-start.4 = (f32[8,8,128]{2,1,0:T(8,128)S(1)}, f32[8,8,128]{2,1,0:T(8,128)S(1)}, u32[]{:S(2)}, u32[]{:S(2)}) collective-permute-start(f32[8,8,128]{2,1,0:T(8,128)S(1)} %add.33), channel_id=1, source_target_pairs={{0,128},{8,136},{16,144},{24,152},{32,160},{40,168},{48,176},{56,1... | collective-permute-start | bytes 98312 | tf_op jit(solution)/shard_map/ppermute | solution.py:372
  20.1 4.3 %collective-permute-start.8 = (f32[8,8,128]{2,1,0:T(8,128)S(1)}, f32[8,8,128]{2,1,0:T(8,128)S(1)}, u32[]{:S(2)}, u32[]{:S(2)}) collective-permute-start(f32[8,8,128]{2,1,0:T(8,128)S(1)} %add.38), channel_id=1, source_target_pairs={{0,128},{8,136},{16,144},{24,152},{32,160},{40,168},{48,176},{56,1... | collective-permute-start | bytes 98312 | tf_op jit(solution)/shard_map/ppermute | solution.py:372
  24.7 41.6 %copy-start = (f32[2,512,32]{1,2,0:T(8,128)S(1)}, f32[2,512,32]{1,2,0:T(8,128)}, u32[]{:S(2)}) copy-start(f32[2,512,32]{1,2,0:T(8,128)} %param.6) | copy-start | bytes 393220
  24.7 41.6 %copy-start.1 = (f32[2,512,32]{1,2,0:T(8,128)S(1)}, f32[2,512,32]{1,2,0:T(8,128)}, u32[]{:S(2)}) copy-start(f32[2,512,32]{1,2,0:T(8,128)} %param.7) | copy-start | bytes 393220
  24.7 4.7 %collective-permute-start.10 = (f32[16,16,128]{2,1,0:T(8,128)S(1)}, f32[16,16,128]{2,1,0:T(8,128)S(1)}, u32[]{:S(2)}, u32[]{:S(2)}) collective-permute-start(f32[16,16,128]{2,1,0:T(8,128)S(1)} %shard_map.70), channel_id=1, source_target_pairs={{0,8},{8,0},{1,9},{9,1},{2,10},{10,2},{3,11},{11,3},{4,12},{12,4},... | collective-permute-start | bytes 393224 | tf_op jit(solution)/shard_map/ppermute | solution.py:338
  27.4 1.3 %collective-permute-start.9 = (f32[16,8,128]{2,1,0:T(8,128)S(1)}, f32[16,8,128]{2,1,0:T(8,128)S(1)}, u32[]{:S(2)}, u32[]{:S(2)}) collective-permute-start(f32[16,8,128]{2,1,0:T(8,128)S(1)} %pad_maximum_fusion.mine_ref.left_ref), channel_id=1, source_target_pairs={{0,8},{8,0},{1,9},{9,1},{2,10},{10,2},{3,11},{11,3},{4,12},{12,4},... | collective-permute-start | bytes 196616 | tf_op jit(solution)/shard_map/ppermute | solution.py:338
  66.3 1.5 %collective-permute-start.11 = (f32[32,8,128]{2,1,0:T(8,128)S(1)}, f32[32,8,128]{2,1,0:T(8,128)S(1)}, u32[]{:S(2)}, u32[]{:S(2)}) collective-permute-start(f32[32,8,128]{2,1,0:T(8,128)S(1)} %bitcast.14), channel_id=1, source_target_pairs={{0,8},{8,0},{1,9},{9,1},{2,10},{10,2},{3,11},{11,3},{4,12},{12,4},... | collective-permute-start | bytes 393224 | tf_op jit(solution)/shard_map/ppermute | solution.py:338

commit v13 on v12

--- a/solution.py
+++ b/solution.py
@@ -236,7 +236,7 @@
 def settled(layer, right_ref, inverse, left_ref, weights_ref, momentum_ref):
     place = (lax.axis_index("zlo") * 4 + lax.axis_index("y")) * 2 + core()
     block = place // 4
-    shift = (4 - place % 4) * 32
+    shift = (4 - place % 4) % 4 * 32
     own = jnp.concatenate([right_ref[8 * t + block] for t in range(4)], axis=0)
     own = pltpu.roll(own, shift, 1)[:, :RANK]
     inverse = jnp.where(layer == 0, inverse[:, :RANK], inverse[:, RANK : 2 * RANK])
@@ -271,21 +271,15 @@
         basis_ref[at] = right_ref[8 * t + j] * scale
 
 
-def early_body(
-    gram_ref, right_ref, left_ref, weights_ref, momentum_ref, inverse_ref, basis_ref, w_ref, m_ref
-):
-    inverse = inverse_factors(gram_ref[...])
-    inverse_ref[...] = inverse
+def early_body(gram_ref, right_ref, inverse_ref, basis_ref):
+    inverse_ref[...] = inverse_factors(gram_ref[...])
     scale = scale_of(right_ref)
     for t in range(4):
         put_scaled(right_ref, scale, t, basis_ref)
-    m_ref[...], w_ref[...] = settled(
-        owned(), right_ref, inverse, left_ref, weights_ref, momentum_ref
-    )
 
 
 def late_body(
-    right_ref, left_ref, weights_ref, momentum_ref, inverse_ref, b_ref, w_ref, m_ref,
+    own_right_ref, right_ref, own_left_ref, left_ref, weights_ref, momentum_ref, inverse_ref, b_ref,
     basis_hbm, w_hbm, m_hbm, basis_ref, new_w_ref, new_m_ref, sems,
 ):
     layer = held()
@@ -296,42 +290,47 @@
         copies[-1].start()
 
     send(b_ref, basis_hbm.at[1 - layer])
-    send(w_ref, w_hbm.at[1 - layer])
-    send(m_ref, m_hbm.at[1 - layer])
-    new, weights = settled(
-        layer, right_ref, inverse_ref[...], left_ref, weights_ref, momentum_ref
-    )
+    inverse = inverse_ref[...]
     scale = scale_of(right_ref)
+    results = [
+        settled(1 - layer, own_right_ref, inverse, own_left_ref, weights_ref, momentum_ref),
+        settled(layer, right_ref, inverse, left_ref, weights_ref, momentum_ref),
+    ]
     for t in range(4):
         put_scaled(right_ref, scale, t, basis_ref)
         rows = slice(8 * t, 8 * t + 8)
         send(basis_ref.at[rows], basis_hbm.at[layer, rows])
-    new_m_ref[...] = new
-    send(new_m_ref, m_hbm.at[layer])
-    new_w_ref[...] = weights
-    send(new_w_ref, w_hbm.at[layer])
+    for i, (new, weights) in enumerate(results):
+        at = layer if i else 1 - layer
+        new_m_ref[i] = new
+        send(new_m_ref.at[i], m_hbm.at[at])
+        new_w_ref[i] = weights
+        send(new_w_ref.at[i], w_hbm.at[at])
     for copy in copies:
         copy.wait()
 
 
-def last(right, left, weights, momentum, early):
+def last(*args):
+    _, basis = args[-2:]
+    weights = args[-4]
     local, far = pl.BlockSpec(memory_space=pltpu.VMEM), pl.BlockSpec(memory_space=pltpu.HBM)
-    shapes = [early[1].shape, early[2].shape, early[3].shape]
     return pl.pallas_call(
         late_body,
-        out_shape=[f32(2, *shape) for shape in shapes],
-        in_specs=[local] * 8,
+        out_shape=[f32(2, *basis.shape), f32(*weights.shape), f32(*weights.shape)],
+        in_specs=[local] * len(args),
         out_specs=[far] * 3,
         scratch_shapes=[
-            *(pltpu.VMEM(shape, jnp.float32) for shape in shapes),
+            pltpu.VMEM(basis.shape, jnp.float32),
+            pltpu.VMEM(weights.shape, jnp.float32),
+            pltpu.VMEM(weights.shape, jnp.float32),
             pltpu.SemaphoreType.DMA((9,)),
         ],
         compiler_params=pltpu.CompilerParams(vmem_limit_bytes=VMEM_LIMIT),
         cost_estimate=pl.CostEstimate(flops=1 << 20, bytes_accessed=1 << 18, transcendentals=0),
-    )(right, left, weights, momentum, *early)
-
-
-DOUBLING = ((1, 0), (3, 1), (4, 1), (8, 0))
+    )(*args)
+
+
+DOUBLING = (((1, 0), (3, 1), (4, 1), (8, 0)), ((4, 1), (8, 0), (1, 0), (3, 1)))
 
 
 def swapped(value):
@@ -348,7 +347,7 @@
 
 def shards(layer_grads, last_basis, layer_weights, momentum):
     grads = layer_grads[0]
-    _, rows, width = grads.shape
+    _, _, width = grads.shape
     basis = jnp.swapaxes(last_basis, 1, 2)
     weights, momentum = jnp.swapaxes(layer_weights, 1, 2), jnp.swapaxes(momentum, 1, 2)
     lefts, rights = f32(PEERS, 8, LANES), f32(PEERS, 16, LANES)
@@ -367,9 +366,12 @@
     away = swapped(away)
     mine = kernel_call(left_body, lefts)(basis, grads)
     halves = [mine[:8] + away[:8], mine[8:] + away[8:]]
-    for flip, cross in DOUBLING:
-        pairs = [(2 * p + c, 2 * (p ^ flip) + (c ^ cross)) for p in range(16) for c in range(2)]
-        halves = [half + lax.ppermute(half, REPLICA, pairs) for half in halves]
+    for steps in zip(*DOUBLING):
+        for h, (flip, cross) in enumerate(steps):
+            pairs = [
+                (2 * p + c, 2 * (p ^ flip) + (c ^ cross)) for p in range(16) for c in range(2)
+            ]
+            halves[h] = halves[h] + lax.ppermute(halves[h], REPLICA, pairs)
     mine = jnp.concatenate(halves, axis=0)
     other = swapped(mine)
     away = kernel_call(sent_body, rights)(mine, grads)
@@ -384,10 +386,10 @@
     right = all_to_all(sent, PLANE)
     right, gram = lax.optimization_barrier((right.reshape(32, 8, LANES), gram))
     late = swapped(right)
-    early = kernel_call(
-        early_body, [f32(RANK, LANES), f32(RANK, width), f32(RANK, rows), f32(RANK, rows)]
-    )(gram, right, other, weights, momentum)
-    new_basis, new_weights, new_momentum = last(late, mine, weights, momentum, early)
+    inverse, early = kernel_call(early_body, [f32(RANK, LANES), f32(RANK, width)])(gram, right)
+    new_basis, new_weights, new_momentum = last(
+        right, late, other, mine, weights, momentum, inverse, early
+    )
     return tuple(jnp.swapaxes(a, 1, 2) for a in (new_weights, new_basis, new_momentum))
 
 

time: 69.4 us -> 69.5 us (level)
  starting transfers between devices: 18.4 us -> 16.6 us
  waiting for transfers between devices: 7.14 us -> 8.22 us
  blocking collectives: 36.8 us -> 37.8 us
    ppermute x4, starting transfers between devices: 6.05 us -> 4.1 us  [swapped(): return lax.ppermute(value, 'core', [(0, 1), (1, 0)])]
    all_to_all x3, blocking collectives: 36.8 us -> 37.8 us  [all_to_all(): lax.all_to_all(value, axes, 0, 0, axis_index_groups=groups, tiled=True)]
  transfers between devices with their start and end apart: 12 -> 12, of which waited for: 7 -> 7; matrix products, arithmetic and copies ran while one was open for 0% -> 0% of each run, Pallas kernels for 4% -> 3%
where the time goes in v13:
time: 69.5 us; the launch traced here: 69.3 us
  blocking collectives  37.8 us (54%)
  starting transfers between devices  16.6 us (24%)
  waiting for transfers between devices  8.22 us (12%)
  Pallas kernels  5.89 us (8%)
  between operations  0.72 us (1%)
    all_to_all x3, blocking collectives, all_to_all(): lax.all_to_all(value, axes, 0, 0, axis_index_groups=groups, tiled=True)  37.8 us
    ppermute x8, starting transfers between devices, shards(): halves[h] = halves[h] + lax.ppermute(halves[h], REPLICA, pairs)  12.5 us
    ppermute x8, waiting for transfers between devices, shards(): halves[h] = halves[h] + lax.ppermute(halves[h], REPLICA, pairs)  6.02 us
    ppermute x4, starting transfers between devices, swapped(): return lax.ppermute(value, 'core', [(0, 1), (1, 0)])  4.1 us
    pallas_call x7, Pallas kernels, kernel_call(): pl.pallas_call(body, out_shape=outs, in_specs=[spec] * len(args), out_spe...  2.34 us
    ppermute x4, waiting for transfers between devices, swapped(): return lax.ppermute(value, 'core', [(0, 1), (1, 0)])  2.2 us
    pallas_call x1, Pallas kernels, last(): pl.pallas_call(late_body, out_shape=[f32(2, *basis.shape), f32(*weights.s...  1.85 us
    pallas_call x1, Pallas kernels, shards(): pl.pallas_call(first_body, out_shape=[lefts, jax.ShapeDtypeStruct(grads.s...  1.7 us
  transfers between devices with their start and end apart: 12, of which 7 were waited for; matrix products, arithmetic and copies ran while one was open for 0% of the time, Pallas kernels for 3%

profile of v13, /device:TPU:1, one launch (start us, length us, event | category | flops | bytes accessed | tf_op | source)
XLA Modules:
  0.0 69.3 jit_solution(12900260020122801494)
XLA Ops:
  0.6 1.7 %shard_map.67 = (f32[16,8,128]{2,1,0:T(8,128)S(1)}, bf16[2,512,1024]{2,1,0:T(8,128)(2,1)S(1)}, f32[2,32,1024]{2,1,0:T(8,128)S(1)}) custom-call(f32[2,32,1024]{2,1,0:T(8,128)} %bitcast.22, bf16[2,512,1024]{2,1,0:T(8,128)(2,1)} %bitcast.21), custom_call_target="tpu_custom_call" | custom-call | flops 1048576 | bytes 262144 | tf_op jit(solution)/shard_map/pallas_call | solution.py:357
  2.3 3.3 %collective-permute-start = (f32[16,8,128]{2,1,0:T(8,128)S(1)}, f32[16,8,128]{2,1,0:T(8,128)S(1)}, u32[]{:S(2)}, u32[]{:S(2)}) collective-permute-start(f32[16,8,128]{2,1,0:T(8,128)S(1)} %get-tuple-element.19), channel_id=1, source_target_pairs={{0,8},{8,0},{1,9},{9,1},{2,10},{10,2},{3,11},{11,3},{4,12},{12,4},... | collective-permute-start | bytes 196616 | tf_op jit(solution)/shard_map/ppermute | solution.py:337
  5.6 0.4 shard_map.68
  6.0 0.5 collective-permute-done
  6.5 0.1 collective-permute-start.1
  6.6 1.7 %collective-permute-start.5 = (f32[8,8,128]{2,1,0:T(8,128)S(1)}, f32[8,8,128]{2,1,0:T(8,128)S(1)}, u32[]{:S(2)}, u32[]{:S(2)}) collective-permute-start(f32[8,8,128]{2,1,0:T(8,128)S(1)} %get-tuple-element.32), channel_id=1, source_target_pairs={{0,72},{8,64},{16,88},{24,80},{32,104},{40,96},{48,120},{56,112},{... | collective-permute-start | bytes 98312 | tf_op jit(solution)/shard_map/ppermute | solution.py:374
  8.4 1.3 %collective-permute-done.1 = f32[8,8,128]{2,1,0:T(8,128)S(1)} collective-permute-done((f32[8,8,128]{2,1,0:T(8,128)S(1)}, f32[8,8,128]{2,1,0:T(8,128)S(1)}, u32[]{:S(2)}, u32[]{:S(2)}) %collective-permute-start.1) | collective-permute-done | bytes 32800 | tf_op jit(solution)/shard_map/ppermute | solution.py:374
  9.7 2.1 %collective-permute-start.2 = (f32[8,8,128]{2,1,0:T(8,128)S(1)}, f32[8,8,128]{2,1,0:T(8,128)S(1)}, u32[]{:S(2)}, u32[]{:S(2)}) collective-permute-start(f32[8,8,128]{2,1,0:T(8,128)S(1)} %add.31), channel_id=1, source_target_pairs={{0,56},{8,48},{16,40},{24,32},{32,24},{40,16},{48,8},{56,0},{64,12... | collective-permute-start | bytes 98312 | tf_op jit(solution)/shard_map/ppermute | solution.py:374
  11.8 0.0 collective-permute-done.5
  11.8 3.1 %collective-permute-start.6 = (f32[8,8,128]{2,1,0:T(8,128)S(1)}, f32[8,8,128]{2,1,0:T(8,128)S(1)}, u32[]{:S(2)}, u32[]{:S(2)}) collective-permute-start(f32[8,8,128]{2,1,0:T(8,128)S(1)} %add.36), channel_id=1, source_target_pairs={{0,128},{8,136},{16,144},{24,152},{32,160},{40,168},{48,176},{56,1... | collective-permute-start | bytes 98312 | tf_op jit(solution)/shard_map/ppermute | solution.py:374
  14.9 0.0 collective-permute-done.2
  14.9 0.9 %collective-permute-start.3 = (f32[8,8,128]{2,1,0:T(8,128)S(1)}, f32[8,8,128]{2,1,0:T(8,128)S(1)}, u32[]{:S(2)}, u32[]{:S(2)}) collective-permute-start(f32[8,8,128]{2,1,0:T(8,128)S(1)} %add.32), channel_id=1, source_target_pairs={{0,72},{8,64},{16,88},{24,80},{32,104},{40,96},{48,120},{56,112},{... | collective-permute-start | bytes 98312 | tf_op jit(solution)/shard_map/ppermute | solution.py:374
  15.8 0.4 collective-permute-done.6
  16.2 0.0 collective-permute-start.7
  16.2 2.3 %collective-permute-done.3 = f32[8,8,128]{2,1,0:T(8,128)S(1)} collective-permute-done((f32[8,8,128]{2,1,0:T(8,128)S(1)}, f32[8,8,128]{2,1,0:T(8,128)S(1)}, u32[]{:S(2)}, u32[]{:S(2)}) %collective-permute-start.3) | collective-permute-done | bytes 32800 | tf_op jit(solution)/shard_map/ppermute | solution.py:374
  18.5 1.3 %collective-permute-start.4 = (f32[8,8,128]{2,1,0:T(8,128)S(1)}, f32[8,8,128]{2,1,0:T(8,128)S(1)}, u32[]{:S(2)}, u32[]{:S(2)}) collective-permute-start(f32[8,8,128]{2,1,0:T(8,128)S(1)} %add.33), channel_id=1, source_target_pairs={{0,128},{8,136},{16,144},{24,152},{32,160},{40,168},{48,176},{56,1... | collective-permute-start | bytes 98312 | tf_op jit(solution)/shard_map/ppermute | solution.py:374
  19.9 0.0 collective-permute-done.7
  19.9 3.2 %collective-permute-start.8 = (f32[8,8,128]{2,1,0:T(8,128)S(1)}, f32[8,8,128]{2,1,0:T(8,128)S(1)}, u32[]{:S(2)}, u32[]{:S(2)}) collective-permute-start(f32[8,8,128]{2,1,0:T(8,128)S(1)} %add.38), channel_id=1, source_target_pairs={{0,56},{8,48},{16,40},{24,32},{32,24},{40,16},{48,8},{56,0},{64,12... | collective-permute-start | bytes 98312 | tf_op jit(solution)/shard_map/ppermute | solution.py:374
  23.1 0.0 collective-permute-done.4
  23.1 2.0 %collective-permute-done.8 = f32[8,8,128]{2,1,0:T(8,128)S(1)} collective-permute-done((f32[8,8,128]{2,1,0:T(8,128)S(1)}, f32[8,8,128]{2,1,0:T(8,128)S(1)}, u32[]{:S(2)}, u32[]{:S(2)}) %collective-permute-start.8) | collective-permute-done | bytes 32800 | tf_op jit(solution)/shard_map/ppermute | solution.py:374
  25.1 0.3 shard_map.70
  25.4 0.7 %collective-permute-start.10 = (f32[16,16,128]{2,1,0:T(8,128)S(1)}, f32[16,16,128]{2,1,0:T(8,128)S(1)}, u32[]{:S(2)}, u32[]{:S(2)}) collective-permute-start(f32[16,16,128]{2,1,0:T(8,128)S(1)} %shard_map.70), channel_id=1, source_target_pairs={{0,8},{8,0},{1,9},{9,1},{2,10},{10,2},{3,11},{11,3},{4,12},{12,4},... | collective-permute-start | bytes 393224 | tf_op jit(solution)/shard_map/ppermute | solution.py:337
  26.1 0.1 collective-permute-start.9
  26.2 1.2 %collective-permute-done.9.other_ref.own_left_ref = f32[16,8,128]{2,1,0:T(8,128)S(1)} collective-permute-done((f32[16,8,128]{2,1,0:T(8,128)S(1)}, f32[16,8,128]{2,1,0:T(8,128)S(1)}, u32[]{:S(2)}, u32[]{:S(2)}) %collective-permute-start.9) | collective-permute-done | bytes 65568 | tf_op jit(solution)/shard_map/ppermute | solution.py:337
  27.4 0.8 %shard_map.69 = (f32[16,16,128]{2,1,0:T(8,128)S(1)}, f32[4,128]{1,0:T(4,128)S(1)}) custom-call(f32[16,8,128]{2,1,0:T(8,128)S(1)} %pad_maximum_fusion.mine_ref.left_ref, f32[16,8,128]{2,1,0:T(8,128)S(1)} %collective-permute-done.9.other_ref.own_left_ref, bf16[2,512,1024]{2,1,0:T(8,128)(2,1)S(1)} %get-tuple-element.18.grads_ref), custom_call_target="tpu_custom_call" | custom-call | flops 1048576 | bytes 262144 | tf_op jit(solution)/shard_map/pallas_call | solution.py:30
  28.2 0.0 collective-permute-done.10.other_ref
  28.2 14.0 %all_to_all.15 = f32[80,4,128]{2,1,0:T(4,128)S(1)} all-to-all(f32[80,4,128]{2,1,0:T(4,128)S(1)} %bitcast.15), channel_id=1, replica_groups={{0,1,2,3,16,17,18,19,40,41,42,43,56,57,58,59},{8,9,10,11,24,25,26,27,32..., dimensions={0} | all-to-all | bytes 327680 | tf_op jit(solution)/shard_map/all_to_all | solution.py:345
  42.2 10.4 %all_to_all.16 = f32[40,4,128]{2,1,0:T(4,128)S(1)} all-to-all(f32[40,4,128]{2,1,0:T(4,128)S(1)} %bitcast.18), channel_id=1, replica_groups={{0,12,68,72,128,140,196,200},{4,8,64,76,132,136,192,204},{1,13,69,73,12..., dimensions={0} | all-to-all | bytes 163840 | tf_op jit(solution)/shard_map/all_to_all | solution.py:345
  52.6 13.5 %all_to_all.17 = f32[16,16,128]{2,1,0:T(8,128)S(1)} all-to-all(f32[16,16,128]{2,1,0:T(8,128)S(1)} %get-tuple-element.22), channel_id=1, replica_groups={{0,1,2,3,16,17,18,19,40,41,42,43,56,57,58,59},{8,9,10,11,24,25,26,27,32..., dimensions={0} | all-to-all | bytes 262144 | tf_op jit(solution)/shard_map/all_to_all | solution.py:345
  66.1 0.8 %shard_map.74 = (f32[32,128]{1,0:T(8,128)S(1)}, f32[32,1024]{1,0:T(8,128)S(1)}) custom-call(f32[16,128]{1,0:T(8,128)S(1)} %get-tuple-element.25.gram_ref, f32[32,8,128]{2,1,0:T(8,128)S(1)} %bitcast.13), custom_call_target="tpu_custom_call" | custom-call | flops 1048576 | bytes 262144 | tf_op jit(solution)/shard_map/pallas_call | solution.py:30
  66.9 0.5 collective-permute-done.11.right_ref
  67.4 1.9 %shard_map.75 = (f32[2,32,1024]{2,1,0:T(8,128)}, f32[2,32,512]{2,1,0:T(8,128)}, f32[2,32,512]{2,1,0:T(8,128)}) custom-call(f32[32,8,128]{2,1,0:T(8,128)S(1)} %bitcast.14, f32[32,8,128]{2,1,0:T(8,128)S(1)} %collective-permute-done.11.right_ref, f32[16,8,128]{2,1,0:T(8,128)S(1)} %collective-permute-done.9.other_ref.own_left_ref, ...), custom_call_target="tpu_custom_call" | custom-call | flops 1048576 | bytes 262144 | tf_op jit(solution)/shard_map/pallas_call | solution.py:317
  (18 shorter events, 0.1 us)
Async XLA Ops:
  2.3 4.2 %collective-permute-start = (f32[16,8,128]{2,1,0:T(8,128)S(1)}, f32[16,8,128]{2,1,0:T(8,128)S(1)}, u32[]{:S(2)}, u32[]{:S(2)}) collective-permute-start(f32[16,8,128]{2,1,0:T(8,128)S(1)} %get-tuple-element.19), channel_id=1, source_target_pairs={{0,8},{8,0},{1,9},{9,1},{2,10},{10,2},{3,11},{11,3},{4,12},{12,4},... | collective-permute-start | bytes 196616 | tf_op jit(solution)/shard_map/ppermute | solution.py:337
  6.5 3.1 %collective-permute-start.1 = (f32[8,8,128]{2,1,0:T(8,128)S(1)}, f32[8,8,128]{2,1,0:T(8,128)S(1)}, u32[]{:S(2)}, u32[]{:S(2)}) collective-permute-start(f32[8,8,128]{2,1,0:T(8,128)S(1)} %get-tuple-element.31), channel_id=1, source_target_pairs={{0,16},{8,24},{16,0},{24,8},{32,48},{40,56},{48,32},{56,40},{64,80... | collective-permute-start | bytes 98312 | tf_op jit(solution)/shard_map/ppermute | solution.py:374
  6.6 5.2 %collective-permute-start.5 = (f32[8,8,128]{2,1,0:T(8,128)S(1)}, f32[8,8,128]{2,1,0:T(8,128)S(1)}, u32[]{:S(2)}, u32[]{:S(2)}) collective-permute-start(f32[8,8,128]{2,1,0:T(8,128)S(1)} %get-tuple-element.32), channel_id=1, source_target_pairs={{0,72},{8,64},{16,88},{24,80},{32,104},{40,96},{48,120},{56,112},{... | collective-permute-start | bytes 98312 | tf_op jit(solution)/shard_map/ppermute | solution.py:374
  9.7 5.2 %collective-permute-start.2 = (f32[8,8,128]{2,1,0:T(8,128)S(1)}, f32[8,8,128]{2,1,0:T(8,128)S(1)}, u32[]{:S(2)}, u32[]{:S(2)}) collective-permute-start(f32[8,8,128]{2,1,0:T(8,128)S(1)} %add.31), channel_id=1, source_target_pairs={{0,56},{8,48},{16,40},{24,32},{32,24},{40,16},{48,8},{56,0},{64,12... | collective-permute-start | bytes 98312 | tf_op jit(solution)/shard_map/ppermute | solution.py:374
  11.8 4.4 %collective-permute-start.6 = (f32[8,8,128]{2,1,0:T(8,128)S(1)}, f32[8,8,128]{2,1,0:T(8,128)S(1)}, u32[]{:S(2)}, u32[]{:S(2)}) collective-permute-start(f32[8,8,128]{2,1,0:T(8,128)S(1)} %add.36), channel_id=1, source_target_pairs={{0,128},{8,136},{16,144},{24,152},{32,160},{40,168},{48,176},{56,1... | collective-permute-start | bytes 98312 | tf_op jit(solution)/shard_map/ppermute | solution.py:374
  14.9 3.6 %collective-permute-start.3 = (f32[8,8,128]{2,1,0:T(8,128)S(1)}, f32[8,8,128]{2,1,0:T(8,128)S(1)}, u32[]{:S(2)}, u32[]{:S(2)}) collective-permute-start(f32[8,8,128]{2,1,0:T(8,128)S(1)} %add.32), channel_id=1, source_target_pairs={{0,72},{8,64},{16,88},{24,80},{32,104},{40,96},{48,120},{56,112},{... | collective-permute-start | bytes 98312 | tf_op jit(solution)/shard_map/ppermute | solution.py:374
  16.2 3.7 %collective-permute-start.7 = (f32[8,8,128]{2,1,0:T(8,128)S(1)}, f32[8,8,128]{2,1,0:T(8,128)S(1)}, u32[]{:S(2)}, u32[]{:S(2)}) collective-permute-start(f32[8,8,128]{2,1,0:T(8,128)S(1)} %add.37), channel_id=1, source_target_pairs={{0,16},{8,24},{16,0},{24,8},{32,48},{40,56},{48,32},{56,40},{64,80... | collective-permute-start | bytes 98312 | tf_op jit(solution)/shard_map/ppermute | solution.py:374
  18.5 4.6 %collective-permute-start.4 = (f32[8,8,128]{2,1,0:T(8,128)S(1)}, f32[8,8,128]{2,1,0:T(8,128)S(1)}, u32[]{:S(2)}, u32[]{:S(2)}) collective-permute-start(f32[8,8,128]{2,1,0:T(8,128)S(1)} %add.33), channel_id=1, source_target_pairs={{0,128},{8,136},{16,144},{24,152},{32,160},{40,168},{48,176},{56,1... | collective-permute-start | bytes 98312 | tf_op jit(solution)/shard_map/ppermute | solution.py:374
  19.9 5.2 %collective-permute-start.8 = (f32[8,8,128]{2,1,0:T(8,128)S(1)}, f32[8,8,128]{2,1,0:T(8,128)S(1)}, u32[]{:S(2)}, u32[]{:S(2)}) collective-permute-start(f32[8,8,128]{2,1,0:T(8,128)S(1)} %add.38), channel_id=1, source_target_pairs={{0,56},{8,48},{16,40},{24,32},{32,24},{40,16},{48,8},{56,0},{64,12... | collective-permute-start | bytes 98312 | tf_op jit(solution)/shard_map/ppermute | solution.py:374
  25.4 42.0 %copy-start = (f32[2,512,32]{1,2,0:T(8,128)S(1)}, f32[2,512,32]{1,2,0:T(8,128)}, u32[]{:S(2)}) copy-start(f32[2,512,32]{1,2,0:T(8,128)} %param.6) | copy-start | bytes 393220
  25.4 42.0 %copy-start.1 = (f32[2,512,32]{1,2,0:T(8,128)S(1)}, f32[2,512,32]{1,2,0:T(8,128)}, u32[]{:S(2)}) copy-start(f32[2,512,32]{1,2,0:T(8,128)} %param.7) | copy-start | bytes 393220
  25.4 2.8 %collective-permute-start.10 = (f32[16,16,128]{2,1,0:T(8,128)S(1)}, f32[16,16,128]{2,1,0:T(8,128)S(1)}, u32[]{:S(2)}, u32[]{:S(2)}) collective-permute-start(f32[16,16,128]{2,1,0:T(8,128)S(1)} %shard_map.70), channel_id=1, source_target_pairs={{0,8},{8,0},{1,9},{9,1},{2,10},{10,2},{3,11},{11,3},{4,12},{12,4},... | collective-permute-start | bytes 393224 | tf_op jit(solution)/shard_map/ppermute | solution.py:337
  26.1 1.3 %collective-permute-start.9 = (f32[16,8,128]{2,1,0:T(8,128)S(1)}, f32[16,8,128]{2,1,0:T(8,128)S(1)}, u32[]{:S(2)}, u32[]{:S(2)}) collective-permute-start(f32[16,8,128]{2,1,0:T(8,128)S(1)} %pad_maximum_fusion.mine_ref.left_ref), channel_id=1, source_target_pairs={{0,8},{8,0},{1,9},{9,1},{2,10},{10,2},{3,11},{11,3},{4,12},{12,4},... | collective-permute-start | bytes 196616 | tf_op jit(solution)/shard_map/ppermute | solution.py:337
  66.1 1.3 %collective-permute-start.11 = (f32[32,8,128]{2,1,0:T(8,128)S(1)}, f32[32,8,128]{2,1,0:T(8,128)S(1)}, u32[]{:S(2)}, u32[]{:S(2)}) collective-permute-start(f32[32,8,128]{2,1,0:T(8,128)S(1)} %bitcast.12), channel_id=1, source_target_pairs={{0,8},{8,0},{1,9},{9,1},{2,10},{10,2},{3,11},{11,3},{4,12},{12,4},... | collective-permute-start | bytes 393224 | tf_op jit(solution)/shard_map/ppermute | solution.py:337

commit v14 on v12

--- a/solution.py
+++ b/solution.py
@@ -236,7 +236,7 @@
 def settled(layer, right_ref, inverse, left_ref, weights_ref, momentum_ref):
     place = (lax.axis_index("zlo") * 4 + lax.axis_index("y")) * 2 + core()
     block = place // 4
-    shift = (4 - place % 4) * 32
+    shift = (4 - place % 4) % 4 * 32
     own = jnp.concatenate([right_ref[8 * t + block] for t in range(4)], axis=0)
     own = pltpu.roll(own, shift, 1)[:, :RANK]
     inverse = jnp.where(layer == 0, inverse[:, :RANK], inverse[:, RANK : 2 * RANK])
@@ -331,7 +331,7 @@
     )(right, left, weights, momentum, *early)
 
 
-DOUBLING = ((1, 0), (3, 1), (4, 1), (8, 0))
+DOUBLING = (((1, 0), (3, 1), (4, 1), (8, 0)), ((4, 1), (8, 0), (1, 0), (3, 1)))
 
 
 def swapped(value):
@@ -366,10 +366,13 @@
     )(*(pltpu.with_memory_space_constraint(a, pltpu.HBM) for a in (basis, grads)))
     away = swapped(away)
     mine = kernel_call(left_body, lefts)(basis, grads)
-    halves = [mine[:8] + away[:8], mine[8:] + away[8:]]
-    for flip, cross in DOUBLING:
-        pairs = [(2 * p + c, 2 * (p ^ flip) + (c ^ cross)) for p in range(16) for c in range(2)]
-        halves = [half + lax.ppermute(half, REPLICA, pairs) for half in halves]
+    halves = [mine[:10] + away[:10], mine[10:] + away[10:]]
+    for steps in zip(*DOUBLING):
+        for h, (flip, cross) in enumerate(steps):
+            pairs = [
+                (2 * p + c, 2 * (p ^ flip) + (c ^ cross)) for p in range(16) for c in range(2)
+            ]
+            halves[h] = halves[h] + lax.ppermute(halves[h], REPLICA, pairs)
     mine = jnp.concatenate(halves, axis=0)
     other = swapped(mine)
     away = kernel_call(sent_body, rights)(mine, grads)

time: 69.4 us -> 73.2 us (1.055)
  waiting for transfers between devices: 7.14 us -> 8.93 us
  blocking collectives: 36.8 us -> 38.2 us
    ppermute x8, waiting for transfers between devices: 5.48 us -> 7.27 us  [shards(): halves[h] = halves[h] + lax.ppermute(halves[h], REPLICA, pairs)]
    ppermute x8, starting transfers between devices: 12.3 us -> 13.8 us  [shards(): halves[h] = halves[h] + lax.ppermute(halves[h], REPLICA, pairs)]
    all_to_all x3, blocking collectives: 36.8 us -> 38.2 us  [all_to_all(): lax.all_to_all(value, axes, 0, 0, axis_index_groups=groups, tiled=True)]
    ppermute x4, starting transfers between devices: 6.05 us -> 5.21 us  [swapped(): return lax.ppermute(value, 'core', [(0, 1), (1, 0)])]
  transfers between devices with their start and end apart: 12 -> 12, of which waited for: 7 -> 6; matrix products, arithmetic and copies ran while one was open for 0% -> 0% of each run, Pallas kernels for 4% -> 4%
where the time goes in v14:
time: 73.2 us; the launch traced here: 73 us
  blocking collectives  38.2 us (52%)
  starting transfers between devices  19 us (26%)
  waiting for transfers between devices  8.93 us (12%)
  Pallas kernels  6.08 us (8%)
  between operations  0.74 us (1%)
    all_to_all x3, blocking collectives, all_to_all(): lax.all_to_all(value, axes, 0, 0, axis_index_groups=groups, tiled=True)  38.2 us
    ppermute x8, starting transfers between devices, shards(): halves[h] = halves[h] + lax.ppermute(halves[h], REPLICA, pairs)  13.8 us
    ppermute x8, waiting for transfers between devices, shards(): halves[h] = halves[h] + lax.ppermute(halves[h], REPLICA, pairs)  7.27 us
    ppermute x4, starting transfers between devices, swapped(): return lax.ppermute(value, 'core', [(0, 1), (1, 0)])  5.21 us
    pallas_call x7, Pallas kernels, kernel_call(): pl.pallas_call(body, out_shape=outs, in_specs=[spec] * len(args), out_spe...  2.98 us
    pallas_call x1, Pallas kernels, shards(): pl.pallas_call(first_body, out_shape=[lefts, jax.ShapeDtypeStruct(grads.s...  1.7 us
    ppermute x4, waiting for transfers between devices, swapped(): return lax.ppermute(value, 'core', [(0, 1), (1, 0)])  1.67 us
  transfers between devices with their start and end apart: 12, of which 6 were waited for; matrix products, arithmetic and copies ran while one was open for 0% of the time, Pallas kernels for 4%

profile of v14, /device:TPU:1, one launch (start us, length us, event | category | flops | bytes accessed | tf_op | source)
XLA Modules:
  0.0 73.0 jit_solution(6411304307759932297)
XLA Ops:
  0.6 1.7 %shard_map.67 = (f32[16,8,128]{2,1,0:T(8,128)S(1)}, bf16[2,512,1024]{2,1,0:T(8,128)(2,1)S(1)}, f32[2,32,1024]{2,1,0:T(8,128)S(1)}) custom-call(f32[2,32,1024]{2,1,0:T(8,128)} %bitcast.23, bf16[2,512,1024]{2,1,0:T(8,128)(2,1)} %bitcast.22), custom_call_target="tpu_custom_call" | custom-call | flops 1048576 | bytes 262144 | tf_op jit(solution)/shard_map/pallas_call | solution.py:358
  2.3 3.3 %collective-permute-start = (f32[16,8,128]{2,1,0:T(8,128)S(1)}, f32[16,8,128]{2,1,0:T(8,128)S(1)}, u32[]{:S(2)}, u32[]{:S(2)}) collective-permute-start(f32[16,8,128]{2,1,0:T(8,128)S(1)} %get-tuple-element.21), channel_id=1, source_target_pairs={{0,8},{8,0},{1,9},{9,1},{2,10},{10,2},{3,11},{11,3},{4,12},{12,4},... | collective-permute-start | bytes 196616 | tf_op jit(solution)/shard_map/ppermute | solution.py:338
  5.6 0.4 shard_map.68
  6.0 0.5 collective-permute-done
  6.5 0.0 collective-permute-start.1
  6.5 2.8 %collective-permute-done.1 = f32[10,8,128]{2,1,0:T(8,128)S(1)} collective-permute-done((f32[10,8,128]{2,1,0:T(8,128)S(1)}, f32[10,8,128]{2,1,0:T(8,128)S(1)}, u32[]{:S(2)}, u32[]{:S(2)}) %collective-permute-start.1) | collective-permute-done | bytes 40992 | tf_op jit(solution)/shard_map/ppermute | solution.py:375
  9.4 2.4 %collective-permute-start.2 = (f32[10,8,128]{2,1,0:T(8,128)S(1)}, f32[10,8,128]{2,1,0:T(8,128)S(1)}, u32[]{:S(2)}, u32[]{:S(2)}) collective-permute-start(f32[10,8,128]{2,1,0:T(8,128)S(1)} %add.31), channel_id=1, source_target_pairs={{0,56},{8,48},{16,40},{24,32},{32,24},{40,16},{48,8},{56,0},{64,12... | collective-permute-start | bytes 122888 | tf_op jit(solution)/shard_map/ppermute | solution.py:375
  11.8 0.5 collective-permute-start.5
  12.3 1.7 %collective-permute-done.2 = f32[10,8,128]{2,1,0:T(8,128)S(1)} collective-permute-done((f32[10,8,128]{2,1,0:T(8,128)S(1)}, f32[10,8,128]{2,1,0:T(8,128)S(1)}, u32[]{:S(2)}, u32[]{:S(2)}) %collective-permute-start.2) | collective-permute-done | bytes 40992 | tf_op jit(solution)/shard_map/ppermute | solution.py:375
  14.0 1.4 %collective-permute-start.3 = (f32[10,8,128]{2,1,0:T(8,128)S(1)}, f32[10,8,128]{2,1,0:T(8,128)S(1)}, u32[]{:S(2)}, u32[]{:S(2)}) collective-permute-start(f32[10,8,128]{2,1,0:T(8,128)S(1)} %add.32), channel_id=1, source_target_pairs={{0,72},{8,64},{16,88},{24,80},{32,104},{40,96},{48,120},{56,112},{... | collective-permute-start | bytes 122888 | tf_op jit(solution)/shard_map/ppermute | solution.py:375
  15.4 0.0 collective-permute-done.5
  15.4 3.1 %collective-permute-start.6 = (f32[6,8,128]{2,1,0:T(8,128)S(1)}, f32[6,8,128]{2,1,0:T(8,128)S(1)}, u32[]{:S(2)}, u32[]{:S(2)}) collective-permute-start(f32[6,8,128]{2,1,0:T(8,128)S(1)} %add.36), channel_id=1, source_target_pairs={{0,128},{8,136},{16,144},{24,152},{32,160},{40,168},{48,176},{56,1... | collective-permute-start | bytes 73736 | tf_op jit(solution)/shard_map/ppermute | solution.py:375
  18.5 1.2 %collective-permute-done.6 = f32[6,8,128]{2,1,0:T(8,128)S(1)} collective-permute-done((f32[6,8,128]{2,1,0:T(8,128)S(1)}, f32[6,8,128]{2,1,0:T(8,128)S(1)}, u32[]{:S(2)}, u32[]{:S(2)}) %collective-permute-start.6) | collective-permute-done | bytes 24608 | tf_op jit(solution)/shard_map/ppermute | solution.py:375
  19.7 0.3 collective-permute-start.7
  20.1 0.0 collective-permute-done.3
  20.1 2.4 %collective-permute-start.4 = (f32[10,8,128]{2,1,0:T(8,128)S(1)}, f32[10,8,128]{2,1,0:T(8,128)S(1)}, u32[]{:S(2)}, u32[]{:S(2)}) collective-permute-start(f32[10,8,128]{2,1,0:T(8,128)S(1)} %add.33), channel_id=1, source_target_pairs={{0,128},{8,136},{16,144},{24,152},{32,160},{40,168},{48,176},{56,1... | collective-permute-start | bytes 122888 | tf_op jit(solution)/shard_map/ppermute | solution.py:375
  22.5 0.0 collective-permute-done.7
  22.5 3.6 %collective-permute-start.8 = (f32[6,8,128]{2,1,0:T(8,128)S(1)}, f32[6,8,128]{2,1,0:T(8,128)S(1)}, u32[]{:S(2)}, u32[]{:S(2)}) collective-permute-start(f32[6,8,128]{2,1,0:T(8,128)S(1)} %add.38), channel_id=1, source_target_pairs={{0,56},{8,48},{16,40},{24,32},{32,24},{40,16},{48,8},{56,0},{64,12... | collective-permute-start | bytes 73736 | tf_op jit(solution)/shard_map/ppermute | solution.py:375
  26.1 1.5 %collective-permute-done.8 = f32[6,8,128]{2,1,0:T(8,128)S(1)} collective-permute-done((f32[6,8,128]{2,1,0:T(8,128)S(1)}, f32[6,8,128]{2,1,0:T(8,128)S(1)}, u32[]{:S(2)}, u32[]{:S(2)}) %collective-permute-start.8) | collective-permute-done | bytes 24608 | tf_op jit(solution)/shard_map/ppermute | solution.py:375
  27.6 0.0 collective-permute-done.4
  27.7 0.3 shard_map.70
  28.0 1.8 %collective-permute-start.10 = (f32[16,16,128]{2,1,0:T(8,128)S(1)}, f32[16,16,128]{2,1,0:T(8,128)S(1)}, u32[]{:S(2)}, u32[]{:S(2)}) collective-permute-start(f32[16,16,128]{2,1,0:T(8,128)S(1)} %shard_map.70), channel_id=1, source_target_pairs={{0,8},{8,0},{1,9},{9,1},{2,10},{10,2},{3,11},{11,3},{4,12},{12,4},... | collective-permute-start | bytes 393224 | tf_op jit(solution)/shard_map/ppermute | solution.py:338
  29.8 0.1 collective-permute-start.9
  29.9 1.2 %collective-permute-done.9.other_ref.left_ref = f32[16,8,128]{2,1,0:T(8,128)S(1)} collective-permute-done((f32[16,8,128]{2,1,0:T(8,128)S(1)}, f32[16,8,128]{2,1,0:T(8,128)S(1)}, u32[]{:S(2)}, u32[]{:S(2)}) %collective-permute-start.9) | collective-permute-done | bytes 65568 | tf_op jit(solution)/shard_map/ppermute | solution.py:338
  31.1 0.8 %shard_map.69 = (f32[16,16,128]{2,1,0:T(8,128)S(1)}, f32[4,128]{1,0:T(4,128)S(1)}) custom-call(f32[16,8,128]{2,1,0:T(8,128)S(1)} %pad_maximum_fusion.mine_ref.left_ref, f32[16,8,128]{2,1,0:T(8,128)S(1)} %collective-permute-done.9.other_ref.left_ref, bf16[2,512,1024]{2,1,0:T(8,128)(2,1)S(1)} %get-tuple-element.20.grads_ref), custom_call_target="tpu_custom_call" | custom-call | flops 1048576 | bytes 262144 | tf_op jit(solution)/shard_map/pallas_call | solution.py:30
  31.8 0.0 collective-permute-done.10.other_ref
  31.9 13.3 %all_to_all.15 = f32[80,4,128]{2,1,0:T(4,128)S(1)} all-to-all(f32[80,4,128]{2,1,0:T(4,128)S(1)} %bitcast.12), channel_id=1, replica_groups={{0,1,2,3,16,17,18,19,40,41,42,43,56,57,58,59},{8,9,10,11,24,25,26,27,32..., dimensions={0} | all-to-all | bytes 327680 | tf_op jit(solution)/shard_map/all_to_all | solution.py:346
  45.2 11.4 %all_to_all.16 = f32[40,4,128]{2,1,0:T(4,128)S(1)} all-to-all(f32[40,4,128]{2,1,0:T(4,128)S(1)} %bitcast.21), channel_id=1, replica_groups={{0,12,68,72,128,140,196,200},{4,8,64,76,132,136,192,204},{1,13,69,73,12..., dimensions={0} | all-to-all | bytes 163840 | tf_op jit(solution)/shard_map/all_to_all | solution.py:346
  56.6 13.5 %all_to_all.17 = f32[16,16,128]{2,1,0:T(8,128)S(1)} all-to-all(f32[16,16,128]{2,1,0:T(8,128)S(1)} %get-tuple-element.24), channel_id=1, replica_groups={{0,1,2,3,16,17,18,19,40,41,42,43,56,57,58,59},{8,9,10,11,24,25,26,27,32..., dimensions={0} | all-to-all | bytes 262144 | tf_op jit(solution)/shard_map/all_to_all | solution.py:346
  70.1 1.4 %shard_map.74 = (f32[32,128]{1,0:T(8,128)S(1)}, f32[32,1024]{1,0:T(8,128)S(1)}, f32[32,512]{1,0:T(8,128)S(1)}, f32[32,512]{1,0:T(8,128)S(1)}) custom-call(f32[16,128]{1,0:T(8,128)S(1)} %get-tuple-element.27.gram_ref, f32[32,8,128]{2,1,0:T(8,128)S(1)} %bitcast.15, f32[16,8,128]{2,1,0:T(8,128)S(1)} %collective-permute-done.9.other_ref.left_ref, ...), custom_call_target="tpu_custom_call" | custom-call | flops 1048576 | bytes 262144 | tf_op jit(solution)/shard_map/pallas_call | solution.py:30
  71.5 0.0 collective-permute-done.11.right_ref
  71.5 1.4 %shard_map.75 = (f32[2,32,1024]{2,1,0:T(8,128)}, f32[2,32,512]{2,1,0:T(8,128)}, f32[2,32,512]{2,1,0:T(8,128)}) custom-call(f32[32,8,128]{2,1,0:T(8,128)S(1)} %collective-permute-done.11.right_ref, f32[16,8,128]{2,1,0:T(8,128)S(1)} %pad_maximum_fusion.mine_ref.left_ref, f32[2,32,512]{2,1,0:T(8,128)S(1)} %bitcast.17, f32[2,32,512]{2,1,0:T(8,128)S(1)} %bitcast.19, ...), custom_call_target="tpu_custom_call" | custom-call | flops 1048576 | bytes 262144 | tf_op jit(solution)/shard_map/pallas_call | solution.py:320
  (19 shorter events, 0.1 us)
Async XLA Ops:
  2.3 4.2 %collective-permute-start = (f32[16,8,128]{2,1,0:T(8,128)S(1)}, f32[16,8,128]{2,1,0:T(8,128)S(1)}, u32[]{:S(2)}, u32[]{:S(2)}) collective-permute-start(f32[16,8,128]{2,1,0:T(8,128)S(1)} %get-tuple-element.21), channel_id=1, source_target_pairs={{0,8},{8,0},{1,9},{9,1},{2,10},{10,2},{3,11},{11,3},{4,12},{12,4},... | collective-permute-start | bytes 196616 | tf_op jit(solution)/shard_map/ppermute | solution.py:338
  6.5 2.9 %collective-permute-start.1 = (f32[10,8,128]{2,1,0:T(8,128)S(1)}, f32[10,8,128]{2,1,0:T(8,128)S(1)}, u32[]{:S(2)}, u32[]{:S(2)}) collective-permute-start(f32[10,8,128]{2,1,0:T(8,128)S(1)} %slice_add_fusion), channel_id=1, source_target_pairs={{0,16},{8,24},{16,0},{24,8},{32,48},{40,56},{48,32},{56,40},{64,80... | collective-permute-start | bytes 122888 | tf_op jit(solution)/shard_map/ppermute | solution.py:375
  9.4 4.6 %collective-permute-start.2 = (f32[10,8,128]{2,1,0:T(8,128)S(1)}, f32[10,8,128]{2,1,0:T(8,128)S(1)}, u32[]{:S(2)}, u32[]{:S(2)}) collective-permute-start(f32[10,8,128]{2,1,0:T(8,128)S(1)} %add.31), channel_id=1, source_target_pairs={{0,56},{8,48},{16,40},{24,32},{32,24},{40,16},{48,8},{56,0},{64,12... | collective-permute-start | bytes 122888 | tf_op jit(solution)/shard_map/ppermute | solution.py:375
  11.8 3.6 %collective-permute-start.5 = (f32[6,8,128]{2,1,0:T(8,128)S(1)}, f32[6,8,128]{2,1,0:T(8,128)S(1)}, u32[]{:S(2)}, u32[]{:S(2)}) collective-permute-start(f32[6,8,128]{2,1,0:T(8,128)S(1)} %slice_add_fusion.1), channel_id=1, source_target_pairs={{0,72},{8,64},{16,88},{24,80},{32,104},{40,96},{48,120},{56,112},{... | collective-permute-start | bytes 73736 | tf_op jit(solution)/shard_map/ppermute | solution.py:375
  14.0 6.0 %collective-permute-start.3 = (f32[10,8,128]{2,1,0:T(8,128)S(1)}, f32[10,8,128]{2,1,0:T(8,128)S(1)}, u32[]{:S(2)}, u32[]{:S(2)}) collective-permute-start(f32[10,8,128]{2,1,0:T(8,128)S(1)} %add.32), channel_id=1, source_target_pairs={{0,72},{8,64},{16,88},{24,80},{32,104},{40,96},{48,120},{56,112},{... | collective-permute-start | bytes 122888 | tf_op jit(solution)/shard_map/ppermute | solution.py:375
  15.4 4.3 %collective-permute-start.6 = (f32[6,8,128]{2,1,0:T(8,128)S(1)}, f32[6,8,128]{2,1,0:T(8,128)S(1)}, u32[]{:S(2)}, u32[]{:S(2)}) collective-permute-start(f32[6,8,128]{2,1,0:T(8,128)S(1)} %add.36), channel_id=1, source_target_pairs={{0,128},{8,136},{16,144},{24,152},{32,160},{40,168},{48,176},{56,1... | collective-permute-start | bytes 73736 | tf_op jit(solution)/shard_map/ppermute | solution.py:375
  19.7 2.8 %collective-permute-start.7 = (f32[6,8,128]{2,1,0:T(8,128)S(1)}, f32[6,8,128]{2,1,0:T(8,128)S(1)}, u32[]{:S(2)}, u32[]{:S(2)}) collective-permute-start(f32[6,8,128]{2,1,0:T(8,128)S(1)} %add.37), channel_id=1, source_target_pairs={{0,16},{8,24},{16,0},{24,8},{32,48},{40,56},{48,32},{56,40},{64,80... | collective-permute-start | bytes 73736 | tf_op jit(solution)/shard_map/ppermute | solution.py:375
  20.1 7.6 %collective-permute-start.4 = (f32[10,8,128]{2,1,0:T(8,128)S(1)}, f32[10,8,128]{2,1,0:T(8,128)S(1)}, u32[]{:S(2)}, u32[]{:S(2)}) collective-permute-start(f32[10,8,128]{2,1,0:T(8,128)S(1)} %add.33), channel_id=1, source_target_pairs={{0,128},{8,136},{16,144},{24,152},{32,160},{40,168},{48,176},{56,1... | collective-permute-start | bytes 122888 | tf_op jit(solution)/shard_map/ppermute | solution.py:375
  22.5 5.1 %collective-permute-start.8 = (f32[6,8,128]{2,1,0:T(8,128)S(1)}, f32[6,8,128]{2,1,0:T(8,128)S(1)}, u32[]{:S(2)}, u32[]{:S(2)}) collective-permute-start(f32[6,8,128]{2,1,0:T(8,128)S(1)} %add.38), channel_id=1, source_target_pairs={{0,56},{8,48},{16,40},{24,32},{32,24},{40,16},{48,8},{56,0},{64,12... | collective-permute-start | bytes 73736 | tf_op jit(solution)/shard_map/ppermute | solution.py:375
  28.0 42.1 %copy-start = (f32[2,512,32]{1,2,0:T(8,128)S(1)}, f32[2,512,32]{1,2,0:T(8,128)}, u32[]{:S(2)}) copy-start(f32[2,512,32]{1,2,0:T(8,128)} %param.6) | copy-start | bytes 393220
  28.0 42.1 %copy-start.1 = (f32[2,512,32]{1,2,0:T(8,128)S(1)}, f32[2,512,32]{1,2,0:T(8,128)}, u32[]{:S(2)}) copy-start(f32[2,512,32]{1,2,0:T(8,128)} %param.7) | copy-start | bytes 393220
  28.0 3.9 %collective-permute-start.10 = (f32[16,16,128]{2,1,0:T(8,128)S(1)}, f32[16,16,128]{2,1,0:T(8,128)S(1)}, u32[]{:S(2)}, u32[]{:S(2)}) collective-permute-start(f32[16,16,128]{2,1,0:T(8,128)S(1)} %shard_map.70), channel_id=1, source_target_pairs={{0,8},{8,0},{1,9},{9,1},{2,10},{10,2},{3,11},{11,3},{4,12},{12,4},... | collective-permute-start | bytes 393224 | tf_op jit(solution)/shard_map/ppermute | solution.py:338
  29.8 1.3 %collective-permute-start.9 = (f32[16,8,128]{2,1,0:T(8,128)S(1)}, f32[16,8,128]{2,1,0:T(8,128)S(1)}, u32[]{:S(2)}, u32[]{:S(2)}) collective-permute-start(f32[16,8,128]{2,1,0:T(8,128)S(1)} %pad_maximum_fusion.mine_ref.left_ref), channel_id=1, source_target_pairs={{0,8},{8,0},{1,9},{9,1},{2,10},{10,2},{3,11},{11,3},{4,12},{12,4},... | collective-permute-start | bytes 196616 | tf_op jit(solution)/shard_map/ppermute | solution.py:338
  70.1 1.5 %collective-permute-start.11 = (f32[32,8,128]{2,1,0:T(8,128)S(1)}, f32[32,8,128]{2,1,0:T(8,128)S(1)}, u32[]{:S(2)}, u32[]{:S(2)}) collective-permute-start(f32[32,8,128]{2,1,0:T(8,128)S(1)} %bitcast.14), channel_id=1, source_target_pairs={{0,8},{8,0},{1,9},{9,1},{2,10},{10,2},{3,11},{11,3},{4,12},{12,4},... | collective-permute-start | bytes 393224 | tf_op jit(solution)/shard_map/ppermute | solution.py:338
